TPU v7x, 1024 devices: a whole 4x8x16 slice. The times are simulated.
1024 devices in a mesh: gx: 8 (over x, core), gy: 128 (over y, z).
Axes of the slice: x: 4, y: 8, z: 16, core: 2. Of those that a mesh axis runs over, the one named last changes fastest.
Arguments:
- right_side: float32 [65536, 128], P(('gx', 'gy')), may hold values from -21 to 21
- mass: float32 [65536, 128], P(('gx', 'gy')), may hold values from 0.5 to 2
- edge_coeff: float32 [65536, 6, 128], P(('gx', 'gy')), may hold values from 0.05 to 0.4
- cell_edges: int32 [65536, 6], P(('gx', 'gy')), may hold values from 0 to 191, as said below
- halo_blocks: int32 [1024, 4, 32], P(('gx', 'gy')), may hold values from 0 to 63, as said below
Outputs:
- solution_field: float32 [65536, 128], P(('gx', 'gy'))
- residual_norm: float32 [], replicated
Inputs may be any that keep to these rules, and one draw needn't show every extreme that they name: `halo_blocks`: for each partition and each of the four directions, 32 distinct local blocks of that partition. `cell_edges`: an entry below 64 names another local block of the same partition, never the row's own block; a larger entry names a block of a received group. No entry names a group from a partition that does not exist. Within a group only a leading run of its 32 blocks is named; its length differs between partitions and directions and is 32 for some partitions.
All inputs are finite; a program needn't handle non-finite values.
Results may differ from a plain program's by a relative error of at most 0.0001.
Values sent between devices are 32-bit elements; how exact they have to be, the bound alone decides.
No kernel may reach another device: no remote copies, remote signals or barrier semaphores. Data moves between devices by JAX's collectives and lax.ppermute only.
A program may use at most 32 MiB of HBM per device.

v0:
```python
import functools

import jax
import jax.numpy as jnp
from jax import lax
from jax.sharding import Mesh
from jax.sharding import PartitionSpec as P

ITERS = 4
GY = ("gy_0", "gy_1")
GX = ("gx_0", "gx_1")
GX_GY = ("gx_0", "gx_1", "gy_0", "gy_1")


spectrum_low = 0.5
spectrum_high = 7.0
lane_shifts = (1, -1, 3, -3, 5, -5)


def passed_along(block, axis, distance):
    devices = range(lax.axis_size(axis))
    route = [(i - distance, i) for i in devices if i - distance in devices]
    return lax.ppermute(block, axis, route)


def by_axis(shard, axes):
    return functools.reduce(lax.psum, axes, shard)


def rotate_lanes(beside):
    rows = [jnp.roll(beside[:, e, :], -lane_shifts[e], axis=-1) for e in range(beside.shape[1])]
    return jnp.stack(rows, axis=1)


def operate(field, mass, edge_coeff, cell_edges, send_list):
    packed = jnp.take(field, send_list.reshape(-1), axis=0).reshape(4, send_list.shape[1], 128)
    pieces = [field]
    for group, offset in ((0, 1), (1, -1)):
        pieces.append(passed_along(packed[group], GY, offset))
    for group, offset in ((2, 1), (3, -1)):
        pieces.append(passed_along(packed[group], GX, offset))
    extended = jnp.concatenate(pieces, axis=0)
    beside = rotate_lanes(jnp.take(extended, cell_edges, axis=0))
    return mass * field + jnp.sum(edge_coeff * (field[:, None, :] - beside), axis=1)


def shards(right_side, mass, edge_coeff, cell_edges, halo_blocks):
    send_list = halo_blocks[0]
    theta = (spectrum_high + spectrum_low) / 2.0
    delta = (spectrum_high - spectrum_low) / 2.0
    sigma = theta / delta
    rho = 1.0 / sigma
    solution_field = jnp.zeros_like(right_side)
    residual = right_side
    direction = residual / theta
    for step in range(ITERS):
        image = operate(direction, mass, edge_coeff, cell_edges, send_list)
        solution_field = solution_field + direction
        residual = residual - image
        if step + 1 < ITERS:
            rho_next = 1.0 / (2.0 * sigma - rho)
            direction = rho_next * rho * direction + 2.0 * rho_next / delta * residual
            rho = rho_next
    remaining = right_side - operate(solution_field, mass, edge_coeff, cell_edges, send_list)
    total = by_axis(jnp.sum(remaining * remaining), GX_GY)
    cells_all = right_side.shape[0] * 128 * lax.axis_size(GX) * lax.axis_size(GY)
    residual_norm = jnp.sqrt(total / cells_all + 1e-06)
    return (solution_field, residual_norm)


def solution(mesh):
    split = Mesh(mesh.devices.reshape(4, 2, 8, 16), ("gx_0", "gx_1", "gy_0", "gy_1"))
    return jax.shard_map(
        shards,
        mesh=split,
        in_specs=(
            P(GX_GY, None),
            P(GX_GY, None),
            P(GX_GY, None, None),
            P(GX_GY, None),
            P(GX_GY, None, None),
        ),
        out_specs=(P(GX_GY, None), P()),
        check_vma=False,
    )
```

profile of v0, /device:TPU:24, one launch (start us, length us, event | category | flops | bytes accessed | tf_op | source)
XLA Modules:
  0.0 152.6 jit_solution(15829972957333594119)
XLA Ops:
  0.6 0.8 reshape_squeeze.2
  1.4 0.8 broadcast_multiply_fusion
  2.2 0.6 gather_fusion
  2.9 4.3 %collective-permute-start = (f32[32,128]{1,0:T(8,128)S(1)}, f32[32,128]{1,0:T(8,128)S(1)}, u32[]{:S(2)}, u32[]{:S(2)}) collective-permute-start(f32[32,128]{1,0:T(8,128)S(1)} %get-tuple-element.49), channel_id=1, source_target_pairs={{0,1},{1,2},{2,3},{3,4},{4,5},{5,6},{6,7},{7,8},{8,9},{9,10},{10,1... | collective-permute-start | bytes 49160 | tf_op jit(solution)/shard_map/ppermute | solution.py:23
  7.2 15.8 %collective-permute-start.1 = (f32[32,128]{1,0:T(8,128)S(1)}, f32[32,128]{1,0:T(8,128)S(1)}, u32[]{:S(2)}, u32[]{:S(2)}) collective-permute-start(f32[32,128]{1,0:T(8,128)S(1)} %get-tuple-element.48), channel_id=1, source_target_pairs={{1,0},{2,1},{3,2},{4,3},{5,4},{6,5},{7,6},{8,7},{9,8},{10,9},{11,1... | collective-permute-start | bytes 49160 | tf_op jit(solution)/shard_map/ppermute | solution.py:23
  23.0 1.5 collective-permute-start.2
  24.5 1.3 collective-permute-start.3
  25.8 0.1 copy.12
  25.9 0.1 reshape.132
  26.0 0.1 copy.11
  26.2 2.9 %collective-permute-done.3 = f32[32,128]{1,0:T(8,128)S(1)} collective-permute-done((f32[32,128]{1,0:T(8,128)S(1)}, f32[32,128]{1,0:T(8,128)S(1)}, u32[]{:S(2)}, u32[]{:S(2)}) %collective-permute-start.3) | collective-permute-done | bytes 16416 | tf_op jit(solution)/shard_map/ppermute | solution.py:23
  29.1 1.1 gather_fusion.1
  30.3 0.1 broadcast_select_fusion.3
  30.4 0.1 fusion.3
  31.5 0.6 copy-done.1
  32.1 0.7 copy-done.2
  32.9 0.6 gather_fusion.2
  33.7 1.9 %collective-permute-start.4 = (f32[32,128]{1,0:T(8,128)S(1)}, f32[32,128]{1,0:T(8,128)S(1)}, u32[]{:S(2)}, u32[]{:S(2)}) collective-permute-start(f32[32,128]{1,0:T(8,128)S(1)} %get-tuple-element.45), channel_id=1, source_target_pairs={{0,1},{1,2},{2,3},{3,4},{4,5},{5,6},{6,7},{7,8},{8,9},{9,10},{10,1... | collective-permute-start | bytes 49160 | tf_op jit(solution)/shard_map/ppermute | solution.py:23
  35.6 6.0 %collective-permute-start.5 = (f32[32,128]{1,0:T(8,128)S(1)}, f32[32,128]{1,0:T(8,128)S(1)}, u32[]{:S(2)}, u32[]{:S(2)}) collective-permute-start(f32[32,128]{1,0:T(8,128)S(1)} %get-tuple-element.44), channel_id=1, source_target_pairs={{1,0},{2,1},{3,2},{4,3},{5,4},{6,5},{7,6},{8,7},{9,8},{10,9},{11,1... | collective-permute-start | bytes 49160 | tf_op jit(solution)/shard_map/ppermute | solution.py:23
  41.6 3.8 %collective-permute-start.6 = (f32[32,128]{1,0:T(8,128)S(1)}, f32[32,128]{1,0:T(8,128)S(1)}, u32[]{:S(2)}, u32[]{:S(2)}) collective-permute-start(f32[32,128]{1,0:T(8,128)S(1)} %get-tuple-element.43), channel_id=1, source_target_pairs={{0,128},{128,256},{256,384},{384,512},{512,640},{640,768},{768,896... | collective-permute-start | bytes 49160 | tf_op jit(solution)/shard_map/ppermute | solution.py:23
  45.5 1.3 collective-permute-start.7
  46.8 1.8 %collective-permute-done.7 = f32[32,128]{1,0:T(8,128)S(1)} collective-permute-done((f32[32,128]{1,0:T(8,128)S(1)}, f32[32,128]{1,0:T(8,128)S(1)}, u32[]{:S(2)}, u32[]{:S(2)}) %collective-permute-start.7) | collective-permute-done | bytes 16416 | tf_op jit(solution)/shard_map/ppermute | solution.py:23
  48.6 1.1 gather_fusion.3
  49.8 0.1 broadcast_select_fusion.2
  49.9 0.1 fusion.2
  51.1 0.6 gather_fusion.4
  51.8 1.9 %collective-permute-start.8 = (f32[32,128]{1,0:T(8,128)S(1)}, f32[32,128]{1,0:T(8,128)S(1)}, u32[]{:S(2)}, u32[]{:S(2)}) collective-permute-start(f32[32,128]{1,0:T(8,128)S(1)} %get-tuple-element.41), channel_id=1, source_target_pairs={{0,1},{1,2},{2,3},{3,4},{4,5},{5,6},{6,7},{7,8},{8,9},{9,10},{10,1... | collective-permute-start | bytes 49160 | tf_op jit(solution)/shard_map/ppermute | solution.py:23
  53.8 6.0 %collective-permute-start.9 = (f32[32,128]{1,0:T(8,128)S(1)}, f32[32,128]{1,0:T(8,128)S(1)}, u32[]{:S(2)}, u32[]{:S(2)}) collective-permute-start(f32[32,128]{1,0:T(8,128)S(1)} %get-tuple-element.40), channel_id=1, source_target_pairs={{1,0},{2,1},{3,2},{4,3},{5,4},{6,5},{7,6},{8,7},{9,8},{10,9},{11,1... | collective-permute-start | bytes 49160 | tf_op jit(solution)/shard_map/ppermute | solution.py:23
  59.8 3.8 %collective-permute-start.10 = (f32[32,128]{1,0:T(8,128)S(1)}, f32[32,128]{1,0:T(8,128)S(1)}, u32[]{:S(2)}, u32[]{:S(2)}) collective-permute-start(f32[32,128]{1,0:T(8,128)S(1)} %get-tuple-element.39), channel_id=1, source_target_pairs={{0,128},{128,256},{256,384},{384,512},{512,640},{640,768},{768,896... | collective-permute-start | bytes 49160 | tf_op jit(solution)/shard_map/ppermute | solution.py:23
  63.6 1.3 collective-permute-start.11
  65.0 1.8 %collective-permute-done.11 = f32[32,128]{1,0:T(8,128)S(1)} collective-permute-done((f32[32,128]{1,0:T(8,128)S(1)}, f32[32,128]{1,0:T(8,128)S(1)}, u32[]{:S(2)}, u32[]{:S(2)}) %collective-permute-start.11) | collective-permute-done | bytes 16416 | tf_op jit(solution)/shard_map/ppermute | solution.py:23
  66.8 1.1 gather_fusion.5
  68.0 0.1 broadcast_select_fusion.1
  68.1 0.1 fusion.1
  69.3 0.6 gather_fusion.6
  70.1 1.9 %collective-permute-start.12 = (f32[32,128]{1,0:T(8,128)S(1)}, f32[32,128]{1,0:T(8,128)S(1)}, u32[]{:S(2)}, u32[]{:S(2)}) collective-permute-start(f32[32,128]{1,0:T(8,128)S(1)} %get-tuple-element.37), channel_id=1, source_target_pairs={{0,1},{1,2},{2,3},{3,4},{4,5},{5,6},{6,7},{7,8},{8,9},{9,10},{10,1... | collective-permute-start | bytes 49160 | tf_op jit(solution)/shard_map/ppermute | solution.py:23
  72.0 6.0 %collective-permute-start.13 = (f32[32,128]{1,0:T(8,128)S(1)}, f32[32,128]{1,0:T(8,128)S(1)}, u32[]{:S(2)}, u32[]{:S(2)}) collective-permute-start(f32[32,128]{1,0:T(8,128)S(1)} %get-tuple-element.36), channel_id=1, source_target_pairs={{1,0},{2,1},{3,2},{4,3},{5,4},{6,5},{7,6},{8,7},{9,8},{10,9},{11,1... | collective-permute-start | bytes 49160 | tf_op jit(solution)/shard_map/ppermute | solution.py:23
  78.0 3.8 %collective-permute-start.14 = (f32[32,128]{1,0:T(8,128)S(1)}, f32[32,128]{1,0:T(8,128)S(1)}, u32[]{:S(2)}, u32[]{:S(2)}) collective-permute-start(f32[32,128]{1,0:T(8,128)S(1)} %get-tuple-element.35), channel_id=1, source_target_pairs={{0,128},{128,256},{256,384},{384,512},{512,640},{640,768},{768,896... | collective-permute-start | bytes 49160 | tf_op jit(solution)/shard_map/ppermute | solution.py:23
  81.9 1.3 collective-permute-start.15
  83.2 1.8 %collective-permute-done.15 = f32[32,128]{1,0:T(8,128)S(1)} collective-permute-done((f32[32,128]{1,0:T(8,128)S(1)}, f32[32,128]{1,0:T(8,128)S(1)}, u32[]{:S(2)}, u32[]{:S(2)}) %collective-permute-start.15) | collective-permute-done | bytes 16416 | tf_op jit(solution)/shard_map/ppermute | solution.py:23
  85.0 1.1 gather_fusion.7
  86.2 0.1 broadcast_select_fusion
  86.3 0.1 fusion
  87.5 0.6 multiply_reduce_fusion.4
  88.1 12.0 %psum.28 = f32[]{:T(128)} all-reduce(f32[]{:T(128)} %multiply_reduce_fusion.4), channel_id=1, replica_groups=mesh['gx_0'=4,'gx_1'=2,'gy_0'=8,'gy_1'=16] {'gx_0'}, use_global_device_ids=true, to_apply=%region_5.8 | all-reduce | flops 1 | bytes 8 | tf_op jit(solution)/shard_map/psum | solution.py:27
  100.1 3.1 %psum.29 = f32[]{:T(128)} all-reduce(f32[]{:T(128)} %psum.28), channel_id=1, replica_groups=mesh['gx_0'=4,'gx_1'=2,'gy_0'=8,'gy_1'=16] {'gx_1'}, use_global_device_ids=true, to_apply=%region_6.9 | all-reduce | flops 1 | bytes 8 | tf_op jit(solution)/shard_map/psum | solution.py:27
  103.2 20.0 %psum.30 = f32[]{:T(128)} all-reduce(f32[]{:T(128)} %psum.29), channel_id=1, replica_groups=mesh['gx_0'=4,'gx_1'=2,'gy_0'=8,'gy_1'=16] {'gy_0'}, use_global_device_ids=true, to_apply=%region_7.10 | all-reduce | flops 1 | bytes 8 | tf_op jit(solution)/shard_map/psum | solution.py:27
  123.1 27.6 %psum.31 = f32[]{:T(128)} all-reduce(f32[]{:T(128)} %psum.30), channel_id=1, replica_groups=mesh['gx_0'=4,'gx_1'=2,'gy_0'=8,'gy_1'=16] {'gy_1'}, use_global_device_ids=true, to_apply=%region_8.11 | all-reduce | flops 1 | bytes 8 | tf_op jit(solution)/shard_map/psum | solution.py:27
  (109 shorter events, 4.6 us)
Async XLA Ops:
  2.9 22.8 %copy-start.4 = (s32[64,6]{0,1:T(8,128)S(1)}, s32[64,6]{0,1:T(8,128)}, u32[]{:S(2)}) copy-start(s32[64,6]{0,1:T(8,128)} %param.12) | copy-start | bytes 4612
  2.9 23.2 %collective-permute-start = (f32[32,128]{1,0:T(8,128)S(1)}, f32[32,128]{1,0:T(8,128)S(1)}, u32[]{:S(2)}, u32[]{:S(2)}) collective-permute-start(f32[32,128]{1,0:T(8,128)S(1)} %get-tuple-element.49), channel_id=1, source_target_pairs={{0,1},{1,2},{2,3},{3,4},{4,5},{5,6},{6,7},{7,8},{8,9},{9,10},{10,1... | collective-permute-start | bytes 49160 | tf_op jit(solution)/shard_map/ppermute | solution.py:23
  7.2 18.9 %collective-permute-start.1 = (f32[32,128]{1,0:T(8,128)S(1)}, f32[32,128]{1,0:T(8,128)S(1)}, u32[]{:S(2)}, u32[]{:S(2)}) collective-permute-start(f32[32,128]{1,0:T(8,128)S(1)} %get-tuple-element.48), channel_id=1, source_target_pairs={{1,0},{2,1},{3,2},{4,3},{5,4},{6,5},{7,6},{8,7},{9,8},{10,9},{11,1... | collective-permute-start | bytes 49160 | tf_op jit(solution)/shard_map/ppermute | solution.py:23
  23.0 3.2 %collective-permute-start.2 = (f32[32,128]{1,0:T(8,128)S(1)}, f32[32,128]{1,0:T(8,128)S(1)}, u32[]{:S(2)}, u32[]{:S(2)}) collective-permute-start(f32[32,128]{1,0:T(8,128)S(1)} %get-tuple-element.47), channel_id=1, source_target_pairs={{0,128},{128,256},{256,384},{384,512},{512,640},{640,768},{768,896... | collective-permute-start | bytes 49160 | tf_op jit(solution)/shard_map/ppermute | solution.py:23
  24.5 4.6 %collective-permute-start.3 = (f32[32,128]{1,0:T(8,128)S(1)}, f32[32,128]{1,0:T(8,128)S(1)}, u32[]{:S(2)}, u32[]{:S(2)}) collective-permute-start(f32[32,128]{1,0:T(8,128)S(1)} %get-tuple-element.46), channel_id=1, source_target_pairs={{128,0},{256,128},{384,256},{512,384},{640,512},{768,640},{896,768... | collective-permute-start | bytes 49160 | tf_op jit(solution)/shard_map/ppermute | solution.py:23
  31.2 0.9 copy-start.1
  32.1 0.8 copy-start.2
  32.1 0.8 copy-start.3
  33.7 13.1 %collective-permute-start.4 = (f32[32,128]{1,0:T(8,128)S(1)}, f32[32,128]{1,0:T(8,128)S(1)}, u32[]{:S(2)}, u32[]{:S(2)}) collective-permute-start(f32[32,128]{1,0:T(8,128)S(1)} %get-tuple-element.45), channel_id=1, source_target_pairs={{0,1},{1,2},{2,3},{3,4},{4,5},{5,6},{6,7},{7,8},{8,9},{9,10},{10,1... | collective-permute-start | bytes 49160 | tf_op jit(solution)/shard_map/ppermute | solution.py:23
  35.6 11.2 %collective-permute-start.5 = (f32[32,128]{1,0:T(8,128)S(1)}, f32[32,128]{1,0:T(8,128)S(1)}, u32[]{:S(2)}, u32[]{:S(2)}) collective-permute-start(f32[32,128]{1,0:T(8,128)S(1)} %get-tuple-element.44), channel_id=1, source_target_pairs={{1,0},{2,1},{3,2},{4,3},{5,4},{6,5},{7,6},{8,7},{9,8},{10,9},{11,1... | collective-permute-start | bytes 49160 | tf_op jit(solution)/shard_map/ppermute | solution.py:23
  41.6 5.2 %collective-permute-start.6 = (f32[32,128]{1,0:T(8,128)S(1)}, f32[32,128]{1,0:T(8,128)S(1)}, u32[]{:S(2)}, u32[]{:S(2)}) collective-permute-start(f32[32,128]{1,0:T(8,128)S(1)} %get-tuple-element.43), channel_id=1, source_target_pairs={{0,128},{128,256},{256,384},{384,512},{512,640},{640,768},{768,896... | collective-permute-start | bytes 49160 | tf_op jit(solution)/shard_map/ppermute | solution.py:23
  45.5 3.2 %collective-permute-start.7 = (f32[32,128]{1,0:T(8,128)S(1)}, f32[32,128]{1,0:T(8,128)S(1)}, u32[]{:S(2)}, u32[]{:S(2)}) collective-permute-start(f32[32,128]{1,0:T(8,128)S(1)} %get-tuple-element.42), channel_id=1, source_target_pairs={{128,0},{256,128},{384,256},{512,384},{640,512},{768,640},{896,768... | collective-permute-start | bytes 49160 | tf_op jit(solution)/shard_map/ppermute | solution.py:23
  51.8 13.1 %collective-permute-start.8 = (f32[32,128]{1,0:T(8,128)S(1)}, f32[32,128]{1,0:T(8,128)S(1)}, u32[]{:S(2)}, u32[]{:S(2)}) collective-permute-start(f32[32,128]{1,0:T(8,128)S(1)} %get-tuple-element.41), channel_id=1, source_target_pairs={{0,1},{1,2},{2,3},{3,4},{4,5},{5,6},{6,7},{7,8},{8,9},{9,10},{10,1... | collective-permute-start | bytes 49160 | tf_op jit(solution)/shard_map/ppermute | solution.py:23
  53.8 11.2 %collective-permute-start.9 = (f32[32,128]{1,0:T(8,128)S(1)}, f32[32,128]{1,0:T(8,128)S(1)}, u32[]{:S(2)}, u32[]{:S(2)}) collective-permute-start(f32[32,128]{1,0:T(8,128)S(1)} %get-tuple-element.40), channel_id=1, source_target_pairs={{1,0},{2,1},{3,2},{4,3},{5,4},{6,5},{7,6},{8,7},{9,8},{10,9},{11,1... | collective-permute-start | bytes 49160 | tf_op jit(solution)/shard_map/ppermute | solution.py:23
  59.8 5.2 %collective-permute-start.10 = (f32[32,128]{1,0:T(8,128)S(1)}, f32[32,128]{1,0:T(8,128)S(1)}, u32[]{:S(2)}, u32[]{:S(2)}) collective-permute-start(f32[32,128]{1,0:T(8,128)S(1)} %get-tuple-element.39), channel_id=1, source_target_pairs={{0,128},{128,256},{256,384},{384,512},{512,640},{640,768},{768,896... | collective-permute-start | bytes 49160 | tf_op jit(solution)/shard_map/ppermute | solution.py:23
  63.6 3.2 %collective-permute-start.11 = (f32[32,128]{1,0:T(8,128)S(1)}, f32[32,128]{1,0:T(8,128)S(1)}, u32[]{:S(2)}, u32[]{:S(2)}) collective-permute-start(f32[32,128]{1,0:T(8,128)S(1)} %get-tuple-element.38), channel_id=1, source_target_pairs={{128,0},{256,128},{384,256},{512,384},{640,512},{768,640},{896,768... | collective-permute-start | bytes 49160 | tf_op jit(solution)/shard_map/ppermute | solution.py:23
  69.3 18.2 %copy-start = (f32[64,128]{1,0:T(8,128)}, f32[64,128]{1,0:T(8,128)S(1)}, u32[]{:S(2)}) copy-start(f32[64,128]{1,0:T(8,128)S(1)} %get-tuple-element.5) | copy-start | bytes 98308
  70.1 13.1 %collective-permute-start.12 = (f32[32,128]{1,0:T(8,128)S(1)}, f32[32,128]{1,0:T(8,128)S(1)}, u32[]{:S(2)}, u32[]{:S(2)}) collective-permute-start(f32[32,128]{1,0:T(8,128)S(1)} %get-tuple-element.37), channel_id=1, source_target_pairs={{0,1},{1,2},{2,3},{3,4},{4,5},{5,6},{6,7},{7,8},{8,9},{9,10},{10,1... | collective-permute-start | bytes 49160 | tf_op jit(solution)/shard_map/ppermute | solution.py:23
  72.0 11.2 %collective-permute-start.13 = (f32[32,128]{1,0:T(8,128)S(1)}, f32[32,128]{1,0:T(8,128)S(1)}, u32[]{:S(2)}, u32[]{:S(2)}) collective-permute-start(f32[32,128]{1,0:T(8,128)S(1)} %get-tuple-element.36), channel_id=1, source_target_pairs={{1,0},{2,1},{3,2},{4,3},{5,4},{6,5},{7,6},{8,7},{9,8},{10,9},{11,1... | collective-permute-start | bytes 49160 | tf_op jit(solution)/shard_map/ppermute | solution.py:23
  78.0 5.2 %collective-permute-start.14 = (f32[32,128]{1,0:T(8,128)S(1)}, f32[32,128]{1,0:T(8,128)S(1)}, u32[]{:S(2)}, u32[]{:S(2)}) collective-permute-start(f32[32,128]{1,0:T(8,128)S(1)} %get-tuple-element.35), channel_id=1, source_target_pairs={{0,128},{128,256},{256,384},{384,512},{512,640},{640,768},{768,896... | collective-permute-start | bytes 49160 | tf_op jit(solution)/shard_map/ppermute | solution.py:23
  81.9 3.2 %collective-permute-start.15 = (f32[32,128]{1,0:T(8,128)S(1)}, f32[32,128]{1,0:T(8,128)S(1)}, u32[]{:S(2)}, u32[]{:S(2)}) collective-permute-start(f32[32,128]{1,0:T(8,128)S(1)} %get-tuple-element.34), channel_id=1, source_target_pairs={{128,0},{256,128},{384,256},{512,384},{640,512},{768,640},{896,768... | collective-permute-start | bytes 49160 | tf_op jit(solution)/shard_map/ppermute | solution.py:23
where the time goes:
time: 153 us
  blocking collectives  62.7 us (41%)
  starting transfers between devices  62 us (41%)
  local copies, waits for them, and re-layouts  12.1 us (8%)
  waiting for transfers between devices  8.31 us (5%)
  other arithmetic  4.43 us (3%)
  between operations  3.09 us (2%)
    psum x4, blocking collectives, by_axis(): return functools.reduce(lax.psum, axes, shard)  62.7 us
    ppermute x16, starting transfers between devices, passed_along(): return lax.ppermute(block, axis, route)  62 us
    ppermute x16, waiting for transfers between devices, passed_along(): return lax.ppermute(block, axis, route)  8.31 us
    gather x8, local copies, waits for them, and re-layouts, operate(): beside = rotate_lanes(jnp.take(extended, cell_edges, axis=0))  4.57 us
  transfers between devices with their start and end apart: 16, of which 4 were waited for; matrix products, arithmetic and copies ran while one was open for 0% of the time, Pallas kernels for 0%

commit v1 on v0

v1 whole, which is shorter than its diff:
```python
import jax
import jax.numpy as jnp
from jax import lax
from jax.experimental import pallas as pl
from jax.experimental.pallas import tpu as pltpu
from jax.sharding import Mesh
from jax.sharding import PartitionSpec as P

ITERS = 4
EDG = 6
BLK = 64
HB = 32
GY = ("gy_0", "gy_1")
GX = ("gx_0", "gx_1")
GX_GY = ("gx_0", "gx_1", "gy_0", "gy_1")
NEAR = ("gx_0", "gx_1", "gy_0")
FAR = ("gy_1",)

spectrum_low = 0.5
spectrum_high = 7.0
lane_shifts = (1, -1, 3, -3, 5, -5)

theta = (spectrum_high + spectrum_low) / 2.0
delta = (spectrum_high - spectrum_low) / 2.0
sigma = theta / delta
PARAMS = pltpu.CompilerParams(vmem_limit_bytes=8 * 1024 * 1024)


def f32(*shape):
    return jax.ShapeDtypeStruct(shape, jnp.float32)


def call(kernel, outs, *args):
    spec = pl.BlockSpec(memory_space=pltpu.VMEM)
    return pl.pallas_call(
        kernel,
        out_shape=outs,
        in_specs=[spec] * len(args),
        out_specs=jax.tree.map(lambda _: spec, outs),
        compiler_params=PARAMS,
    )(*args)


def three_parts(value):
    high = value.astype(jnp.bfloat16)
    rest = value - high.astype(jnp.float32)
    middle = rest.astype(jnp.bfloat16)
    low = (rest - middle.astype(jnp.float32)).astype(jnp.bfloat16)
    return jnp.concatenate([high, middle, low], axis=1)


def chosen(one_hot, parts):
    rows = jnp.dot(one_hot, parts, preferred_element_type=jnp.float32)
    return rows[:, :128] + rows[:, 128:256] + rows[:, 256:]


def one_hot_rows(numbers, depth):
    n = numbers.shape[1]
    table = lax.broadcasted_iota(jnp.int32, (depth, n), 0) == numbers
    return table.astype(jnp.float32).T.astype(jnp.bfloat16)


def send(field, pick_ref, out_refs):
    packed = chosen(pick_ref[...], three_parts(field))
    for g in range(4):
        out_refs[g][...] = packed[g * HB : (g + 1) * HB]


def first_kernel(b_ref, list_ref, s0, s1, s2, s3, pick_ref):
    for g in range(4):
        pick_ref[g * HB : (g + 1) * HB, :] = one_hot_rows(list_ref[0, g : g + 1, :], BLK)
    send(b_ref[...] * (1.0 / theta), pick_ref, (s0, s1, s2, s3))


def table_kernel(edges_ref, mass_ref, coeff_ref, hot_ref, diag_ref):
    diag = mass_ref[...]
    for e in range(EDG):
        hot_ref[e * BLK : (e + 1) * BLK, :] = one_hot_rows(edges_ref[e : e + 1, :], BLK + 4 * HB)
        diag = diag + coeff_ref[e]
    diag_ref[...] = diag


def operate(field, groups, hot_ref, coeff_ref, diag_ref):
    extended = jnp.concatenate([field] + [g[...] for g in groups], axis=0)
    beside = chosen(hot_ref[...], three_parts(extended))
    image = diag_ref[...] * field
    for e in range(EDG):
        rows = pltpu.roll(beside[e * BLK : (e + 1) * BLK], (-lane_shifts[e]) % 128, 1)
        image = image - coeff_ref[e] * rows
    return image


def steps():
    rho = 1.0 / sigma
    found = []
    for _ in range(ITERS - 1):
        rho_next = 1.0 / (2.0 * sigma - rho)
        found.append((rho_next * rho, 2.0 * rho_next / delta))
        rho = rho_next
    return found


STEPS = steps()


def kernel_1(b_ref, g0, g1, g2, g3, hot, pick, coeff, diag, r_ref, d_ref, s0, s1, s2, s3):
    field = b_ref[...] * (1.0 / theta)
    residual = b_ref[...] - operate(field, (g0, g1, g2, g3), hot, coeff, diag)
    direction = STEPS[0][0] * field + STEPS[0][1] * residual
    send(direction, pick, (s0, s1, s2, s3))
    r_ref[...] = residual
    d_ref[...] = direction


def kernel_2(r0_ref, d0_ref, g0, g1, g2, g3, hot, pick, coeff, diag, r_ref, d_ref, s0, s1, s2, s3):
    field = d0_ref[...]
    residual = r0_ref[...] - operate(field, (g0, g1, g2, g3), hot, coeff, diag)
    direction = STEPS[1][0] * field + STEPS[1][1] * residual
    send(direction, pick, (s0, s1, s2, s3))
    r_ref[...] = residual
    d_ref[...] = direction


def kernel_3(b_ref, d1_ref, r0_ref, d0_ref, g0, g1, g2, g3, hot, pick, coeff, diag, x_ref, s0, s1, s2, s3):
    field = d0_ref[...]
    residual = r0_ref[...] - operate(field, (g0, g1, g2, g3), hot, coeff, diag)
    direction = STEPS[2][0] * field + STEPS[2][1] * residual
    solved = b_ref[...] * (1.0 / theta) + d1_ref[...] + field + direction
    send(solved, pick, (s0, s1, s2, s3))
    x_ref[...] = solved


def kernel_4(b_ref, x_ref, g0, g1, g2, g3, hot, coeff, diag, sum_ref):
    remaining = b_ref[...] - operate(x_ref[...], (g0, g1, g2, g3), hot, coeff, diag)
    sums = jnp.sum(remaining * remaining, axis=0, keepdims=True)
    sum_ref[...] = jnp.broadcast_to(sums, sum_ref.shape)


def chain(block, axis, distance):
    devices = range(lax.axis_size(axis))
    return lax.ppermute(block, axis, [(i - distance, i) for i in devices if i - distance in devices])


def cycle(block, axis, distance):
    n = lax.axis_size(axis)
    return lax.ppermute(block, axis, [(i, (i + distance) % n) for i in range(n)])


def exchange(packed):
    return (
        chain(packed[0], GY, 1),
        chain(packed[1], GY, -1),
        cycle(packed[2], GX, 1),
        cycle(packed[3], GX, -1),
    )


def shards(right_side, mass, edge_coeff, cell_edges, halo_blocks):
    coeff = jnp.transpose(edge_coeff, (1, 0, 2))
    edges = cell_edges.T
    field = f32(BLK, 128)
    sends = [f32(HB, 128)] * 4
    *packed, pick = call(first_kernel, sends + [jax.ShapeDtypeStruct((4 * HB, BLK), jnp.bfloat16)], right_side, halo_blocks)
    hot, diag = call(
        table_kernel,
        [jax.ShapeDtypeStruct((EDG * BLK, BLK + 4 * HB), jnp.bfloat16), field],
        edges, mass, coeff,
    )
    tables = (hot, pick, coeff, diag)
    r1, d1, *packed = call(kernel_1, [field, field] + sends, right_side, *exchange(packed), *tables)
    r2, d2, *packed = call(kernel_2, [field, field] + sends, r1, d1, *exchange(packed), *tables)
    solved, *packed = call(kernel_3, [field] + sends, right_side, d1, r2, d2, *exchange(packed), *tables)
    near, far = lax.axis_size(NEAR), lax.axis_size(FAR)
    part = call(kernel_4, f32(near, 128), right_side, solved, *exchange(packed), hot, coeff, diag)
    part = lax.all_to_all(part, NEAR, 0, 0, tiled=True)
    part = jnp.broadcast_to(jnp.sum(part, axis=0, keepdims=True), (far, 128))
    total = jnp.sum(lax.all_to_all(part, FAR, 0, 0, tiled=True))
    cells_all = right_side.shape[0] * 128 * near * far
    return solved, jnp.sqrt(total / cells_all + 1e-06)


def solution(mesh):
    split = Mesh(mesh.devices.reshape(4, 2, 8, 16), GX_GY)
    return jax.shard_map(
        shards,
        mesh=split,
        in_specs=(
            P(GX_GY, None),
            P(GX_GY, None),
            P(GX_GY, None, None),
            P(GX_GY, None),
            P(GX_GY, None, None),
        ),
        out_specs=(P(GX_GY, None), P()),
        check_vma=False,
    )
```

time: 153 us -> 109 us (0.71)
  the two profiles are of different devices: /device:TPU:24 before, /device:TPU:1 now
where the time goes in v1:
time: 109 us; the launch traced here: 108 us
  blocking collectives  51.2 us (47%)
  starting transfers between devices  44.3 us (41%)
  local copies, waits for them, and re-layouts  3.88 us (4%)
  between operations  2.62 us (2%)
  Pallas kernels  2.61 us (2%)
  waiting for transfers between devices  2.52 us (2%)
    all_to_all x1, blocking collectives, shards(): part = lax.all_to_all(part, NEAR, 0, 0, tiled=True)  37.4 us
    ppermute x8, starting transfers between devices, chain(): lax.ppermute(block, axis, [(i - distance, i) for i in devices if i - dist...  22.8 us
    ppermute x8, starting transfers between devices, cycle(): lax.ppermute(block, axis, [(i, (i + distance) % n) for i in range(n)])  21.6 us
    all_to_all x1, blocking collectives, shards(): total = jnp.sum(lax.all_to_all(part, FAR, 0, 0, tiled=True))  13.8 us
    unnamed x16, local copies, waits for them, and re-layouts  3.87 us
    pallas_call x6, Pallas kernels, call(): pl.pallas_call(kernel, out_shape=outs, in_specs=[spec] * len(args), out_s...  2.61 us
    ppermute x8, waiting for transfers between devices, cycle(): lax.ppermute(block, axis, [(i, (i + distance) % n) for i in range(n)])  2.5 us
  transfers between devices with their start and end apart: 16, of which 6 were waited for; matrix products, arithmetic and copies ran while one was open for 0% of the time, Pallas kernels for 0%

profile of v1, /device:TPU:1, one launch (start us, length us, event | category | flops | bytes accessed | tf_op | source)
XLA Modules:
  0.0 107.9 jit_solution(741019306676769878)
XLA Ops:
  0.6 0.0 copy-start.2
  0.6 0.7 copy-done.2
  1.4 0.7 copy-done.7
  2.1 0.2 shard_map.68
  2.3 4.8 %collective-permute-start = (f32[32,128]{1,0:T(8,128)S(1)}, f32[32,128]{1,0:T(8,128)S(1)}, u32[]{:S(2)}, u32[]{:S(2)}) collective-permute-start(f32[32,128]{1,0:T(8,128)S(1)} %get-tuple-element.26), channel_id=1, source_target_pairs={{0,1},{1,2},{2,3},{3,4},{4,5},{5,6},{6,7},{7,8},{8,9},{9,10},{10,1... | collective-permute-start | bytes 49160 | tf_op jit(solution)/shard_map/ppermute | solution.py:141
  7.1 0.0 copy-start.6
  7.1 1.3 %collective-permute-start.1 = (f32[32,128]{1,0:T(8,128)S(1)}, f32[32,128]{1,0:T(8,128)S(1)}, u32[]{:S(2)}, u32[]{:S(2)}) collective-permute-start(f32[32,128]{1,0:T(8,128)S(1)} %get-tuple-element.27), channel_id=1, source_target_pairs={{1,0},{2,1},{3,2},{4,3},{5,4},{6,5},{7,6},{8,7},{9,8},{10,9},{11,1... | collective-permute-start | bytes 49160 | tf_op jit(solution)/shard_map/ppermute | solution.py:141
  8.4 2.1 %collective-permute-start.2 = (f32[32,128]{1,0:T(8,128)S(1)}, f32[32,128]{1,0:T(8,128)S(1)}, u32[]{:S(2)}, u32[]{:S(2)}) collective-permute-start(f32[32,128]{1,0:T(8,128)S(1)} %get-tuple-element.28), channel_id=1, source_target_pairs={{0,128},{128,256},{256,384},{384,512},{512,640},{640,768},{768,896... | collective-permute-start | bytes 49160 | tf_op jit(solution)/shard_map/ppermute | solution.py:146
  10.5 8.6 %collective-permute-start.3 = (f32[32,128]{1,0:T(8,128)S(1)}, f32[32,128]{1,0:T(8,128)S(1)}, u32[]{:S(2)}, u32[]{:S(2)}) collective-permute-start(f32[32,128]{1,0:T(8,128)S(1)} %get-tuple-element.29), channel_id=1, source_target_pairs={{0,896},{128,0},{256,128},{384,256},{512,384},{640,512},{768,640},... | collective-permute-start | bytes 49160 | tf_op jit(solution)/shard_map/ppermute | solution.py:146
  19.1 0.9 copy-done
  20.0 0.1 shard_map.69
  20.1 0.0 collective-permute-done.g0
  20.2 0.0 collective-permute-done.1.g1
  20.2 0.0 collective-permute-done.2.g2
  20.2 0.0 collective-permute-done.3.g3
  20.2 0.7 copy-done.1
  20.9 0.5 shard_map.70
  21.4 4.3 %collective-permute-start.4 = (f32[32,128]{1,0:T(8,128)S(1)}, f32[32,128]{1,0:T(8,128)S(1)}, u32[]{:S(2)}, u32[]{:S(2)}) collective-permute-start(f32[32,128]{1,0:T(8,128)S(1)} %get-tuple-element.35), channel_id=1, source_target_pairs={{0,1},{1,2},{2,3},{3,4},{4,5},{5,6},{6,7},{7,8},{8,9},{9,10},{10,1... | collective-permute-start | bytes 49160 | tf_op jit(solution)/shard_map/ppermute | solution.py:141
  25.7 1.3 %collective-permute-start.5 = (f32[32,128]{1,0:T(8,128)S(1)}, f32[32,128]{1,0:T(8,128)S(1)}, u32[]{:S(2)}, u32[]{:S(2)}) collective-permute-start(f32[32,128]{1,0:T(8,128)S(1)} %get-tuple-element.36), channel_id=1, source_target_pairs={{1,0},{2,1},{3,2},{4,3},{5,4},{6,5},{7,6},{8,7},{9,8},{10,9},{11,1... | collective-permute-start | bytes 49160 | tf_op jit(solution)/shard_map/ppermute | solution.py:141
  27.0 0.0 collective-permute-start.6
  27.0 3.2 %collective-permute-start.7 = (f32[32,128]{1,0:T(8,128)S(1)}, f32[32,128]{1,0:T(8,128)S(1)}, u32[]{:S(2)}, u32[]{:S(2)}) collective-permute-start(f32[32,128]{1,0:T(8,128)S(1)} %get-tuple-element.38), channel_id=1, source_target_pairs={{0,896},{128,0},{256,128},{384,256},{512,384},{640,512},{768,640},... | collective-permute-start | bytes 49160 | tf_op jit(solution)/shard_map/ppermute | solution.py:146
  30.2 0.0 collective-permute-done.4.g0
  30.2 0.6 collective-permute-done.6.g2
  30.9 0.2 collective-permute-done.7.g3
  31.1 0.5 shard_map.71
  31.6 4.3 %collective-permute-start.8 = (f32[32,128]{1,0:T(8,128)S(1)}, f32[32,128]{1,0:T(8,128)S(1)}, u32[]{:S(2)}, u32[]{:S(2)}) collective-permute-start(f32[32,128]{1,0:T(8,128)S(1)} %get-tuple-element.41), channel_id=1, source_target_pairs={{0,1},{1,2},{2,3},{3,4},{4,5},{5,6},{6,7},{7,8},{8,9},{9,10},{10,1... | collective-permute-start | bytes 49160 | tf_op jit(solution)/shard_map/ppermute | solution.py:141
  35.8 1.3 %collective-permute-start.9 = (f32[32,128]{1,0:T(8,128)S(1)}, f32[32,128]{1,0:T(8,128)S(1)}, u32[]{:S(2)}, u32[]{:S(2)}) collective-permute-start(f32[32,128]{1,0:T(8,128)S(1)} %get-tuple-element.42), channel_id=1, source_target_pairs={{1,0},{2,1},{3,2},{4,3},{5,4},{6,5},{7,6},{8,7},{9,8},{10,9},{11,1... | collective-permute-start | bytes 49160 | tf_op jit(solution)/shard_map/ppermute | solution.py:141
  37.1 0.0 collective-permute-start.10
  37.2 3.8 %collective-permute-start.11 = (f32[32,128]{1,0:T(8,128)S(1)}, f32[32,128]{1,0:T(8,128)S(1)}, u32[]{:S(2)}, u32[]{:S(2)}) collective-permute-start(f32[32,128]{1,0:T(8,128)S(1)} %get-tuple-element.44), channel_id=1, source_target_pairs={{0,896},{128,0},{256,128},{384,256},{512,384},{640,512},{768,640},... | collective-permute-start | bytes 49160 | tf_op jit(solution)/shard_map/ppermute | solution.py:146
  41.0 0.0 collective-permute-done.8.g0
  41.0 0.0 collective-permute-done.9.g1
  41.0 0.6 collective-permute-done.10.g2
  41.6 0.2 collective-permute-done.11.g3
  41.8 0.9 shard_map.72
  42.8 4.3 %collective-permute-start.12 = (f32[32,128]{1,0:T(8,128)S(1)}, f32[32,128]{1,0:T(8,128)S(1)}, u32[]{:S(2)}, u32[]{:S(2)}) collective-permute-start(f32[32,128]{1,0:T(8,128)S(1)} %get-tuple-element.46), channel_id=1, source_target_pairs={{0,1},{1,2},{2,3},{3,4},{4,5},{5,6},{6,7},{7,8},{8,9},{9,10},{10,1... | collective-permute-start | bytes 49160 | tf_op jit(solution)/shard_map/ppermute | solution.py:141
  47.0 1.3 %collective-permute-start.13 = (f32[32,128]{1,0:T(8,128)S(1)}, f32[32,128]{1,0:T(8,128)S(1)}, u32[]{:S(2)}, u32[]{:S(2)}) collective-permute-start(f32[32,128]{1,0:T(8,128)S(1)} %get-tuple-element.47), channel_id=1, source_target_pairs={{1,0},{2,1},{3,2},{4,3},{5,4},{6,5},{7,6},{8,7},{9,8},{10,9},{11,1... | collective-permute-start | bytes 49160 | tf_op jit(solution)/shard_map/ppermute | solution.py:141
  48.3 0.0 collective-permute-start.14
  48.4 3.8 %collective-permute-start.15 = (f32[32,128]{1,0:T(8,128)S(1)}, f32[32,128]{1,0:T(8,128)S(1)}, u32[]{:S(2)}, u32[]{:S(2)}) collective-permute-start(f32[32,128]{1,0:T(8,128)S(1)} %get-tuple-element.49), channel_id=1, source_target_pairs={{0,896},{128,0},{256,128},{384,256},{512,384},{640,512},{768,640},... | collective-permute-start | bytes 49160 | tf_op jit(solution)/shard_map/ppermute | solution.py:146
  52.2 0.0 collective-permute-done.12.g0
  52.2 0.0 collective-permute-done.13.g1
  52.2 0.6 collective-permute-done.14.g2
  52.8 0.2 collective-permute-done.15.g3
  53.0 0.8 copy-done.5
  53.8 0.3 shard_map.73
  54.1 37.4 %all_to_all.15 = f32[64,1,128]{2,1,0:T(1,128)S(1)} all-to-all(f32[64,1,128]{2,1,0:T(1,128)S(1)} %bitcast.11), channel_id=1, replica_groups=mesh['gx_0'=4,'gx_1'=2,'gy_0'=8,'gy_1'=16] {'gx_0','gx_1','gy_0'}, dimensions={0} | all-to-all | bytes 65536 | tf_op jit(solution)/shard_map/all_to_all | solution.py:175
  91.5 0.1 reduce_sum.18
  91.6 13.8 %all_to_all.16 = f32[16,1,128]{2,1,0:T(1,128)S(1)} all-to-all(f32[16,1,128]{2,1,0:T(1,128)S(1)} %broadcast_in_dim.2), channel_id=1, replica_groups=mesh['gx_0'=4,'gx_1'=2,'gy_0'=8,'gy_1'=16] {'gy_1'}, dimensions={0} | all-to-all | bytes 16384 | tf_op jit(solution)/shard_map/all_to_all | solution.py:177
  105.5 0.6 reduce_sum.19
  (11 shorter events, 0.0 us)
Async XLA Ops:
  0.6 0.8 copy-start.2
  1.4 0.7 copy-start.7
  2.1 17.0 %copy-start.4 = (f32[64,128]{1,0:T(8,128)S(1)}, f32[64,128]{1,0:T(8,128)}, u32[]{:S(2)}) copy-start(f32[64,128]{1,0:T(8,128)} %mass_ref.1) | copy-start | bytes 98308
  2.3 17.8 %collective-permute-start = (f32[32,128]{1,0:T(8,128)S(1)}, f32[32,128]{1,0:T(8,128)S(1)}, u32[]{:S(2)}, u32[]{:S(2)}) collective-permute-start(f32[32,128]{1,0:T(8,128)S(1)} %get-tuple-element.26), channel_id=1, source_target_pairs={{0,1},{1,2},{2,3},{3,4},{4,5},{5,6},{6,7},{7,8},{8,9},{9,10},{10,1... | collective-permute-start | bytes 49160 | tf_op jit(solution)/shard_map/ppermute | solution.py:141
  7.1 11.9 %copy-start.6 = (s32[64,6]{0,1:T(8,128)S(1)}, s32[64,6]{0,1:T(8,128)}, u32[]{:S(2)}) copy-start(s32[64,6]{0,1:T(8,128)} %param.8) | copy-start | bytes 4612
  7.1 13.0 %collective-permute-start.1 = (f32[32,128]{1,0:T(8,128)S(1)}, f32[32,128]{1,0:T(8,128)S(1)}, u32[]{:S(2)}, u32[]{:S(2)}) collective-permute-start(f32[32,128]{1,0:T(8,128)S(1)} %get-tuple-element.27), channel_id=1, source_target_pairs={{1,0},{2,1},{3,2},{4,3},{5,4},{6,5},{7,6},{8,7},{9,8},{10,9},{11,1... | collective-permute-start | bytes 49160 | tf_op jit(solution)/shard_map/ppermute | solution.py:141
  8.4 11.7 %collective-permute-start.2 = (f32[32,128]{1,0:T(8,128)S(1)}, f32[32,128]{1,0:T(8,128)S(1)}, u32[]{:S(2)}, u32[]{:S(2)}) collective-permute-start(f32[32,128]{1,0:T(8,128)S(1)} %get-tuple-element.28), channel_id=1, source_target_pairs={{0,128},{128,256},{256,384},{384,512},{512,640},{640,768},{768,896... | collective-permute-start | bytes 49160 | tf_op jit(solution)/shard_map/ppermute | solution.py:146
  10.5 9.7 %collective-permute-start.3 = (f32[32,128]{1,0:T(8,128)S(1)}, f32[32,128]{1,0:T(8,128)S(1)}, u32[]{:S(2)}, u32[]{:S(2)}) collective-permute-start(f32[32,128]{1,0:T(8,128)S(1)} %get-tuple-element.29), channel_id=1, source_target_pairs={{0,896},{128,0},{256,128},{384,256},{512,384},{640,512},{768,640},... | collective-permute-start | bytes 49160 | tf_op jit(solution)/shard_map/ppermute | solution.py:146
  19.1 0.9 copy-start
  20.0 0.9 copy-start.1
  20.0 0.9 copy-start.3
  21.4 8.8 %collective-permute-start.4 = (f32[32,128]{1,0:T(8,128)S(1)}, f32[32,128]{1,0:T(8,128)S(1)}, u32[]{:S(2)}, u32[]{:S(2)}) collective-permute-start(f32[32,128]{1,0:T(8,128)S(1)} %get-tuple-element.35), channel_id=1, source_target_pairs={{0,1},{1,2},{2,3},{3,4},{4,5},{5,6},{6,7},{7,8},{8,9},{9,10},{10,1... | collective-permute-start | bytes 49160 | tf_op jit(solution)/shard_map/ppermute | solution.py:141
  25.7 4.6 %collective-permute-start.5 = (f32[32,128]{1,0:T(8,128)S(1)}, f32[32,128]{1,0:T(8,128)S(1)}, u32[]{:S(2)}, u32[]{:S(2)}) collective-permute-start(f32[32,128]{1,0:T(8,128)S(1)} %get-tuple-element.36), channel_id=1, source_target_pairs={{1,0},{2,1},{3,2},{4,3},{5,4},{6,5},{7,6},{8,7},{9,8},{10,9},{11,1... | collective-permute-start | bytes 49160 | tf_op jit(solution)/shard_map/ppermute | solution.py:141
  27.0 3.9 %collective-permute-start.6 = (f32[32,128]{1,0:T(8,128)S(1)}, f32[32,128]{1,0:T(8,128)S(1)}, u32[]{:S(2)}, u32[]{:S(2)}) collective-permute-start(f32[32,128]{1,0:T(8,128)S(1)} %get-tuple-element.37), channel_id=1, source_target_pairs={{0,128},{128,256},{256,384},{384,512},{512,640},{640,768},{768,896... | collective-permute-start | bytes 49160 | tf_op jit(solution)/shard_map/ppermute | solution.py:146
  27.0 4.1 %collective-permute-start.7 = (f32[32,128]{1,0:T(8,128)S(1)}, f32[32,128]{1,0:T(8,128)S(1)}, u32[]{:S(2)}, u32[]{:S(2)}) collective-permute-start(f32[32,128]{1,0:T(8,128)S(1)} %get-tuple-element.38), channel_id=1, source_target_pairs={{0,896},{128,0},{256,128},{384,256},{512,384},{640,512},{768,640},... | collective-permute-start | bytes 49160 | tf_op jit(solution)/shard_map/ppermute | solution.py:146
  31.6 9.4 %collective-permute-start.8 = (f32[32,128]{1,0:T(8,128)S(1)}, f32[32,128]{1,0:T(8,128)S(1)}, u32[]{:S(2)}, u32[]{:S(2)}) collective-permute-start(f32[32,128]{1,0:T(8,128)S(1)} %get-tuple-element.41), channel_id=1, source_target_pairs={{0,1},{1,2},{2,3},{3,4},{4,5},{5,6},{6,7},{7,8},{8,9},{9,10},{10,1... | collective-permute-start | bytes 49160 | tf_op jit(solution)/shard_map/ppermute | solution.py:141
  35.8 5.2 %collective-permute-start.9 = (f32[32,128]{1,0:T(8,128)S(1)}, f32[32,128]{1,0:T(8,128)S(1)}, u32[]{:S(2)}, u32[]{:S(2)}) collective-permute-start(f32[32,128]{1,0:T(8,128)S(1)} %get-tuple-element.42), channel_id=1, source_target_pairs={{1,0},{2,1},{3,2},{4,3},{5,4},{6,5},{7,6},{8,7},{9,8},{10,9},{11,1... | collective-permute-start | bytes 49160 | tf_op jit(solution)/shard_map/ppermute | solution.py:141
  37.1 4.5 %collective-permute-start.10 = (f32[32,128]{1,0:T(8,128)S(1)}, f32[32,128]{1,0:T(8,128)S(1)}, u32[]{:S(2)}, u32[]{:S(2)}) collective-permute-start(f32[32,128]{1,0:T(8,128)S(1)} %get-tuple-element.43), channel_id=1, source_target_pairs={{0,128},{128,256},{256,384},{384,512},{512,640},{640,768},{768,896... | collective-permute-start | bytes 49160 | tf_op jit(solution)/shard_map/ppermute | solution.py:146
  37.2 4.7 %collective-permute-start.11 = (f32[32,128]{1,0:T(8,128)S(1)}, f32[32,128]{1,0:T(8,128)S(1)}, u32[]{:S(2)}, u32[]{:S(2)}) collective-permute-start(f32[32,128]{1,0:T(8,128)S(1)} %get-tuple-element.44), channel_id=1, source_target_pairs={{0,896},{128,0},{256,128},{384,256},{512,384},{640,512},{768,640},... | collective-permute-start | bytes 49160 | tf_op jit(solution)/shard_map/ppermute | solution.py:146
  42.8 9.4 %collective-permute-start.12 = (f32[32,128]{1,0:T(8,128)S(1)}, f32[32,128]{1,0:T(8,128)S(1)}, u32[]{:S(2)}, u32[]{:S(2)}) collective-permute-start(f32[32,128]{1,0:T(8,128)S(1)} %get-tuple-element.46), channel_id=1, source_target_pairs={{0,1},{1,2},{2,3},{3,4},{4,5},{5,6},{6,7},{7,8},{8,9},{9,10},{10,1... | collective-permute-start | bytes 49160 | tf_op jit(solution)/shard_map/ppermute | solution.py:141
  47.0 5.2 %collective-permute-start.13 = (f32[32,128]{1,0:T(8,128)S(1)}, f32[32,128]{1,0:T(8,128)S(1)}, u32[]{:S(2)}, u32[]{:S(2)}) collective-permute-start(f32[32,128]{1,0:T(8,128)S(1)} %get-tuple-element.47), channel_id=1, source_target_pairs={{1,0},{2,1},{3,2},{4,3},{5,4},{6,5},{7,6},{8,7},{9,8},{10,9},{11,1... | collective-permute-start | bytes 49160 | tf_op jit(solution)/shard_map/ppermute | solution.py:141
  48.3 4.5 %collective-permute-start.14 = (f32[32,128]{1,0:T(8,128)S(1)}, f32[32,128]{1,0:T(8,128)S(1)}, u32[]{:S(2)}, u32[]{:S(2)}) collective-permute-start(f32[32,128]{1,0:T(8,128)S(1)} %get-tuple-element.48), channel_id=1, source_target_pairs={{0,128},{128,256},{256,384},{384,512},{512,640},{640,768},{768,896... | collective-permute-start | bytes 49160 | tf_op jit(solution)/shard_map/ppermute | solution.py:146
  48.4 4.7 %collective-permute-start.15 = (f32[32,128]{1,0:T(8,128)S(1)}, f32[32,128]{1,0:T(8,128)S(1)}, u32[]{:S(2)}, u32[]{:S(2)}) collective-permute-start(f32[32,128]{1,0:T(8,128)S(1)} %get-tuple-element.49), channel_id=1, source_target_pairs={{0,896},{128,0},{256,128},{384,256},{512,384},{640,512},{768,640},... | collective-permute-start | bytes 49160 | tf_op jit(solution)/shard_map/ppermute | solution.py:146
  53.0 0.8 copy-start.5

commit v2 on v1

--- a/solution.py
+++ b/solution.py
@@ -19,6 +19,7 @@
 spectrum_low = 0.5
 spectrum_high = 7.0
 lane_shifts = (1, -1, 3, -3, 5, -5)
+ORDER = (0, 1, 2, 3)
 
 theta = (spectrum_high + spectrum_low) / 2.0
 delta = (spectrum_high - spectrum_low) / 2.0
@@ -62,26 +63,43 @@
 
 def send(field, pick_ref, out_refs):
     packed = chosen(pick_ref[...], three_parts(field))
+    for out_ref, g in zip(out_refs, ORDER):
+        out_ref[...] = packed[g * HB : (g + 1) * HB]
+
+
+def pick_kernel(list_ref, pick_ref):
+    odd = lax.axis_index("gy_1") % 2 == 1
+    up, down = list_ref[0, 0:1, :], list_ref[0, 1:2, :]
+    rows = (jnp.where(odd, up, down), jnp.where(odd, down, up), list_ref[0, 2:3, :], list_ref[0, 3:4, :])
     for g in range(4):
-        out_refs[g][...] = packed[g * HB : (g + 1) * HB]
-
-
-def first_kernel(b_ref, list_ref, s0, s1, s2, s3, pick_ref):
-    for g in range(4):
-        pick_ref[g * HB : (g + 1) * HB, :] = one_hot_rows(list_ref[0, g : g + 1, :], BLK)
+        pick_ref[g * HB : (g + 1) * HB, :] = one_hot_rows(rows[g], BLK)
+
+
+def first_kernel(pick_ref, b_ref, held_ref, s0, s1, s2, s3):
+    held_ref[...] = b_ref[...]
     send(b_ref[...] * (1.0 / theta), pick_ref, (s0, s1, s2, s3))
 
 
-def table_kernel(edges_ref, mass_ref, coeff_ref, hot_ref, diag_ref):
+def table_kernel(edges_ref, mass_ref, coeff_ref, hot_ref, diag_ref, held_ref):
     diag = mass_ref[...]
     for e in range(EDG):
-        hot_ref[e * BLK : (e + 1) * BLK, :] = one_hot_rows(edges_ref[e : e + 1, :], BLK + 4 * HB)
         diag = diag + coeff_ref[e]
+        held_ref[e] = coeff_ref[e]
     diag_ref[...] = diag
+    odd = lax.axis_index("gy_1") % 2 == 1
+    edges = edges_ref[...]
+    edges = jnp.where(odd & (edges >= BLK) & (edges < BLK + 2 * HB), edges ^ HB, edges)
+    for e in range(EDG):
+        hot_ref[e * BLK : (e + 1) * BLK, :] = one_hot_rows(edges[e : e + 1, :], BLK + 4 * HB)
+
+
+def copy_kernel(x_ref, y_ref):
+    y_ref[...] = x_ref[...]
 
 
 def operate(field, groups, hot_ref, coeff_ref, diag_ref):
-    extended = jnp.concatenate([field] + [g[...] for g in groups], axis=0)
+    placed = {g: ref[...] for g, ref in zip(ORDER, groups)}
+    extended = jnp.concatenate([field] + [placed[g] for g in range(4)], axis=0)
     beside = chosen(hot_ref[...], three_parts(extended))
     image = diag_ref[...] * field
     for e in range(EDG):
@@ -136,9 +154,10 @@
     sum_ref[...] = jnp.broadcast_to(sums, sum_ref.shape)
 
 
-def chain(block, axis, distance):
-    devices = range(lax.axis_size(axis))
-    return lax.ppermute(block, axis, [(i - distance, i) for i in devices if i - distance in devices])
+def swap(block, first):
+    n = lax.axis_size(GY)
+    pairs = [(i, i + 1) for i in range(first, n - 1, 2)]
+    return lax.ppermute(block, GY, pairs + [(j, i) for i, j in pairs])
 
 
 def cycle(block, axis, distance):
@@ -147,36 +166,37 @@
 
 
 def exchange(packed):
-    return (
-        chain(packed[0], GY, 1),
-        chain(packed[1], GY, -1),
-        cycle(packed[2], GX, 1),
-        cycle(packed[3], GX, -1),
+    moves = (
+        lambda block: swap(block, 1),
+        lambda block: swap(block, 0),
+        lambda block: cycle(block, GX, 1),
+        lambda block: cycle(block, GX, -1),
     )
+    return [moves[g](block) for g, block in zip(ORDER, packed)]
 
 
 def shards(right_side, mass, edge_coeff, cell_edges, halo_blocks):
-    coeff = jnp.transpose(edge_coeff, (1, 0, 2))
-    edges = cell_edges.T
     field = f32(BLK, 128)
     sends = [f32(HB, 128)] * 4
-    *packed, pick = call(first_kernel, sends + [jax.ShapeDtypeStruct((4 * HB, BLK), jnp.bfloat16)], right_side, halo_blocks)
-    hot, diag = call(
+    pick = call(pick_kernel, jax.ShapeDtypeStruct((4 * HB, BLK), jnp.bfloat16), halo_blocks)
+    held_b, *packed = call(first_kernel, [field] + sends, pick, right_side)
+    hot, diag, coeff = call(
         table_kernel,
-        [jax.ShapeDtypeStruct((EDG * BLK, BLK + 4 * HB), jnp.bfloat16), field],
-        edges, mass, coeff,
+        [jax.ShapeDtypeStruct((EDG * BLK, BLK + 4 * HB), jnp.bfloat16), field, f32(EDG, BLK, 128)],
+        cell_edges.T, mass, jnp.transpose(edge_coeff, (1, 0, 2)),
     )
     tables = (hot, pick, coeff, diag)
-    r1, d1, *packed = call(kernel_1, [field, field] + sends, right_side, *exchange(packed), *tables)
+    r1, d1, *packed = call(kernel_1, [field, field] + sends, held_b, *exchange(packed), *tables)
     r2, d2, *packed = call(kernel_2, [field, field] + sends, r1, d1, *exchange(packed), *tables)
-    solved, *packed = call(kernel_3, [field] + sends, right_side, d1, r2, d2, *exchange(packed), *tables)
+    solved, *packed = call(kernel_3, [field] + sends, held_b, d1, r2, d2, *exchange(packed), *tables)
     near, far = lax.axis_size(NEAR), lax.axis_size(FAR)
-    part = call(kernel_4, f32(near, 128), right_side, solved, *exchange(packed), hot, coeff, diag)
+    groups, solution_field = lax.optimization_barrier((exchange(packed), call(copy_kernel, field, solved)))
+    part = call(kernel_4, f32(near, 128), held_b, solved, *groups, hot, coeff, diag)
     part = lax.all_to_all(part, NEAR, 0, 0, tiled=True)
     part = jnp.broadcast_to(jnp.sum(part, axis=0, keepdims=True), (far, 128))
     total = jnp.sum(lax.all_to_all(part, FAR, 0, 0, tiled=True))
     cells_all = right_side.shape[0] * 128 * near * far
-    return solved, jnp.sqrt(total / cells_all + 1e-06)
+    return solution_field, jnp.sqrt(total / cells_all + 1e-06)
 
 
 def solution(mesh):

time: 109 us -> 101 us (0.927)
  blocking collectives: 51.2 us -> 42.4 us
  starting transfers between devices: 44.3 us -> 47.6 us
  local copies, waits for them, and re-layouts: 3.88 us -> 1.63 us
    all_to_all x1, blocking collectives: 37.4 us -> 24.8 us  [shards(): part = lax.all_to_all(part, NEAR, 0, 0, tiled=True)]
    ppermute x8, starting transfers between devices: 22.8 us -> 31.4 us  [swap(): return lax.ppermute(block, GY, pairs + [(j, i) for i, j in pairs])]
    ppermute x8, starting transfers between devices: 21.6 us -> 16.2 us  [cycle(): lax.ppermute(block, axis, [(i, (i + distance) % n) for i in range(n)])]
    all_to_all x1, blocking collectives: 13.8 us -> 17.6 us  [shards(): total = jnp.sum(lax.all_to_all(part, FAR, 0, 0, tiled=True))]
    unnamed x16 -> x10, local copies, waits for them, and re-layouts: 3.87 us -> 1.62 us
    pallas_call x6 -> x8, Pallas kernels: 2.61 us -> 2.78 us  [call(): pl.pallas_call(kernel, out_shape=outs, in_specs=[spec] * len(args), out_s...]
  transfers between devices with their start and end apart: 16 -> 16, of which waited for: 6 -> 5; matrix products, arithmetic and copies ran while one was open for 0% -> 0% of each run, Pallas kernels for 0% -> 1%
where the time goes in v2:
time: 101 us
  starting transfers between devices  47.6 us (47%)
  blocking collectives  42.4 us (42%)
  waiting for transfers between devices  2.88 us (3%)
  Pallas kernels  2.78 us (3%)
  between operations  2.64 us (3%)
  local copies, waits for them, and re-layouts  1.63 us (2%)
    ppermute x8, starting transfers between devices, swap(): return lax.ppermute(block, GY, pairs + [(j, i) for i, j in pairs])  31.4 us
    all_to_all x1, blocking collectives, shards(): part = lax.all_to_all(part, NEAR, 0, 0, tiled=True)  24.8 us
    all_to_all x1, blocking collectives, shards(): total = jnp.sum(lax.all_to_all(part, FAR, 0, 0, tiled=True))  17.6 us
    ppermute x8, starting transfers between devices, cycle(): lax.ppermute(block, axis, [(i, (i + distance) % n) for i in range(n)])  16.2 us
    ppermute x8, waiting for transfers between devices, cycle(): lax.ppermute(block, axis, [(i, (i + distance) % n) for i in range(n)])  2.85 us
    pallas_call x8, Pallas kernels, call(): pl.pallas_call(kernel, out_shape=outs, in_specs=[spec] * len(args), out_s...  2.78 us
  transfers between devices with their start and end apart: 16, of which 5 were waited for; matrix products, arithmetic and copies ran while one was open for 0% of the time, Pallas kernels for 1%

profile of v2, /device:TPU:1, one launch (start us, length us, event | category | flops | bytes accessed | tf_op | source)
XLA Modules:
  0.0 100.7 jit_solution(5307561036457033896)
XLA Ops:
  0.6 0.7 copy-done.4
  1.3 0.1 shard_map.68.pick_ref.pick
  1.4 0.0 copy-start.1
  1.4 0.2 shard_map.69
  1.6 0.7 collective-permute-start
  2.3 0.0 copy-start.3
  2.3 8.2 %collective-permute-start.1 = (f32[32,128]{1,0:T(8,128)S(1)}, f32[32,128]{1,0:T(8,128)S(1)}, u32[]{:S(2)}, u32[]{:S(2)}) collective-permute-start(f32[32,128]{1,0:T(8,128)S(1)} %get-tuple-element.34), channel_id=1, source_target_pairs={{0,1},{2,3},{4,5},{6,7},{8,9},{10,11},{12,13},{14,15},{16,17},{18,... | collective-permute-start | bytes 49160 | tf_op jit(solution)/shard_map/ppermute | solution.py:160
  10.4 2.3 %collective-permute-start.2 = (f32[32,128]{1,0:T(8,128)S(1)}, f32[32,128]{1,0:T(8,128)S(1)}, u32[]{:S(2)}, u32[]{:S(2)}) collective-permute-start(f32[32,128]{1,0:T(8,128)S(1)} %get-tuple-element.35), channel_id=1, source_target_pairs={{0,128},{128,256},{256,384},{384,512},{512,640},{640,768},{768,896... | collective-permute-start | bytes 49160 | tf_op jit(solution)/shard_map/ppermute | solution.py:165
  12.8 5.6 %collective-permute-start.3 = (f32[32,128]{1,0:T(8,128)S(1)}, f32[32,128]{1,0:T(8,128)S(1)}, u32[]{:S(2)}, u32[]{:S(2)}) collective-permute-start(f32[32,128]{1,0:T(8,128)S(1)} %get-tuple-element.36), channel_id=1, source_target_pairs={{0,896},{128,0},{256,128},{384,256},{512,384},{640,512},{768,640},... | collective-permute-start | bytes 49160 | tf_op jit(solution)/shard_map/ppermute | solution.py:165
  18.4 0.9 copy-done
  19.3 0.1 shard_map.70
  19.4 0.0 collective-permute-done.g0
  19.5 0.0 collective-permute-done.1.g1
  19.5 0.0 collective-permute-done.2.g2
  19.5 0.0 collective-permute-done.3.g3
  19.5 0.5 shard_map.71
  20.0 0.7 collective-permute-start.4
  20.6 5.0 %collective-permute-start.5 = (f32[32,128]{1,0:T(8,128)S(1)}, f32[32,128]{1,0:T(8,128)S(1)}, u32[]{:S(2)}, u32[]{:S(2)}) collective-permute-start(f32[32,128]{1,0:T(8,128)S(1)} %get-tuple-element.43), channel_id=1, source_target_pairs={{0,1},{2,3},{4,5},{6,7},{8,9},{10,11},{12,13},{14,15},{16,17},{18,... | collective-permute-start | bytes 49160 | tf_op jit(solution)/shard_map/ppermute | solution.py:160
  25.7 0.6 collective-permute-start.6
  26.3 2.8 %collective-permute-start.7 = (f32[32,128]{1,0:T(8,128)S(1)}, f32[32,128]{1,0:T(8,128)S(1)}, u32[]{:S(2)}, u32[]{:S(2)}) collective-permute-start(f32[32,128]{1,0:T(8,128)S(1)} %get-tuple-element.45), channel_id=1, source_target_pairs={{0,896},{128,0},{256,128},{384,256},{512,384},{640,512},{768,640},... | collective-permute-start | bytes 49160 | tf_op jit(solution)/shard_map/ppermute | solution.py:165
  29.1 0.0 collective-permute-done.4.g0
  29.1 0.0 collective-permute-done.5.g1
  29.1 0.6 collective-permute-done.6.g2
  29.8 0.2 collective-permute-done.7.g3
  30.0 0.5 shard_map.72
  30.4 0.7 collective-permute-start.8
  31.1 7.1 %collective-permute-start.9 = (f32[32,128]{1,0:T(8,128)S(1)}, f32[32,128]{1,0:T(8,128)S(1)}, u32[]{:S(2)}, u32[]{:S(2)}) collective-permute-start(f32[32,128]{1,0:T(8,128)S(1)} %get-tuple-element.49), channel_id=1, source_target_pairs={{0,1},{2,3},{4,5},{6,7},{8,9},{10,11},{12,13},{14,15},{16,17},{18,... | collective-permute-start | bytes 49160 | tf_op jit(solution)/shard_map/ppermute | solution.py:160
  38.2 0.4 collective-permute-start.10
  38.5 1.4 %collective-permute-start.11 = (f32[32,128]{1,0:T(8,128)S(1)}, f32[32,128]{1,0:T(8,128)S(1)}, u32[]{:S(2)}, u32[]{:S(2)}) collective-permute-start(f32[32,128]{1,0:T(8,128)S(1)} %get-tuple-element.51), channel_id=1, source_target_pairs={{0,896},{128,0},{256,128},{384,256},{512,384},{640,512},{768,640},... | collective-permute-start | bytes 49160 | tf_op jit(solution)/shard_map/ppermute | solution.py:165
  39.9 0.0 collective-permute-done.8.g0
  39.9 0.0 collective-permute-done.9.g1
  39.9 0.6 collective-permute-done.10.g2
  40.5 1.2 %collective-permute-done.11.g3 = f32[32,128]{1,0:T(8,128)S(1)} collective-permute-done((f32[32,128]{1,0:T(8,128)S(1)}, f32[32,128]{1,0:T(8,128)S(1)}, u32[]{:S(2)}, u32[]{:S(2)}) %collective-permute-start.11) | collective-permute-done | bytes 16416 | tf_op jit(solution)/shard_map/ppermute | solution.py:165
  41.7 0.5 shard_map.73
  42.2 0.7 collective-permute-start.12
  42.8 8.6 %collective-permute-start.13 = (f32[32,128]{1,0:T(8,128)S(1)}, f32[32,128]{1,0:T(8,128)S(1)}, u32[]{:S(2)}, u32[]{:S(2)}) collective-permute-start(f32[32,128]{1,0:T(8,128)S(1)} %get-tuple-element.53), channel_id=1, source_target_pairs={{0,1},{2,3},{4,5},{6,7},{8,9},{10,11},{12,13},{14,15},{16,17},{18,... | collective-permute-start | bytes 49160 | tf_op jit(solution)/shard_map/ppermute | solution.py:160
  51.4 0.6 collective-permute-start.14
  52.0 2.6 %collective-permute-start.15 = (f32[32,128]{1,0:T(8,128)S(1)}, f32[32,128]{1,0:T(8,128)S(1)}, u32[]{:S(2)}, u32[]{:S(2)}) collective-permute-start(f32[32,128]{1,0:T(8,128)S(1)} %get-tuple-element.55), channel_id=1, source_target_pairs={{0,896},{128,0},{256,128},{384,256},{512,384},{640,512},{768,640},... | collective-permute-start | bytes 49160 | tf_op jit(solution)/shard_map/ppermute | solution.py:165
  54.6 0.6 shard_map.74
  55.2 0.0 collective-permute-done.12.g0
  55.2 0.0 collective-permute-done.13.g1
  55.2 0.0 collective-permute-done.14.g2
  55.2 0.2 collective-permute-done.15.g3
  55.4 0.3 shard_map.75
  55.7 24.8 %all_to_all.15 = f32[64,1,128]{2,1,0:T(1,128)S(1)} all-to-all(f32[64,1,128]{2,1,0:T(1,128)S(1)} %bitcast.7), channel_id=1, replica_groups=mesh['gx_0'=4,'gx_1'=2,'gy_0'=8,'gy_1'=16] {'gx_0','gx_1','gy_0'}, dimensions={0} | all-to-all | bytes 65536 | tf_op jit(solution)/shard_map/all_to_all | solution.py:195
  80.6 0.1 reduce_sum.18
  80.6 17.6 %all_to_all.16 = f32[16,1,128]{2,1,0:T(1,128)S(1)} all-to-all(f32[16,1,128]{2,1,0:T(1,128)S(1)} %broadcast_in_dim.2), channel_id=1, replica_groups=mesh['gx_0'=4,'gx_1'=2,'gy_0'=8,'gy_1'=16] {'gy_1'}, dimensions={0} | all-to-all | bytes 16384 | tf_op jit(solution)/shard_map/all_to_all | solution.py:197
  98.3 0.6 reduce_sum.19
  (7 shorter events, 0.0 us)
Async XLA Ops:
  0.6 0.8 copy-start.2
  0.6 0.7 copy-start.4
  1.4 16.9 %copy-start.1 = (f32[64,128]{1,0:T(8,128)S(1)}, f32[64,128]{1,0:T(8,128)}, u32[]{:S(2)}) copy-start(f32[64,128]{1,0:T(8,128)} %mass_ref.1) | copy-start | bytes 98308
  1.6 17.8 %collective-permute-start = (f32[32,128]{1,0:T(8,128)S(1)}, f32[32,128]{1,0:T(8,128)S(1)}, u32[]{:S(2)}, u32[]{:S(2)}) collective-permute-start(f32[32,128]{1,0:T(8,128)S(1)} %get-tuple-element.33), channel_id=1, source_target_pairs={{1,2},{3,4},{5,6},{7,8},{9,10},{11,12},{13,14},{15,16},{17,18},{19... | collective-permute-start | bytes 49160 | tf_op jit(solution)/shard_map/ppermute | solution.py:160
  2.3 16.1 %copy-start.3 = (s32[64,6]{0,1:T(8,128)S(1)}, s32[64,6]{0,1:T(8,128)}, u32[]{:S(2)}) copy-start(s32[64,6]{0,1:T(8,128)} %param.8) | copy-start | bytes 4612
  2.3 17.2 %collective-permute-start.1 = (f32[32,128]{1,0:T(8,128)S(1)}, f32[32,128]{1,0:T(8,128)S(1)}, u32[]{:S(2)}, u32[]{:S(2)}) collective-permute-start(f32[32,128]{1,0:T(8,128)S(1)} %get-tuple-element.34), channel_id=1, source_target_pairs={{0,1},{2,3},{4,5},{6,7},{8,9},{10,11},{12,13},{14,15},{16,17},{18,... | collective-permute-start | bytes 49160 | tf_op jit(solution)/shard_map/ppermute | solution.py:160
  10.4 9.0 %collective-permute-start.2 = (f32[32,128]{1,0:T(8,128)S(1)}, f32[32,128]{1,0:T(8,128)S(1)}, u32[]{:S(2)}, u32[]{:S(2)}) collective-permute-start(f32[32,128]{1,0:T(8,128)S(1)} %get-tuple-element.35), channel_id=1, source_target_pairs={{0,128},{128,256},{256,384},{384,512},{512,640},{640,768},{768,896... | collective-permute-start | bytes 49160 | tf_op jit(solution)/shard_map/ppermute | solution.py:165
  12.8 6.7 %collective-permute-start.3 = (f32[32,128]{1,0:T(8,128)S(1)}, f32[32,128]{1,0:T(8,128)S(1)}, u32[]{:S(2)}, u32[]{:S(2)}) collective-permute-start(f32[32,128]{1,0:T(8,128)S(1)} %get-tuple-element.36), channel_id=1, source_target_pairs={{0,896},{128,0},{256,128},{384,256},{512,384},{640,512},{768,640},... | collective-permute-start | bytes 49160 | tf_op jit(solution)/shard_map/ppermute | solution.py:165
  18.4 0.9 copy-start
  20.0 9.1 %collective-permute-start.4 = (f32[32,128]{1,0:T(8,128)S(1)}, f32[32,128]{1,0:T(8,128)S(1)}, u32[]{:S(2)}, u32[]{:S(2)}) collective-permute-start(f32[32,128]{1,0:T(8,128)S(1)} %get-tuple-element.42), channel_id=1, source_target_pairs={{1,2},{3,4},{5,6},{7,8},{9,10},{11,12},{13,14},{15,16},{17,18},{19... | collective-permute-start | bytes 49160 | tf_op jit(solution)/shard_map/ppermute | solution.py:160
  20.6 8.5 %collective-permute-start.5 = (f32[32,128]{1,0:T(8,128)S(1)}, f32[32,128]{1,0:T(8,128)S(1)}, u32[]{:S(2)}, u32[]{:S(2)}) collective-permute-start(f32[32,128]{1,0:T(8,128)S(1)} %get-tuple-element.43), channel_id=1, source_target_pairs={{0,1},{2,3},{4,5},{6,7},{8,9},{10,11},{12,13},{14,15},{16,17},{18,... | collective-permute-start | bytes 49160 | tf_op jit(solution)/shard_map/ppermute | solution.py:160
  25.7 4.1 %collective-permute-start.6 = (f32[32,128]{1,0:T(8,128)S(1)}, f32[32,128]{1,0:T(8,128)S(1)}, u32[]{:S(2)}, u32[]{:S(2)}) collective-permute-start(f32[32,128]{1,0:T(8,128)S(1)} %get-tuple-element.44), channel_id=1, source_target_pairs={{0,128},{128,256},{256,384},{384,512},{512,640},{640,768},{768,896... | collective-permute-start | bytes 49160 | tf_op jit(solution)/shard_map/ppermute | solution.py:165
  26.3 3.7 %collective-permute-start.7 = (f32[32,128]{1,0:T(8,128)S(1)}, f32[32,128]{1,0:T(8,128)S(1)}, u32[]{:S(2)}, u32[]{:S(2)}) collective-permute-start(f32[32,128]{1,0:T(8,128)S(1)} %get-tuple-element.45), channel_id=1, source_target_pairs={{0,896},{128,0},{256,128},{384,256},{512,384},{640,512},{768,640},... | collective-permute-start | bytes 49160 | tf_op jit(solution)/shard_map/ppermute | solution.py:165
  30.4 9.4 %collective-permute-start.8 = (f32[32,128]{1,0:T(8,128)S(1)}, f32[32,128]{1,0:T(8,128)S(1)}, u32[]{:S(2)}, u32[]{:S(2)}) collective-permute-start(f32[32,128]{1,0:T(8,128)S(1)} %get-tuple-element.48), channel_id=1, source_target_pairs={{1,2},{3,4},{5,6},{7,8},{9,10},{11,12},{13,14},{15,16},{17,18},{19... | collective-permute-start | bytes 49160 | tf_op jit(solution)/shard_map/ppermute | solution.py:160
  31.1 8.8 %collective-permute-start.9 = (f32[32,128]{1,0:T(8,128)S(1)}, f32[32,128]{1,0:T(8,128)S(1)}, u32[]{:S(2)}, u32[]{:S(2)}) collective-permute-start(f32[32,128]{1,0:T(8,128)S(1)} %get-tuple-element.49), channel_id=1, source_target_pairs={{0,1},{2,3},{4,5},{6,7},{8,9},{10,11},{12,13},{14,15},{16,17},{18,... | collective-permute-start | bytes 49160 | tf_op jit(solution)/shard_map/ppermute | solution.py:160
  38.2 2.4 %collective-permute-start.10 = (f32[32,128]{1,0:T(8,128)S(1)}, f32[32,128]{1,0:T(8,128)S(1)}, u32[]{:S(2)}, u32[]{:S(2)}) collective-permute-start(f32[32,128]{1,0:T(8,128)S(1)} %get-tuple-element.50), channel_id=1, source_target_pairs={{0,128},{128,256},{256,384},{384,512},{512,640},{640,768},{768,896... | collective-permute-start | bytes 49160 | tf_op jit(solution)/shard_map/ppermute | solution.py:165
  38.5 3.2 %collective-permute-start.11 = (f32[32,128]{1,0:T(8,128)S(1)}, f32[32,128]{1,0:T(8,128)S(1)}, u32[]{:S(2)}, u32[]{:S(2)}) collective-permute-start(f32[32,128]{1,0:T(8,128)S(1)} %get-tuple-element.51), channel_id=1, source_target_pairs={{0,896},{128,0},{256,128},{384,256},{512,384},{640,512},{768,640},... | collective-permute-start | bytes 49160 | tf_op jit(solution)/shard_map/ppermute | solution.py:165
  42.2 13.0 %collective-permute-start.12 = (f32[32,128]{1,0:T(8,128)S(1)}, f32[32,128]{1,0:T(8,128)S(1)}, u32[]{:S(2)}, u32[]{:S(2)}) collective-permute-start(f32[32,128]{1,0:T(8,128)S(1)} %get-tuple-element.52), channel_id=1, source_target_pairs={{1,2},{3,4},{5,6},{7,8},{9,10},{11,12},{13,14},{15,16},{17,18},{19... | collective-permute-start | bytes 49160 | tf_op jit(solution)/shard_map/ppermute | solution.py:160
  42.8 12.3 %collective-permute-start.13 = (f32[32,128]{1,0:T(8,128)S(1)}, f32[32,128]{1,0:T(8,128)S(1)}, u32[]{:S(2)}, u32[]{:S(2)}) collective-permute-start(f32[32,128]{1,0:T(8,128)S(1)} %get-tuple-element.53), channel_id=1, source_target_pairs={{0,1},{2,3},{4,5},{6,7},{8,9},{10,11},{12,13},{14,15},{16,17},{18,... | collective-permute-start | bytes 49160 | tf_op jit(solution)/shard_map/ppermute | solution.py:160
  51.4 3.8 %collective-permute-start.14 = (f32[32,128]{1,0:T(8,128)S(1)}, f32[32,128]{1,0:T(8,128)S(1)}, u32[]{:S(2)}, u32[]{:S(2)}) collective-permute-start(f32[32,128]{1,0:T(8,128)S(1)} %get-tuple-element.54), channel_id=1, source_target_pairs={{0,128},{128,256},{256,384},{384,512},{512,640},{640,768},{768,896... | collective-permute-start | bytes 49160 | tf_op jit(solution)/shard_map/ppermute | solution.py:165
  52.0 3.4 %collective-permute-start.15 = (f32[32,128]{1,0:T(8,128)S(1)}, f32[32,128]{1,0:T(8,128)S(1)}, u32[]{:S(2)}, u32[]{:S(2)}) collective-permute-start(f32[32,128]{1,0:T(8,128)S(1)} %get-tuple-element.55), channel_id=1, source_target_pairs={{0,896},{128,0},{256,128},{384,256},{512,384},{640,512},{768,640},... | collective-permute-start | bytes 49160 | tf_op jit(solution)/shard_map/ppermute | solution.py:165

commit v3 on v2

--- a/solution.py
+++ b/solution.py
@@ -19,7 +19,7 @@
 spectrum_low = 0.5
 spectrum_high = 7.0
 lane_shifts = (1, -1, 3, -3, 5, -5)
-ORDER = (0, 1, 2, 3)
+ORDER = (2, 0, 1, 3)
 
 theta = (spectrum_high + spectrum_low) / 2.0
 delta = (spectrum_high - spectrum_low) / 2.0

time: 101 us -> 99.3 us (0.983)
  starting transfers between devices: 47.6 us -> 46.5 us
    ppermute x8, starting transfers between devices: 31.4 us -> 30.2 us  [swap(): return lax.ppermute(block, GY, pairs + [(j, i) for i, j in pairs])]
  transfers between devices with their start and end apart: 16 -> 16, of which waited for: 5 -> 3; matrix products, arithmetic and copies ran while one was open for 0% -> 0% of each run, Pallas kernels for 1% -> 1%
where the time goes in v3:
time: 99.3 us; the launch traced here: 98.8 us
  starting transfers between devices  46.5 us (47%)
  blocking collectives  41.7 us (42%)
  waiting for transfers between devices  2.86 us (3%)
  Pallas kernels  2.78 us (3%)
  between operations  2.65 us (3%)
  local copies, waits for them, and re-layouts  1.63 us (2%)
    ppermute x8, starting transfers between devices, swap(): return lax.ppermute(block, GY, pairs + [(j, i) for i, j in pairs])  30.2 us
    all_to_all x1, blocking collectives, shards(): part = lax.all_to_all(part, NEAR, 0, 0, tiled=True)  24.6 us
    all_to_all x1, blocking collectives, shards(): total = jnp.sum(lax.all_to_all(part, FAR, 0, 0, tiled=True))  17 us
    ppermute x8, starting transfers between devices, cycle(): lax.ppermute(block, axis, [(i, (i + distance) % n) for i in range(n)])  16.4 us
    ppermute x8, waiting for transfers between devices, cycle(): lax.ppermute(block, axis, [(i, (i + distance) % n) for i in range(n)])  2.84 us
    pallas_call x8, Pallas kernels, call(): pl.pallas_call(kernel, out_shape=outs, in_specs=[spec] * len(args), out_s...  2.78 us
  transfers between devices with their start and end apart: 16, of which 3 were waited for; matrix products, arithmetic and copies ran while one was open for 0% of the time, Pallas kernels for 1%

profile of v3, /device:TPU:1, one launch (start us, length us, event | category | flops | bytes accessed | tf_op | source)
XLA Modules:
  0.0 98.8 jit_solution(17854637997675202618)
XLA Ops:
  0.6 0.7 copy-done.4
  1.3 0.1 shard_map.68.pick_ref.pick
  1.4 0.0 copy-done.2
  1.4 0.0 copy-start.1
  1.4 0.2 shard_map.69
  1.6 2.6 %collective-permute-start = (f32[32,128]{1,0:T(8,128)S(1)}, f32[32,128]{1,0:T(8,128)S(1)}, u32[]{:S(2)}, u32[]{:S(2)}) collective-permute-start(f32[32,128]{1,0:T(8,128)S(1)} %get-tuple-element.33), channel_id=1, source_target_pairs={{0,128},{128,256},{256,384},{384,512},{512,640},{640,768},{768,896... | collective-permute-start | bytes 49160 | tf_op jit(solution)/shard_map/ppermute | solution.py:165
  4.2 0.8 collective-permute-start.1
  5.0 7.3 %collective-permute-start.2 = (f32[32,128]{1,0:T(8,128)S(1)}, f32[32,128]{1,0:T(8,128)S(1)}, u32[]{:S(2)}, u32[]{:S(2)}) collective-permute-start(f32[32,128]{1,0:T(8,128)S(1)} %get-tuple-element.35), channel_id=1, source_target_pairs={{0,1},{2,3},{4,5},{6,7},{8,9},{10,11},{12,13},{14,15},{16,17},{18,... | collective-permute-start | bytes 49160 | tf_op jit(solution)/shard_map/ppermute | solution.py:160
  12.3 6.0 %collective-permute-start.3 = (f32[32,128]{1,0:T(8,128)S(1)}, f32[32,128]{1,0:T(8,128)S(1)}, u32[]{:S(2)}, u32[]{:S(2)}) collective-permute-start(f32[32,128]{1,0:T(8,128)S(1)} %get-tuple-element.36), channel_id=1, source_target_pairs={{0,896},{128,0},{256,128},{384,256},{512,384},{640,512},{768,640},... | collective-permute-start | bytes 49160 | tf_op jit(solution)/shard_map/ppermute | solution.py:165
  18.4 0.9 copy-done
  19.3 0.1 shard_map.70
  19.4 0.0 collective-permute-done.g0
  19.5 0.0 collective-permute-done.1.g1
  19.5 0.0 collective-permute-done.2.g2
  19.5 0.0 collective-permute-done.3.g3
  19.5 0.5 shard_map.71
  20.0 0.0 collective-permute-start.4
  20.0 0.7 collective-permute-start.5
  20.7 4.9 %collective-permute-start.6 = (f32[32,128]{1,0:T(8,128)S(1)}, f32[32,128]{1,0:T(8,128)S(1)}, u32[]{:S(2)}, u32[]{:S(2)}) collective-permute-start(f32[32,128]{1,0:T(8,128)S(1)} %get-tuple-element.44), channel_id=1, source_target_pairs={{0,1},{2,3},{4,5},{6,7},{8,9},{10,11},{12,13},{14,15},{16,17},{18,... | collective-permute-start | bytes 49160 | tf_op jit(solution)/shard_map/ppermute | solution.py:160
  25.6 3.4 %collective-permute-start.7 = (f32[32,128]{1,0:T(8,128)S(1)}, f32[32,128]{1,0:T(8,128)S(1)}, u32[]{:S(2)}, u32[]{:S(2)}) collective-permute-start(f32[32,128]{1,0:T(8,128)S(1)} %get-tuple-element.45), channel_id=1, source_target_pairs={{0,896},{128,0},{256,128},{384,256},{512,384},{640,512},{768,640},... | collective-permute-start | bytes 49160 | tf_op jit(solution)/shard_map/ppermute | solution.py:165
  29.0 0.0 collective-permute-done.4.g0
  29.0 0.0 collective-permute-done.5.g1
  29.0 0.0 collective-permute-done.6.g2
  29.0 0.8 collective-permute-done.7.g3
  29.8 0.5 shard_map.72
  30.3 0.0 collective-permute-start.8
  30.3 0.7 collective-permute-start.9
  31.0 6.6 %collective-permute-start.10 = (f32[32,128]{1,0:T(8,128)S(1)}, f32[32,128]{1,0:T(8,128)S(1)}, u32[]{:S(2)}, u32[]{:S(2)}) collective-permute-start(f32[32,128]{1,0:T(8,128)S(1)} %get-tuple-element.50), channel_id=1, source_target_pairs={{0,1},{2,3},{4,5},{6,7},{8,9},{10,11},{12,13},{14,15},{16,17},{18,... | collective-permute-start | bytes 49160 | tf_op jit(solution)/shard_map/ppermute | solution.py:160
  37.6 1.8 %collective-permute-start.11 = (f32[32,128]{1,0:T(8,128)S(1)}, f32[32,128]{1,0:T(8,128)S(1)}, u32[]{:S(2)}, u32[]{:S(2)}) collective-permute-start(f32[32,128]{1,0:T(8,128)S(1)} %get-tuple-element.51), channel_id=1, source_target_pairs={{0,896},{128,0},{256,128},{384,256},{512,384},{640,512},{768,640},... | collective-permute-start | bytes 49160 | tf_op jit(solution)/shard_map/ppermute | solution.py:165
  39.4 0.0 collective-permute-done.8.g0
  39.4 0.0 collective-permute-done.9.g1
  39.4 0.0 collective-permute-done.10.g2
  39.4 1.3 %collective-permute-done.11.g3 = f32[32,128]{1,0:T(8,128)S(1)} collective-permute-done((f32[32,128]{1,0:T(8,128)S(1)}, f32[32,128]{1,0:T(8,128)S(1)}, u32[]{:S(2)}, u32[]{:S(2)}) %collective-permute-start.11) | collective-permute-done | bytes 16416 | tf_op jit(solution)/shard_map/ppermute | solution.py:165
  40.8 0.5 shard_map.73
  41.3 0.1 collective-permute-start.12
  41.4 0.7 collective-permute-start.13
  42.1 8.6 %collective-permute-start.14 = (f32[32,128]{1,0:T(8,128)S(1)}, f32[32,128]{1,0:T(8,128)S(1)}, u32[]{:S(2)}, u32[]{:S(2)}) collective-permute-start(f32[32,128]{1,0:T(8,128)S(1)} %get-tuple-element.54), channel_id=1, source_target_pairs={{0,1},{2,3},{4,5},{6,7},{8,9},{10,11},{12,13},{14,15},{16,17},{18,... | collective-permute-start | bytes 49160 | tf_op jit(solution)/shard_map/ppermute | solution.py:160
  50.6 2.4 %collective-permute-start.15 = (f32[32,128]{1,0:T(8,128)S(1)}, f32[32,128]{1,0:T(8,128)S(1)}, u32[]{:S(2)}, u32[]{:S(2)}) collective-permute-start(f32[32,128]{1,0:T(8,128)S(1)} %get-tuple-element.55), channel_id=1, source_target_pairs={{0,896},{128,0},{256,128},{384,256},{512,384},{640,512},{768,640},... | collective-permute-start | bytes 49160 | tf_op jit(solution)/shard_map/ppermute | solution.py:165
  53.0 0.6 shard_map.74
  53.6 0.0 collective-permute-done.12.g0
  53.6 0.0 collective-permute-done.13.g1
  53.6 0.0 collective-permute-done.14.g2
  53.6 0.7 collective-permute-done.15.g3
  54.3 0.3 shard_map.75
  54.6 24.6 %all_to_all.15 = f32[64,1,128]{2,1,0:T(1,128)S(1)} all-to-all(f32[64,1,128]{2,1,0:T(1,128)S(1)} %bitcast.7), channel_id=1, replica_groups=mesh['gx_0'=4,'gx_1'=2,'gy_0'=8,'gy_1'=16] {'gx_0','gx_1','gy_0'}, dimensions={0} | all-to-all | bytes 65536 | tf_op jit(solution)/shard_map/all_to_all | solution.py:195
  79.3 0.1 reduce_sum.18
  79.4 17.0 %all_to_all.16 = f32[16,1,128]{2,1,0:T(1,128)S(1)} all-to-all(f32[16,1,128]{2,1,0:T(1,128)S(1)} %broadcast_in_dim.2), channel_id=1, replica_groups=mesh['gx_0'=4,'gx_1'=2,'gy_0'=8,'gy_1'=16] {'gy_1'}, dimensions={0} | all-to-all | bytes 16384 | tf_op jit(solution)/shard_map/all_to_all | solution.py:197
  96.4 0.6 reduce_sum.19
  (7 shorter events, 0.0 us)
Async XLA Ops:
  0.6 0.8 copy-start.2
  0.6 0.7 copy-start.4
  1.4 16.9 %copy-start.1 = (f32[64,128]{1,0:T(8,128)S(1)}, f32[64,128]{1,0:T(8,128)}, u32[]{:S(2)}) copy-start(f32[64,128]{1,0:T(8,128)} %mass_ref.1) | copy-start | bytes 98308
  1.6 17.8 %collective-permute-start = (f32[32,128]{1,0:T(8,128)S(1)}, f32[32,128]{1,0:T(8,128)S(1)}, u32[]{:S(2)}, u32[]{:S(2)}) collective-permute-start(f32[32,128]{1,0:T(8,128)S(1)} %get-tuple-element.33), channel_id=1, source_target_pairs={{0,128},{128,256},{256,384},{384,512},{512,640},{640,768},{768,896... | collective-permute-start | bytes 49160 | tf_op jit(solution)/shard_map/ppermute | solution.py:165
  4.2 14.2 %copy-start.3 = (s32[64,6]{0,1:T(8,128)S(1)}, s32[64,6]{0,1:T(8,128)}, u32[]{:S(2)}) copy-start(s32[64,6]{0,1:T(8,128)} %param.8) | copy-start | bytes 4612
  4.2 15.3 %collective-permute-start.1 = (f32[32,128]{1,0:T(8,128)S(1)}, f32[32,128]{1,0:T(8,128)S(1)}, u32[]{:S(2)}, u32[]{:S(2)}) collective-permute-start(f32[32,128]{1,0:T(8,128)S(1)} %get-tuple-element.34), channel_id=1, source_target_pairs={{1,2},{3,4},{5,6},{7,8},{9,10},{11,12},{13,14},{15,16},{17,18},{19... | collective-permute-start | bytes 49160 | tf_op jit(solution)/shard_map/ppermute | solution.py:160
  5.0 14.5 %collective-permute-start.2 = (f32[32,128]{1,0:T(8,128)S(1)}, f32[32,128]{1,0:T(8,128)S(1)}, u32[]{:S(2)}, u32[]{:S(2)}) collective-permute-start(f32[32,128]{1,0:T(8,128)S(1)} %get-tuple-element.35), channel_id=1, source_target_pairs={{0,1},{2,3},{4,5},{6,7},{8,9},{10,11},{12,13},{14,15},{16,17},{18,... | collective-permute-start | bytes 49160 | tf_op jit(solution)/shard_map/ppermute | solution.py:160
  12.3 7.1 %collective-permute-start.3 = (f32[32,128]{1,0:T(8,128)S(1)}, f32[32,128]{1,0:T(8,128)S(1)}, u32[]{:S(2)}, u32[]{:S(2)}) collective-permute-start(f32[32,128]{1,0:T(8,128)S(1)} %get-tuple-element.36), channel_id=1, source_target_pairs={{0,896},{128,0},{256,128},{384,256},{512,384},{640,512},{768,640},... | collective-permute-start | bytes 49160 | tf_op jit(solution)/shard_map/ppermute | solution.py:165
  18.4 0.9 copy-start
  20.0 9.0 %collective-permute-start.4 = (f32[32,128]{1,0:T(8,128)S(1)}, f32[32,128]{1,0:T(8,128)S(1)}, u32[]{:S(2)}, u32[]{:S(2)}) collective-permute-start(f32[32,128]{1,0:T(8,128)S(1)} %get-tuple-element.42), channel_id=1, source_target_pairs={{0,128},{128,256},{256,384},{384,512},{512,640},{640,768},{768,896... | collective-permute-start | bytes 49160 | tf_op jit(solution)/shard_map/ppermute | solution.py:165
  20.0 9.0 %collective-permute-start.5 = (f32[32,128]{1,0:T(8,128)S(1)}, f32[32,128]{1,0:T(8,128)S(1)}, u32[]{:S(2)}, u32[]{:S(2)}) collective-permute-start(f32[32,128]{1,0:T(8,128)S(1)} %get-tuple-element.43), channel_id=1, source_target_pairs={{1,2},{3,4},{5,6},{7,8},{9,10},{11,12},{13,14},{15,16},{17,18},{19... | collective-permute-start | bytes 49160 | tf_op jit(solution)/shard_map/ppermute | solution.py:160
  20.7 8.3 %collective-permute-start.6 = (f32[32,128]{1,0:T(8,128)S(1)}, f32[32,128]{1,0:T(8,128)S(1)}, u32[]{:S(2)}, u32[]{:S(2)}) collective-permute-start(f32[32,128]{1,0:T(8,128)S(1)} %get-tuple-element.44), channel_id=1, source_target_pairs={{0,1},{2,3},{4,5},{6,7},{8,9},{10,11},{12,13},{14,15},{16,17},{18,... | collective-permute-start | bytes 49160 | tf_op jit(solution)/shard_map/ppermute | solution.py:160
  25.6 4.2 %collective-permute-start.7 = (f32[32,128]{1,0:T(8,128)S(1)}, f32[32,128]{1,0:T(8,128)S(1)}, u32[]{:S(2)}, u32[]{:S(2)}) collective-permute-start(f32[32,128]{1,0:T(8,128)S(1)} %get-tuple-element.45), channel_id=1, source_target_pairs={{0,896},{128,0},{256,128},{384,256},{512,384},{640,512},{768,640},... | collective-permute-start | bytes 49160 | tf_op jit(solution)/shard_map/ppermute | solution.py:165
  30.3 9.2 %collective-permute-start.8 = (f32[32,128]{1,0:T(8,128)S(1)}, f32[32,128]{1,0:T(8,128)S(1)}, u32[]{:S(2)}, u32[]{:S(2)}) collective-permute-start(f32[32,128]{1,0:T(8,128)S(1)} %get-tuple-element.48), channel_id=1, source_target_pairs={{0,128},{128,256},{256,384},{384,512},{512,640},{640,768},{768,896... | collective-permute-start | bytes 49160 | tf_op jit(solution)/shard_map/ppermute | solution.py:165
  30.3 9.1 %collective-permute-start.9 = (f32[32,128]{1,0:T(8,128)S(1)}, f32[32,128]{1,0:T(8,128)S(1)}, u32[]{:S(2)}, u32[]{:S(2)}) collective-permute-start(f32[32,128]{1,0:T(8,128)S(1)} %get-tuple-element.49), channel_id=1, source_target_pairs={{1,2},{3,4},{5,6},{7,8},{9,10},{11,12},{13,14},{15,16},{17,18},{19... | collective-permute-start | bytes 49160 | tf_op jit(solution)/shard_map/ppermute | solution.py:160
  31.0 8.5 %collective-permute-start.10 = (f32[32,128]{1,0:T(8,128)S(1)}, f32[32,128]{1,0:T(8,128)S(1)}, u32[]{:S(2)}, u32[]{:S(2)}) collective-permute-start(f32[32,128]{1,0:T(8,128)S(1)} %get-tuple-element.50), channel_id=1, source_target_pairs={{0,1},{2,3},{4,5},{6,7},{8,9},{10,11},{12,13},{14,15},{16,17},{18,... | collective-permute-start | bytes 49160 | tf_op jit(solution)/shard_map/ppermute | solution.py:160
  37.6 3.2 %collective-permute-start.11 = (f32[32,128]{1,0:T(8,128)S(1)}, f32[32,128]{1,0:T(8,128)S(1)}, u32[]{:S(2)}, u32[]{:S(2)}) collective-permute-start(f32[32,128]{1,0:T(8,128)S(1)} %get-tuple-element.51), channel_id=1, source_target_pairs={{0,896},{128,0},{256,128},{384,256},{512,384},{640,512},{768,640},... | collective-permute-start | bytes 49160 | tf_op jit(solution)/shard_map/ppermute | solution.py:165
  41.3 12.4 %collective-permute-start.12 = (f32[32,128]{1,0:T(8,128)S(1)}, f32[32,128]{1,0:T(8,128)S(1)}, u32[]{:S(2)}, u32[]{:S(2)}) collective-permute-start(f32[32,128]{1,0:T(8,128)S(1)} %get-tuple-element.52), channel_id=1, source_target_pairs={{0,128},{128,256},{256,384},{384,512},{512,640},{640,768},{768,896... | collective-permute-start | bytes 49160 | tf_op jit(solution)/shard_map/ppermute | solution.py:165
  41.4 12.2 %collective-permute-start.13 = (f32[32,128]{1,0:T(8,128)S(1)}, f32[32,128]{1,0:T(8,128)S(1)}, u32[]{:S(2)}, u32[]{:S(2)}) collective-permute-start(f32[32,128]{1,0:T(8,128)S(1)} %get-tuple-element.53), channel_id=1, source_target_pairs={{1,2},{3,4},{5,6},{7,8},{9,10},{11,12},{13,14},{15,16},{17,18},{19... | collective-permute-start | bytes 49160 | tf_op jit(solution)/shard_map/ppermute | solution.py:160
  42.1 11.6 %collective-permute-start.14 = (f32[32,128]{1,0:T(8,128)S(1)}, f32[32,128]{1,0:T(8,128)S(1)}, u32[]{:S(2)}, u32[]{:S(2)}) collective-permute-start(f32[32,128]{1,0:T(8,128)S(1)} %get-tuple-element.54), channel_id=1, source_target_pairs={{0,1},{2,3},{4,5},{6,7},{8,9},{10,11},{12,13},{14,15},{16,17},{18,... | collective-permute-start | bytes 49160 | tf_op jit(solution)/shard_map/ppermute | solution.py:160
  50.6 3.7 %collective-permute-start.15 = (f32[32,128]{1,0:T(8,128)S(1)}, f32[32,128]{1,0:T(8,128)S(1)}, u32[]{:S(2)}, u32[]{:S(2)}) collective-permute-start(f32[32,128]{1,0:T(8,128)S(1)} %get-tuple-element.55), channel_id=1, source_target_pairs={{0,896},{128,0},{256,128},{384,256},{512,384},{640,512},{768,640},... | collective-permute-start | bytes 49160 | tf_op jit(solution)/shard_map/ppermute | solution.py:165

commit v4 on v3

--- a/solution.py
+++ b/solution.py
@@ -19,6 +19,7 @@
 spectrum_low = 0.5
 spectrum_high = 7.0
 lane_shifts = (1, -1, 3, -3, 5, -5)
+FIRST = ("up", 2, "down", 3)
 ORDER = (2, 0, 1, 3)
 
 theta = (spectrum_high + spectrum_low) / 2.0
@@ -61,14 +62,23 @@
     return table.astype(jnp.float32).T.astype(jnp.bfloat16)
 
 
-def send(field, pick_ref, out_refs):
+def odd_row():
+    return lax.axis_index("gy_1") % 2 == 1
+
+
+def send(field, pick_ref, out_refs, order=ORDER):
     packed = chosen(pick_ref[...], three_parts(field))
-    for out_ref, g in zip(out_refs, ORDER):
-        out_ref[...] = packed[g * HB : (g + 1) * HB]
+    placed = {g: packed[g * HB : (g + 1) * HB] for g in range(4)}
+    if order is FIRST:
+        odd = odd_row()
+        placed["up"] = jnp.where(odd, placed[0], placed[1])
+        placed["down"] = jnp.where(odd, placed[1], placed[0])
+    for out_ref, g in zip(out_refs, order):
+        out_ref[...] = placed[g]
 
 
 def pick_kernel(list_ref, pick_ref):
-    odd = lax.axis_index("gy_1") % 2 == 1
+    odd = odd_row()
     up, down = list_ref[0, 0:1, :], list_ref[0, 1:2, :]
     rows = (jnp.where(odd, up, down), jnp.where(odd, down, up), list_ref[0, 2:3, :], list_ref[0, 3:4, :])
     for g in range(4):
@@ -77,7 +87,7 @@
 
 def first_kernel(pick_ref, b_ref, held_ref, s0, s1, s2, s3):
     held_ref[...] = b_ref[...]
-    send(b_ref[...] * (1.0 / theta), pick_ref, (s0, s1, s2, s3))
+    send(b_ref[...] * (1.0 / theta), pick_ref, (s0, s1, s2, s3), FIRST)
 
 
 def table_kernel(edges_ref, mass_ref, coeff_ref, hot_ref, diag_ref, held_ref):
@@ -86,7 +96,7 @@
         diag = diag + coeff_ref[e]
         held_ref[e] = coeff_ref[e]
     diag_ref[...] = diag
-    odd = lax.axis_index("gy_1") % 2 == 1
+    odd = odd_row()
     edges = edges_ref[...]
     edges = jnp.where(odd & (edges >= BLK) & (edges < BLK + 2 * HB), edges ^ HB, edges)
     for e in range(EDG):
@@ -97,8 +107,12 @@
     y_ref[...] = x_ref[...]
 
 
-def operate(field, groups, hot_ref, coeff_ref, diag_ref):
-    placed = {g: ref[...] for g, ref in zip(ORDER, groups)}
+def operate(field, groups, hot_ref, coeff_ref, diag_ref, order=ORDER):
+    placed = {g: ref[...] for g, ref in zip(order, groups)}
+    if order is FIRST:
+        odd = odd_row()
+        placed[0] = jnp.where(odd, placed["down"], placed["up"])
+        placed[1] = jnp.where(odd, placed["up"], placed["down"])
     extended = jnp.concatenate([field] + [placed[g] for g in range(4)], axis=0)
     beside = chosen(hot_ref[...], three_parts(extended))
     image = diag_ref[...] * field
@@ -123,7 +137,7 @@
 
 def kernel_1(b_ref, g0, g1, g2, g3, hot, pick, coeff, diag, r_ref, d_ref, s0, s1, s2, s3):
     field = b_ref[...] * (1.0 / theta)
-    residual = b_ref[...] - operate(field, (g0, g1, g2, g3), hot, coeff, diag)
+    residual = b_ref[...] - operate(field, (g0, g1, g2, g3), hot, coeff, diag, FIRST)
     direction = STEPS[0][0] * field + STEPS[0][1] * residual
     send(direction, pick, (s0, s1, s2, s3))
     r_ref[...] = residual
@@ -165,14 +179,21 @@
     return lax.ppermute(block, axis, [(i, (i + distance) % n) for i in range(n)])
 
 
-def exchange(packed):
-    moves = (
-        lambda block: swap(block, 1),
-        lambda block: swap(block, 0),
-        lambda block: cycle(block, GX, 1),
-        lambda block: cycle(block, GX, -1),
-    )
-    return [moves[g](block) for g, block in zip(ORDER, packed)]
+def chain(block, axis, distance):
+    n = lax.axis_size(axis)
+    return lax.ppermute(block, axis, [(i - distance, i) for i in range(n) if 0 <= i - distance < n])
+
+
+def exchange(packed, order=ORDER):
+    moves = {
+        0: lambda block: swap(block, 1),
+        1: lambda block: swap(block, 0),
+        2: lambda block: cycle(block, GX, 1),
+        3: lambda block: cycle(block, GX, -1),
+        "up": lambda block: chain(block, GY, 1),
+        "down": lambda block: chain(block, GY, -1),
+    }
+    return [moves[g](block) for g, block in zip(order, packed)]
 
 
 def shards(right_side, mass, edge_coeff, cell_edges, halo_blocks):
@@ -186,7 +207,7 @@
         cell_edges.T, mass, jnp.transpose(edge_coeff, (1, 0, 2)),
     )
     tables = (hot, pick, coeff, diag)
-    r1, d1, *packed = call(kernel_1, [field, field] + sends, held_b, *exchange(packed), *tables)
+    r1, d1, *packed = call(kernel_1, [field, field] + sends, held_b, *exchange(packed, FIRST), *tables)
     r2, d2, *packed = call(kernel_2, [field, field] + sends, r1, d1, *exchange(packed), *tables)
     solved, *packed = call(kernel_3, [field] + sends, held_b, d1, r2, d2, *exchange(packed), *tables)
     near, far = lax.axis_size(NEAR), lax.axis_size(FAR)

time: 99.3 us -> 99.2 us (level)
  starting transfers between devices: 46.5 us -> 44.8 us
  blocking collectives: 41.7 us -> 43.2 us
    ppermute x8 -> x6, starting transfers between devices: 30.2 us -> 19.8 us  [swap(): return lax.ppermute(block, GY, pairs + [(j, i) for i, j in pairs])]
    ppermute x0 -> x2, starting transfers between devices: none -> 6.09 us  [chain(): lax.ppermute(block, axis, [(i - distance, i) for i in range(n) if 0 <= i...]
    all_to_all x1, blocking collectives: 24.6 us -> 27.5 us  [shards(): part = lax.all_to_all(part, NEAR, 0, 0, tiled=True)]
    ppermute x8, starting transfers between devices: 16.4 us -> 18.9 us  [cycle(): lax.ppermute(block, axis, [(i, (i + distance) % n) for i in range(n)])]
    all_to_all x1, blocking collectives: 17 us -> 15.7 us  [shards(): total = jnp.sum(lax.all_to_all(part, FAR, 0, 0, tiled=True))]
where the time goes in v4:
time: 99.2 us; the launch traced here: 98.7 us
  starting transfers between devices  44.8 us (45%)
  blocking collectives  43.2 us (44%)
  waiting for transfers between devices  2.95 us (3%)
  Pallas kernels  2.79 us (3%)
  between operations  2.66 us (3%)
  local copies, waits for them, and re-layouts  1.63 us (2%)
    all_to_all x1, blocking collectives, shards(): part = lax.all_to_all(part, NEAR, 0, 0, tiled=True)  27.5 us
    ppermute x6, starting transfers between devices, swap(): return lax.ppermute(block, GY, pairs + [(j, i) for i, j in pairs])  19.8 us
    ppermute x8, starting transfers between devices, cycle(): lax.ppermute(block, axis, [(i, (i + distance) % n) for i in range(n)])  18.9 us
    all_to_all x1, blocking collectives, shards(): total = jnp.sum(lax.all_to_all(part, FAR, 0, 0, tiled=True))  15.7 us
    ppermute x2, starting transfers between devices, chain(): lax.ppermute(block, axis, [(i - distance, i) for i in range(n) if 0 <= i...  6.09 us
    ppermute x8, waiting for transfers between devices, cycle(): lax.ppermute(block, axis, [(i, (i + distance) % n) for i in range(n)])  2.93 us
    pallas_call x8, Pallas kernels, call(): pl.pallas_call(kernel, out_shape=outs, in_specs=[spec] * len(args), out_s...  2.79 us
  transfers between devices with their start and end apart: 16, of which 3 were waited for; matrix products, arithmetic and copies ran while one was open for 0% of the time, Pallas kernels for 1%

profile of v4, /device:TPU:1, one launch (start us, length us, event | category | flops | bytes accessed | tf_op | source)
XLA Modules:
  0.0 98.7 jit_solution(569878697342917484)
XLA Ops:
  0.6 0.7 copy-done.4
  1.3 0.1 shard_map.68.pick_ref.pick
  1.4 0.0 copy-start.1
  1.4 0.2 shard_map.69
  1.6 4.8 %collective-permute-start = (f32[32,128]{1,0:T(8,128)S(1)}, f32[32,128]{1,0:T(8,128)S(1)}, u32[]{:S(2)}, u32[]{:S(2)}) collective-permute-start(f32[32,128]{1,0:T(8,128)S(1)} %get-tuple-element.33), channel_id=1, source_target_pairs={{0,1},{1,2},{2,3},{3,4},{4,5},{5,6},{6,7},{7,8},{8,9},{9,10},{10,1... | collective-permute-start | bytes 49160 | tf_op jit(solution)/shard_map/ppermute | solution.py:184
  6.4 0.0 copy-start.3
  6.4 2.1 %collective-permute-start.1 = (f32[32,128]{1,0:T(8,128)S(1)}, f32[32,128]{1,0:T(8,128)S(1)}, u32[]{:S(2)}, u32[]{:S(2)}) collective-permute-start(f32[32,128]{1,0:T(8,128)S(1)} %get-tuple-element.34), channel_id=1, source_target_pairs={{0,128},{128,256},{256,384},{384,512},{512,640},{640,768},{768,896... | collective-permute-start | bytes 49160 | tf_op jit(solution)/shard_map/ppermute | solution.py:179
  8.5 1.3 %collective-permute-start.2 = (f32[32,128]{1,0:T(8,128)S(1)}, f32[32,128]{1,0:T(8,128)S(1)}, u32[]{:S(2)}, u32[]{:S(2)}) collective-permute-start(f32[32,128]{1,0:T(8,128)S(1)} %get-tuple-element.35), channel_id=1, source_target_pairs={{1,0},{2,1},{3,2},{4,3},{5,4},{6,5},{7,6},{8,7},{9,8},{10,9},{11,1... | collective-permute-start | bytes 49160 | tf_op jit(solution)/shard_map/ppermute | solution.py:184
  9.8 8.6 %collective-permute-start.3 = (f32[32,128]{1,0:T(8,128)S(1)}, f32[32,128]{1,0:T(8,128)S(1)}, u32[]{:S(2)}, u32[]{:S(2)}) collective-permute-start(f32[32,128]{1,0:T(8,128)S(1)} %get-tuple-element.36), channel_id=1, source_target_pairs={{0,896},{128,0},{256,128},{384,256},{512,384},{640,512},{768,640},... | collective-permute-start | bytes 49160 | tf_op jit(solution)/shard_map/ppermute | solution.py:179
  18.4 0.9 copy-done
  19.3 0.1 shard_map.70
  19.4 0.0 collective-permute-done.g0
  19.5 0.0 collective-permute-done.1.g1
  19.5 0.0 collective-permute-done.2.g2
  19.5 0.0 collective-permute-done.3.g3
  19.5 0.5 shard_map.71
  20.0 0.0 collective-permute-start.4
  20.0 0.7 collective-permute-start.5
  20.7 5.5 %collective-permute-start.6 = (f32[32,128]{1,0:T(8,128)S(1)}, f32[32,128]{1,0:T(8,128)S(1)}, u32[]{:S(2)}, u32[]{:S(2)}) collective-permute-start(f32[32,128]{1,0:T(8,128)S(1)} %get-tuple-element.44), channel_id=1, source_target_pairs={{0,1},{2,3},{4,5},{6,7},{8,9},{10,11},{12,13},{14,15},{16,17},{18,... | collective-permute-start | bytes 49160 | tf_op jit(solution)/shard_map/ppermute | solution.py:174
  26.2 3.3 %collective-permute-start.7 = (f32[32,128]{1,0:T(8,128)S(1)}, f32[32,128]{1,0:T(8,128)S(1)}, u32[]{:S(2)}, u32[]{:S(2)}) collective-permute-start(f32[32,128]{1,0:T(8,128)S(1)} %get-tuple-element.45), channel_id=1, source_target_pairs={{0,896},{128,0},{256,128},{384,256},{512,384},{640,512},{768,640},... | collective-permute-start | bytes 49160 | tf_op jit(solution)/shard_map/ppermute | solution.py:179
  29.5 0.0 collective-permute-done.4.g0
  29.5 0.0 collective-permute-done.5.g1
  29.5 0.0 collective-permute-done.6.g2
  29.5 0.8 collective-permute-done.7.g3
  30.3 0.5 shard_map.72
  30.8 0.0 collective-permute-start.8
  30.8 0.7 collective-permute-start.9
  31.5 4.8 %collective-permute-start.10 = (f32[32,128]{1,0:T(8,128)S(1)}, f32[32,128]{1,0:T(8,128)S(1)}, u32[]{:S(2)}, u32[]{:S(2)}) collective-permute-start(f32[32,128]{1,0:T(8,128)S(1)} %get-tuple-element.50), channel_id=1, source_target_pairs={{0,1},{2,3},{4,5},{6,7},{8,9},{10,11},{12,13},{14,15},{16,17},{18,... | collective-permute-start | bytes 49160 | tf_op jit(solution)/shard_map/ppermute | solution.py:174
  36.3 3.7 %collective-permute-start.11 = (f32[32,128]{1,0:T(8,128)S(1)}, f32[32,128]{1,0:T(8,128)S(1)}, u32[]{:S(2)}, u32[]{:S(2)}) collective-permute-start(f32[32,128]{1,0:T(8,128)S(1)} %get-tuple-element.51), channel_id=1, source_target_pairs={{0,896},{128,0},{256,128},{384,256},{512,384},{640,512},{768,640},... | collective-permute-start | bytes 49160 | tf_op jit(solution)/shard_map/ppermute | solution.py:179
  39.9 0.0 collective-permute-done.8.g0
  39.9 0.0 collective-permute-done.9.g1
  39.9 0.0 collective-permute-done.10.g2
  40.0 0.8 collective-permute-done.11.g3
  40.8 0.5 shard_map.73
  41.3 0.0 collective-permute-start.12
  41.3 0.7 collective-permute-start.13
  42.0 7.5 %collective-permute-start.14 = (f32[32,128]{1,0:T(8,128)S(1)}, f32[32,128]{1,0:T(8,128)S(1)}, u32[]{:S(2)}, u32[]{:S(2)}) collective-permute-start(f32[32,128]{1,0:T(8,128)S(1)} %get-tuple-element.54), channel_id=1, source_target_pairs={{0,1},{2,3},{4,5},{6,7},{8,9},{10,11},{12,13},{14,15},{16,17},{18,... | collective-permute-start | bytes 49160 | tf_op jit(solution)/shard_map/ppermute | solution.py:174
  49.5 1.3 %collective-permute-start.15 = (f32[32,128]{1,0:T(8,128)S(1)}, f32[32,128]{1,0:T(8,128)S(1)}, u32[]{:S(2)}, u32[]{:S(2)}) collective-permute-start(f32[32,128]{1,0:T(8,128)S(1)} %get-tuple-element.55), channel_id=1, source_target_pairs={{0,896},{128,0},{256,128},{384,256},{512,384},{640,512},{768,640},... | collective-permute-start | bytes 49160 | tf_op jit(solution)/shard_map/ppermute | solution.py:179
  50.8 0.6 shard_map.74
  51.4 0.0 collective-permute-done.12.g0
  51.4 0.0 collective-permute-done.13.g1
  51.4 0.0 collective-permute-done.14.g2
  51.4 1.3 %collective-permute-done.15.g3 = f32[32,128]{1,0:T(8,128)S(1)} collective-permute-done((f32[32,128]{1,0:T(8,128)S(1)}, f32[32,128]{1,0:T(8,128)S(1)}, u32[]{:S(2)}, u32[]{:S(2)}) %collective-permute-start.15) | collective-permute-done | bytes 16416 | tf_op jit(solution)/shard_map/ppermute | solution.py:179
  52.7 0.3 shard_map.75
  53.0 27.5 %all_to_all.15 = f32[64,1,128]{2,1,0:T(1,128)S(1)} all-to-all(f32[64,1,128]{2,1,0:T(1,128)S(1)} %bitcast.7), channel_id=1, replica_groups=mesh['gx_0'=4,'gx_1'=2,'gy_0'=8,'gy_1'=16] {'gx_0','gx_1','gy_0'}, dimensions={0} | all-to-all | bytes 65536 | tf_op jit(solution)/shard_map/all_to_all | solution.py:216
  80.5 0.1 reduce_sum.18
  80.6 15.7 %all_to_all.16 = f32[16,1,128]{2,1,0:T(1,128)S(1)} all-to-all(f32[16,1,128]{2,1,0:T(1,128)S(1)} %broadcast_in_dim.2), channel_id=1, replica_groups=mesh['gx_0'=4,'gx_1'=2,'gy_0'=8,'gy_1'=16] {'gy_1'}, dimensions={0} | all-to-all | bytes 16384 | tf_op jit(solution)/shard_map/all_to_all | solution.py:218
  96.3 0.6 reduce_sum.19
  (7 shorter events, 0.0 us)
Async XLA Ops:
  0.6 0.8 copy-start.2
  0.6 0.7 copy-start.4
  1.4 16.9 %copy-start.1 = (f32[64,128]{1,0:T(8,128)S(1)}, f32[64,128]{1,0:T(8,128)}, u32[]{:S(2)}) copy-start(f32[64,128]{1,0:T(8,128)} %mass_ref.1) | copy-start | bytes 98308
  1.6 17.8 %collective-permute-start = (f32[32,128]{1,0:T(8,128)S(1)}, f32[32,128]{1,0:T(8,128)S(1)}, u32[]{:S(2)}, u32[]{:S(2)}) collective-permute-start(f32[32,128]{1,0:T(8,128)S(1)} %get-tuple-element.33), channel_id=1, source_target_pairs={{0,1},{1,2},{2,3},{3,4},{4,5},{5,6},{6,7},{7,8},{8,9},{9,10},{10,1... | collective-permute-start | bytes 49160 | tf_op jit(solution)/shard_map/ppermute | solution.py:184
  6.4 11.9 %copy-start.3 = (s32[64,6]{0,1:T(8,128)S(1)}, s32[64,6]{0,1:T(8,128)}, u32[]{:S(2)}) copy-start(s32[64,6]{0,1:T(8,128)} %param.8) | copy-start | bytes 4612
  6.4 13.0 %collective-permute-start.1 = (f32[32,128]{1,0:T(8,128)S(1)}, f32[32,128]{1,0:T(8,128)S(1)}, u32[]{:S(2)}, u32[]{:S(2)}) collective-permute-start(f32[32,128]{1,0:T(8,128)S(1)} %get-tuple-element.34), channel_id=1, source_target_pairs={{0,128},{128,256},{256,384},{384,512},{512,640},{640,768},{768,896... | collective-permute-start | bytes 49160 | tf_op jit(solution)/shard_map/ppermute | solution.py:179
  8.5 11.0 %collective-permute-start.2 = (f32[32,128]{1,0:T(8,128)S(1)}, f32[32,128]{1,0:T(8,128)S(1)}, u32[]{:S(2)}, u32[]{:S(2)}) collective-permute-start(f32[32,128]{1,0:T(8,128)S(1)} %get-tuple-element.35), channel_id=1, source_target_pairs={{1,0},{2,1},{3,2},{4,3},{5,4},{6,5},{7,6},{8,7},{9,8},{10,9},{11,1... | collective-permute-start | bytes 49160 | tf_op jit(solution)/shard_map/ppermute | solution.py:184
  9.8 9.7 %collective-permute-start.3 = (f32[32,128]{1,0:T(8,128)S(1)}, f32[32,128]{1,0:T(8,128)S(1)}, u32[]{:S(2)}, u32[]{:S(2)}) collective-permute-start(f32[32,128]{1,0:T(8,128)S(1)} %get-tuple-element.36), channel_id=1, source_target_pairs={{0,896},{128,0},{256,128},{384,256},{512,384},{640,512},{768,640},... | collective-permute-start | bytes 49160 | tf_op jit(solution)/shard_map/ppermute | solution.py:179
  18.4 0.9 copy-start
  20.0 9.5 %collective-permute-start.4 = (f32[32,128]{1,0:T(8,128)S(1)}, f32[32,128]{1,0:T(8,128)S(1)}, u32[]{:S(2)}, u32[]{:S(2)}) collective-permute-start(f32[32,128]{1,0:T(8,128)S(1)} %get-tuple-element.42), channel_id=1, source_target_pairs={{0,128},{128,256},{256,384},{384,512},{512,640},{640,768},{768,896... | collective-permute-start | bytes 49160 | tf_op jit(solution)/shard_map/ppermute | solution.py:179
  20.0 9.5 %collective-permute-start.5 = (f32[32,128]{1,0:T(8,128)S(1)}, f32[32,128]{1,0:T(8,128)S(1)}, u32[]{:S(2)}, u32[]{:S(2)}) collective-permute-start(f32[32,128]{1,0:T(8,128)S(1)} %get-tuple-element.43), channel_id=1, source_target_pairs={{1,2},{3,4},{5,6},{7,8},{9,10},{11,12},{13,14},{15,16},{17,18},{19... | collective-permute-start | bytes 49160 | tf_op jit(solution)/shard_map/ppermute | solution.py:174
  20.7 8.8 %collective-permute-start.6 = (f32[32,128]{1,0:T(8,128)S(1)}, f32[32,128]{1,0:T(8,128)S(1)}, u32[]{:S(2)}, u32[]{:S(2)}) collective-permute-start(f32[32,128]{1,0:T(8,128)S(1)} %get-tuple-element.44), channel_id=1, source_target_pairs={{0,1},{2,3},{4,5},{6,7},{8,9},{10,11},{12,13},{14,15},{16,17},{18,... | collective-permute-start | bytes 49160 | tf_op jit(solution)/shard_map/ppermute | solution.py:174
  26.2 4.1 %collective-permute-start.7 = (f32[32,128]{1,0:T(8,128)S(1)}, f32[32,128]{1,0:T(8,128)S(1)}, u32[]{:S(2)}, u32[]{:S(2)}) collective-permute-start(f32[32,128]{1,0:T(8,128)S(1)} %get-tuple-element.45), channel_id=1, source_target_pairs={{0,896},{128,0},{256,128},{384,256},{512,384},{640,512},{768,640},... | collective-permute-start | bytes 49160 | tf_op jit(solution)/shard_map/ppermute | solution.py:179
  30.8 9.2 %collective-permute-start.8 = (f32[32,128]{1,0:T(8,128)S(1)}, f32[32,128]{1,0:T(8,128)S(1)}, u32[]{:S(2)}, u32[]{:S(2)}) collective-permute-start(f32[32,128]{1,0:T(8,128)S(1)} %get-tuple-element.48), channel_id=1, source_target_pairs={{0,128},{128,256},{256,384},{384,512},{512,640},{640,768},{768,896... | collective-permute-start | bytes 49160 | tf_op jit(solution)/shard_map/ppermute | solution.py:179
  30.8 9.1 %collective-permute-start.9 = (f32[32,128]{1,0:T(8,128)S(1)}, f32[32,128]{1,0:T(8,128)S(1)}, u32[]{:S(2)}, u32[]{:S(2)}) collective-permute-start(f32[32,128]{1,0:T(8,128)S(1)} %get-tuple-element.49), channel_id=1, source_target_pairs={{1,2},{3,4},{5,6},{7,8},{9,10},{11,12},{13,14},{15,16},{17,18},{19... | collective-permute-start | bytes 49160 | tf_op jit(solution)/shard_map/ppermute | solution.py:174
  31.5 8.5 %collective-permute-start.10 = (f32[32,128]{1,0:T(8,128)S(1)}, f32[32,128]{1,0:T(8,128)S(1)}, u32[]{:S(2)}, u32[]{:S(2)}) collective-permute-start(f32[32,128]{1,0:T(8,128)S(1)} %get-tuple-element.50), channel_id=1, source_target_pairs={{0,1},{2,3},{4,5},{6,7},{8,9},{10,11},{12,13},{14,15},{16,17},{18,... | collective-permute-start | bytes 49160 | tf_op jit(solution)/shard_map/ppermute | solution.py:174
  36.3 4.5 %collective-permute-start.11 = (f32[32,128]{1,0:T(8,128)S(1)}, f32[32,128]{1,0:T(8,128)S(1)}, u32[]{:S(2)}, u32[]{:S(2)}) collective-permute-start(f32[32,128]{1,0:T(8,128)S(1)} %get-tuple-element.51), channel_id=1, source_target_pairs={{0,896},{128,0},{256,128},{384,256},{512,384},{640,512},{768,640},... | collective-permute-start | bytes 49160 | tf_op jit(solution)/shard_map/ppermute | solution.py:179
  41.3 10.1 %collective-permute-start.12 = (f32[32,128]{1,0:T(8,128)S(1)}, f32[32,128]{1,0:T(8,128)S(1)}, u32[]{:S(2)}, u32[]{:S(2)}) collective-permute-start(f32[32,128]{1,0:T(8,128)S(1)} %get-tuple-element.52), channel_id=1, source_target_pairs={{0,128},{128,256},{256,384},{384,512},{512,640},{640,768},{768,896... | collective-permute-start | bytes 49160 | tf_op jit(solution)/shard_map/ppermute | solution.py:179
  41.3 10.1 %collective-permute-start.13 = (f32[32,128]{1,0:T(8,128)S(1)}, f32[32,128]{1,0:T(8,128)S(1)}, u32[]{:S(2)}, u32[]{:S(2)}) collective-permute-start(f32[32,128]{1,0:T(8,128)S(1)} %get-tuple-element.53), channel_id=1, source_target_pairs={{1,2},{3,4},{5,6},{7,8},{9,10},{11,12},{13,14},{15,16},{17,18},{19... | collective-permute-start | bytes 49160 | tf_op jit(solution)/shard_map/ppermute | solution.py:174
  42.0 9.4 %collective-permute-start.14 = (f32[32,128]{1,0:T(8,128)S(1)}, f32[32,128]{1,0:T(8,128)S(1)}, u32[]{:S(2)}, u32[]{:S(2)}) collective-permute-start(f32[32,128]{1,0:T(8,128)S(1)} %get-tuple-element.54), channel_id=1, source_target_pairs={{0,1},{2,3},{4,5},{6,7},{8,9},{10,11},{12,13},{14,15},{16,17},{18,... | collective-permute-start | bytes 49160 | tf_op jit(solution)/shard_map/ppermute | solution.py:174
  49.5 3.2 %collective-permute-start.15 = (f32[32,128]{1,0:T(8,128)S(1)}, f32[32,128]{1,0:T(8,128)S(1)}, u32[]{:S(2)}, u32[]{:S(2)}) collective-permute-start(f32[32,128]{1,0:T(8,128)S(1)} %get-tuple-element.55), channel_id=1, source_target_pairs={{0,896},{128,0},{256,128},{384,256},{512,384},{640,512},{768,640},... | collective-permute-start | bytes 49160 | tf_op jit(solution)/shard_map/ppermute | solution.py:179

commit v5 on v3

--- a/solution.py
+++ b/solution.py
@@ -1,3 +1,5 @@
+import functools
+
 import jax
 import jax.numpy as jnp
 from jax import lax
@@ -152,6 +154,11 @@
     remaining = b_ref[...] - operate(x_ref[...], (g0, g1, g2, g3), hot, coeff, diag)
     sums = jnp.sum(remaining * remaining, axis=0, keepdims=True)
     sum_ref[...] = jnp.broadcast_to(sums, sum_ref.shape)
+
+
+def norm_kernel(cells, part_ref, norm_ref):
+    mean = jnp.sum(part_ref[...], keepdims=True) / cells
+    norm_ref[0, 0] = jnp.sqrt(mean + 1e-06)[0, 0]
 
 
 def swap(block, first):
@@ -194,9 +201,16 @@
     part = call(kernel_4, f32(near, 128), held_b, solved, *groups, hot, coeff, diag)
     part = lax.all_to_all(part, NEAR, 0, 0, tiled=True)
     part = jnp.broadcast_to(jnp.sum(part, axis=0, keepdims=True), (far, 128))
-    total = jnp.sum(lax.all_to_all(part, FAR, 0, 0, tiled=True))
+    part = lax.all_to_all(part, FAR, 0, 0, tiled=True)
     cells_all = right_side.shape[0] * 128 * near * far
-    return solution_field, jnp.sqrt(total / cells_all + 1e-06)
+    norm = pl.pallas_call(
+        functools.partial(norm_kernel, float(cells_all)),
+        out_shape=f32(1, 1),
+        in_specs=[pl.BlockSpec(memory_space=pltpu.VMEM)],
+        out_specs=pl.BlockSpec(memory_space=pltpu.SMEM),
+        compiler_params=PARAMS,
+    )(part)
+    return solution_field, norm.reshape(())
 
 
 def solution(mesh):

time: 99.3 us -> 97.6 us (0.983)
  between operations: 2.65 us -> 0.83 us
where the time goes in v5:
time: 97.6 us; the launch traced here: 97.1 us
  starting transfers between devices  46.5 us (48%)
  blocking collectives  41.7 us (43%)
  Pallas kernels  3.46 us (4%)
  waiting for transfers between devices  2.86 us (3%)
  local copies, waits for them, and re-layouts  1.63 us (2%)
    ppermute x8, starting transfers between devices, swap(): return lax.ppermute(block, GY, pairs + [(j, i) for i, j in pairs])  30.2 us
    all_to_all x1, blocking collectives, shards(): part = lax.all_to_all(part, NEAR, 0, 0, tiled=True)  24.6 us
    all_to_all x1, blocking collectives, shards(): part = lax.all_to_all(part, FAR, 0, 0, tiled=True)  17 us
    ppermute x8, starting transfers between devices, cycle(): lax.ppermute(block, axis, [(i, (i + distance) % n) for i in range(n)])  16.4 us
    ppermute x8, waiting for transfers between devices, cycle(): lax.ppermute(block, axis, [(i, (i + distance) % n) for i in range(n)])  2.84 us
    pallas_call x8, Pallas kernels, call(): pl.pallas_call(kernel, out_shape=outs, in_specs=[spec] * len(args), out_s...  2.78 us
  transfers between devices with their start and end apart: 16, of which 3 were waited for; matrix products, arithmetic and copies ran while one was open for 0% of the time, Pallas kernels for 1%

profile of v5, /device:TPU:1, one launch (start us, length us, event | category | flops | bytes accessed | tf_op | source)
XLA Modules:
  0.0 97.1 jit_solution(10874350042607681578)
XLA Ops:
  0.6 0.7 copy-done.4
  1.3 0.1 shard_map.68.pick_ref.pick
  1.4 0.0 copy-start.1
  1.4 0.2 shard_map.69
  1.6 2.6 %collective-permute-start = (f32[32,128]{1,0:T(8,128)S(1)}, f32[32,128]{1,0:T(8,128)S(1)}, u32[]{:S(2)}, u32[]{:S(2)}) collective-permute-start(f32[32,128]{1,0:T(8,128)S(1)} %get-tuple-element.33), channel_id=1, source_target_pairs={{0,128},{128,256},{256,384},{384,512},{512,640},{640,768},{768,896... | collective-permute-start | bytes 49160 | tf_op jit(solution)/shard_map/ppermute | solution.py:172
  4.2 0.8 collective-permute-start.1
  5.0 7.3 %collective-permute-start.2 = (f32[32,128]{1,0:T(8,128)S(1)}, f32[32,128]{1,0:T(8,128)S(1)}, u32[]{:S(2)}, u32[]{:S(2)}) collective-permute-start(f32[32,128]{1,0:T(8,128)S(1)} %get-tuple-element.35), channel_id=1, source_target_pairs={{0,1},{2,3},{4,5},{6,7},{8,9},{10,11},{12,13},{14,15},{16,17},{18,... | collective-permute-start | bytes 49160 | tf_op jit(solution)/shard_map/ppermute | solution.py:167
  12.3 6.0 %collective-permute-start.3 = (f32[32,128]{1,0:T(8,128)S(1)}, f32[32,128]{1,0:T(8,128)S(1)}, u32[]{:S(2)}, u32[]{:S(2)}) collective-permute-start(f32[32,128]{1,0:T(8,128)S(1)} %get-tuple-element.36), channel_id=1, source_target_pairs={{0,896},{128,0},{256,128},{384,256},{512,384},{640,512},{768,640},... | collective-permute-start | bytes 49160 | tf_op jit(solution)/shard_map/ppermute | solution.py:172
  18.4 0.0 copy-done.1
  18.4 0.9 copy-done
  19.3 0.1 shard_map.70
  19.4 0.0 collective-permute-done.g0
  19.5 0.0 collective-permute-done.1.g1
  19.5 0.0 collective-permute-done.2.g2
  19.5 0.0 collective-permute-done.3.g3
  19.5 0.5 shard_map.71
  20.0 0.0 collective-permute-start.4
  20.0 0.7 collective-permute-start.5
  20.7 4.9 %collective-permute-start.6 = (f32[32,128]{1,0:T(8,128)S(1)}, f32[32,128]{1,0:T(8,128)S(1)}, u32[]{:S(2)}, u32[]{:S(2)}) collective-permute-start(f32[32,128]{1,0:T(8,128)S(1)} %get-tuple-element.44), channel_id=1, source_target_pairs={{0,1},{2,3},{4,5},{6,7},{8,9},{10,11},{12,13},{14,15},{16,17},{18,... | collective-permute-start | bytes 49160 | tf_op jit(solution)/shard_map/ppermute | solution.py:167
  25.6 3.4 %collective-permute-start.7 = (f32[32,128]{1,0:T(8,128)S(1)}, f32[32,128]{1,0:T(8,128)S(1)}, u32[]{:S(2)}, u32[]{:S(2)}) collective-permute-start(f32[32,128]{1,0:T(8,128)S(1)} %get-tuple-element.45), channel_id=1, source_target_pairs={{0,896},{128,0},{256,128},{384,256},{512,384},{640,512},{768,640},... | collective-permute-start | bytes 49160 | tf_op jit(solution)/shard_map/ppermute | solution.py:172
  29.0 0.0 collective-permute-done.4.g0
  29.0 0.0 collective-permute-done.5.g1
  29.0 0.0 collective-permute-done.6.g2
  29.0 0.8 collective-permute-done.7.g3
  29.8 0.5 shard_map.72
  30.3 0.0 collective-permute-start.8
  30.3 0.7 collective-permute-start.9
  31.0 6.6 %collective-permute-start.10 = (f32[32,128]{1,0:T(8,128)S(1)}, f32[32,128]{1,0:T(8,128)S(1)}, u32[]{:S(2)}, u32[]{:S(2)}) collective-permute-start(f32[32,128]{1,0:T(8,128)S(1)} %get-tuple-element.50), channel_id=1, source_target_pairs={{0,1},{2,3},{4,5},{6,7},{8,9},{10,11},{12,13},{14,15},{16,17},{18,... | collective-permute-start | bytes 49160 | tf_op jit(solution)/shard_map/ppermute | solution.py:167
  37.6 1.8 %collective-permute-start.11 = (f32[32,128]{1,0:T(8,128)S(1)}, f32[32,128]{1,0:T(8,128)S(1)}, u32[]{:S(2)}, u32[]{:S(2)}) collective-permute-start(f32[32,128]{1,0:T(8,128)S(1)} %get-tuple-element.51), channel_id=1, source_target_pairs={{0,896},{128,0},{256,128},{384,256},{512,384},{640,512},{768,640},... | collective-permute-start | bytes 49160 | tf_op jit(solution)/shard_map/ppermute | solution.py:172
  39.4 0.0 collective-permute-done.8.g0
  39.4 0.0 collective-permute-done.9.g1
  39.4 0.0 collective-permute-done.10.g2
  39.4 1.3 %collective-permute-done.11.g3 = f32[32,128]{1,0:T(8,128)S(1)} collective-permute-done((f32[32,128]{1,0:T(8,128)S(1)}, f32[32,128]{1,0:T(8,128)S(1)}, u32[]{:S(2)}, u32[]{:S(2)}) %collective-permute-start.11) | collective-permute-done | bytes 16416 | tf_op jit(solution)/shard_map/ppermute | solution.py:172
  40.8 0.5 shard_map.73
  41.3 0.1 collective-permute-start.12
  41.4 0.7 collective-permute-start.13
  42.1 8.6 %collective-permute-start.14 = (f32[32,128]{1,0:T(8,128)S(1)}, f32[32,128]{1,0:T(8,128)S(1)}, u32[]{:S(2)}, u32[]{:S(2)}) collective-permute-start(f32[32,128]{1,0:T(8,128)S(1)} %get-tuple-element.54), channel_id=1, source_target_pairs={{0,1},{2,3},{4,5},{6,7},{8,9},{10,11},{12,13},{14,15},{16,17},{18,... | collective-permute-start | bytes 49160 | tf_op jit(solution)/shard_map/ppermute | solution.py:167
  50.6 2.4 %collective-permute-start.15 = (f32[32,128]{1,0:T(8,128)S(1)}, f32[32,128]{1,0:T(8,128)S(1)}, u32[]{:S(2)}, u32[]{:S(2)}) collective-permute-start(f32[32,128]{1,0:T(8,128)S(1)} %get-tuple-element.55), channel_id=1, source_target_pairs={{0,896},{128,0},{256,128},{384,256},{512,384},{640,512},{768,640},... | collective-permute-start | bytes 49160 | tf_op jit(solution)/shard_map/ppermute | solution.py:172
  53.0 0.6 shard_map.74
  53.6 0.0 collective-permute-done.12.g0
  53.6 0.0 collective-permute-done.13.g1
  53.6 0.0 collective-permute-done.14.g2
  53.6 0.7 collective-permute-done.15.g3
  54.3 0.3 shard_map.75
  54.6 24.6 %all_to_all.17 = f32[64,1,128]{2,1,0:T(1,128)S(1)} all-to-all(f32[64,1,128]{2,1,0:T(1,128)S(1)} %bitcast.8), channel_id=1, replica_groups=mesh['gx_0'=4,'gx_1'=2,'gy_0'=8,'gy_1'=16] {'gx_0','gx_1','gy_0'}, dimensions={0} | all-to-all | bytes 65536 | tf_op jit(solution)/shard_map/all_to_all | solution.py:202
  79.3 0.1 reduce_sum.9
  79.4 17.0 %all_to_all.18 = f32[16,1,128]{2,1,0:T(1,128)S(1)} all-to-all(f32[16,1,128]{2,1,0:T(1,128)S(1)} %broadcast_in_dim.2), channel_id=1, replica_groups=mesh['gx_0'=4,'gx_1'=2,'gy_0'=8,'gy_1'=16] {'gy_1'}, dimensions={0} | all-to-all | bytes 16384 | tf_op jit(solution)/shard_map/all_to_all | solution.py:204
  96.4 0.7 shard_map.76
  (7 shorter events, 0.0 us)
Async XLA Ops:
  0.6 0.8 copy-start.2
  0.6 0.7 copy-start.4
  1.4 16.9 %copy-start.1 = (f32[64,128]{1,0:T(8,128)S(1)}, f32[64,128]{1,0:T(8,128)}, u32[]{:S(2)}) copy-start(f32[64,128]{1,0:T(8,128)} %mass_ref.1) | copy-start | bytes 98308
  1.6 17.8 %collective-permute-start = (f32[32,128]{1,0:T(8,128)S(1)}, f32[32,128]{1,0:T(8,128)S(1)}, u32[]{:S(2)}, u32[]{:S(2)}) collective-permute-start(f32[32,128]{1,0:T(8,128)S(1)} %get-tuple-element.33), channel_id=1, source_target_pairs={{0,128},{128,256},{256,384},{384,512},{512,640},{640,768},{768,896... | collective-permute-start | bytes 49160 | tf_op jit(solution)/shard_map/ppermute | solution.py:172
  4.2 14.2 %copy-start.3 = (s32[64,6]{0,1:T(8,128)S(1)}, s32[64,6]{0,1:T(8,128)}, u32[]{:S(2)}) copy-start(s32[64,6]{0,1:T(8,128)} %param.8) | copy-start | bytes 4612
  4.2 15.3 %collective-permute-start.1 = (f32[32,128]{1,0:T(8,128)S(1)}, f32[32,128]{1,0:T(8,128)S(1)}, u32[]{:S(2)}, u32[]{:S(2)}) collective-permute-start(f32[32,128]{1,0:T(8,128)S(1)} %get-tuple-element.34), channel_id=1, source_target_pairs={{1,2},{3,4},{5,6},{7,8},{9,10},{11,12},{13,14},{15,16},{17,18},{19... | collective-permute-start | bytes 49160 | tf_op jit(solution)/shard_map/ppermute | solution.py:167
  5.0 14.5 %collective-permute-start.2 = (f32[32,128]{1,0:T(8,128)S(1)}, f32[32,128]{1,0:T(8,128)S(1)}, u32[]{:S(2)}, u32[]{:S(2)}) collective-permute-start(f32[32,128]{1,0:T(8,128)S(1)} %get-tuple-element.35), channel_id=1, source_target_pairs={{0,1},{2,3},{4,5},{6,7},{8,9},{10,11},{12,13},{14,15},{16,17},{18,... | collective-permute-start | bytes 49160 | tf_op jit(solution)/shard_map/ppermute | solution.py:167
  12.3 7.1 %collective-permute-start.3 = (f32[32,128]{1,0:T(8,128)S(1)}, f32[32,128]{1,0:T(8,128)S(1)}, u32[]{:S(2)}, u32[]{:S(2)}) collective-permute-start(f32[32,128]{1,0:T(8,128)S(1)} %get-tuple-element.36), channel_id=1, source_target_pairs={{0,896},{128,0},{256,128},{384,256},{512,384},{640,512},{768,640},... | collective-permute-start | bytes 49160 | tf_op jit(solution)/shard_map/ppermute | solution.py:172
  18.4 0.9 copy-start
  20.0 9.0 %collective-permute-start.4 = (f32[32,128]{1,0:T(8,128)S(1)}, f32[32,128]{1,0:T(8,128)S(1)}, u32[]{:S(2)}, u32[]{:S(2)}) collective-permute-start(f32[32,128]{1,0:T(8,128)S(1)} %get-tuple-element.42), channel_id=1, source_target_pairs={{0,128},{128,256},{256,384},{384,512},{512,640},{640,768},{768,896... | collective-permute-start | bytes 49160 | tf_op jit(solution)/shard_map/ppermute | solution.py:172
  20.0 9.0 %collective-permute-start.5 = (f32[32,128]{1,0:T(8,128)S(1)}, f32[32,128]{1,0:T(8,128)S(1)}, u32[]{:S(2)}, u32[]{:S(2)}) collective-permute-start(f32[32,128]{1,0:T(8,128)S(1)} %get-tuple-element.43), channel_id=1, source_target_pairs={{1,2},{3,4},{5,6},{7,8},{9,10},{11,12},{13,14},{15,16},{17,18},{19... | collective-permute-start | bytes 49160 | tf_op jit(solution)/shard_map/ppermute | solution.py:167
  20.7 8.3 %collective-permute-start.6 = (f32[32,128]{1,0:T(8,128)S(1)}, f32[32,128]{1,0:T(8,128)S(1)}, u32[]{:S(2)}, u32[]{:S(2)}) collective-permute-start(f32[32,128]{1,0:T(8,128)S(1)} %get-tuple-element.44), channel_id=1, source_target_pairs={{0,1},{2,3},{4,5},{6,7},{8,9},{10,11},{12,13},{14,15},{16,17},{18,... | collective-permute-start | bytes 49160 | tf_op jit(solution)/shard_map/ppermute | solution.py:167
  25.6 4.2 %collective-permute-start.7 = (f32[32,128]{1,0:T(8,128)S(1)}, f32[32,128]{1,0:T(8,128)S(1)}, u32[]{:S(2)}, u32[]{:S(2)}) collective-permute-start(f32[32,128]{1,0:T(8,128)S(1)} %get-tuple-element.45), channel_id=1, source_target_pairs={{0,896},{128,0},{256,128},{384,256},{512,384},{640,512},{768,640},... | collective-permute-start | bytes 49160 | tf_op jit(solution)/shard_map/ppermute | solution.py:172
  30.3 9.2 %collective-permute-start.8 = (f32[32,128]{1,0:T(8,128)S(1)}, f32[32,128]{1,0:T(8,128)S(1)}, u32[]{:S(2)}, u32[]{:S(2)}) collective-permute-start(f32[32,128]{1,0:T(8,128)S(1)} %get-tuple-element.48), channel_id=1, source_target_pairs={{0,128},{128,256},{256,384},{384,512},{512,640},{640,768},{768,896... | collective-permute-start | bytes 49160 | tf_op jit(solution)/shard_map/ppermute | solution.py:172
  30.3 9.1 %collective-permute-start.9 = (f32[32,128]{1,0:T(8,128)S(1)}, f32[32,128]{1,0:T(8,128)S(1)}, u32[]{:S(2)}, u32[]{:S(2)}) collective-permute-start(f32[32,128]{1,0:T(8,128)S(1)} %get-tuple-element.49), channel_id=1, source_target_pairs={{1,2},{3,4},{5,6},{7,8},{9,10},{11,12},{13,14},{15,16},{17,18},{19... | collective-permute-start | bytes 49160 | tf_op jit(solution)/shard_map/ppermute | solution.py:167
  31.0 8.5 %collective-permute-start.10 = (f32[32,128]{1,0:T(8,128)S(1)}, f32[32,128]{1,0:T(8,128)S(1)}, u32[]{:S(2)}, u32[]{:S(2)}) collective-permute-start(f32[32,128]{1,0:T(8,128)S(1)} %get-tuple-element.50), channel_id=1, source_target_pairs={{0,1},{2,3},{4,5},{6,7},{8,9},{10,11},{12,13},{14,15},{16,17},{18,... | collective-permute-start | bytes 49160 | tf_op jit(solution)/shard_map/ppermute | solution.py:167
  37.6 3.2 %collective-permute-start.11 = (f32[32,128]{1,0:T(8,128)S(1)}, f32[32,128]{1,0:T(8,128)S(1)}, u32[]{:S(2)}, u32[]{:S(2)}) collective-permute-start(f32[32,128]{1,0:T(8,128)S(1)} %get-tuple-element.51), channel_id=1, source_target_pairs={{0,896},{128,0},{256,128},{384,256},{512,384},{640,512},{768,640},... | collective-permute-start | bytes 49160 | tf_op jit(solution)/shard_map/ppermute | solution.py:172
  41.3 12.4 %collective-permute-start.12 = (f32[32,128]{1,0:T(8,128)S(1)}, f32[32,128]{1,0:T(8,128)S(1)}, u32[]{:S(2)}, u32[]{:S(2)}) collective-permute-start(f32[32,128]{1,0:T(8,128)S(1)} %get-tuple-element.52), channel_id=1, source_target_pairs={{0,128},{128,256},{256,384},{384,512},{512,640},{640,768},{768,896... | collective-permute-start | bytes 49160 | tf_op jit(solution)/shard_map/ppermute | solution.py:172
  41.4 12.2 %collective-permute-start.13 = (f32[32,128]{1,0:T(8,128)S(1)}, f32[32,128]{1,0:T(8,128)S(1)}, u32[]{:S(2)}, u32[]{:S(2)}) collective-permute-start(f32[32,128]{1,0:T(8,128)S(1)} %get-tuple-element.53), channel_id=1, source_target_pairs={{1,2},{3,4},{5,6},{7,8},{9,10},{11,12},{13,14},{15,16},{17,18},{19... | collective-permute-start | bytes 49160 | tf_op jit(solution)/shard_map/ppermute | solution.py:167
  42.1 11.6 %collective-permute-start.14 = (f32[32,128]{1,0:T(8,128)S(1)}, f32[32,128]{1,0:T(8,128)S(1)}, u32[]{:S(2)}, u32[]{:S(2)}) collective-permute-start(f32[32,128]{1,0:T(8,128)S(1)} %get-tuple-element.54), channel_id=1, source_target_pairs={{0,1},{2,3},{4,5},{6,7},{8,9},{10,11},{12,13},{14,15},{16,17},{18,... | collective-permute-start | bytes 49160 | tf_op jit(solution)/shard_map/ppermute | solution.py:167
  50.6 3.7 %collective-permute-start.15 = (f32[32,128]{1,0:T(8,128)S(1)}, f32[32,128]{1,0:T(8,128)S(1)}, u32[]{:S(2)}, u32[]{:S(2)}) collective-permute-start(f32[32,128]{1,0:T(8,128)S(1)} %get-tuple-element.55), channel_id=1, source_target_pairs={{0,896},{128,0},{256,128},{384,256},{512,384},{640,512},{768,640},... | collective-permute-start | bytes 49160 | tf_op jit(solution)/shard_map/ppermute | solution.py:172

commit v6 on v5

--- a/solution.py
+++ b/solution.py
@@ -15,8 +15,8 @@
 GY = ("gy_0", "gy_1")
 GX = ("gx_0", "gx_1")
 GX_GY = ("gx_0", "gx_1", "gy_0", "gy_1")
-NEAR = ("gx_0", "gx_1", "gy_0")
-FAR = ("gy_1",)
+NEAR = ("gx_0", "gy_0")
+FAR = ("gx_1", "gy_1")
 
 spectrum_low = 0.5
 spectrum_high = 7.0

time: 97.6 us -> 97.8 us (level)
    all_to_all x1, blocking collectives: 17 us -> 18.4 us  [shards(): part = lax.all_to_all(part, FAR, 0, 0, tiled=True)]
    all_to_all x1, blocking collectives: 24.6 us -> 23.5 us  [shards(): part = lax.all_to_all(part, NEAR, 0, 0, tiled=True)]
where the time goes in v6:
time: 97.8 us; the launch traced here: 97.3 us
  starting transfers between devices  46.5 us (48%)
  blocking collectives  41.9 us (43%)
  Pallas kernels  3.46 us (4%)
  waiting for transfers between devices  2.86 us (3%)
  local copies, waits for them, and re-layouts  1.64 us (2%)
    ppermute x8, starting transfers between devices, swap(): return lax.ppermute(block, GY, pairs + [(j, i) for i, j in pairs])  30.2 us
    all_to_all x1, blocking collectives, shards(): part = lax.all_to_all(part, NEAR, 0, 0, tiled=True)  23.5 us
    all_to_all x1, blocking collectives, shards(): part = lax.all_to_all(part, FAR, 0, 0, tiled=True)  18.4 us
    ppermute x8, starting transfers between devices, cycle(): lax.ppermute(block, axis, [(i, (i + distance) % n) for i in range(n)])  16.4 us
    ppermute x8, waiting for transfers between devices, cycle(): lax.ppermute(block, axis, [(i, (i + distance) % n) for i in range(n)])  2.84 us
    pallas_call x8, Pallas kernels, call(): pl.pallas_call(kernel, out_shape=outs, in_specs=[spec] * len(args), out_s...  2.78 us
  transfers between devices with their start and end apart: 16, of which 3 were waited for; matrix products, arithmetic and copies ran while one was open for 0% of the time, Pallas kernels for 1%

profile of v6, /device:TPU:1, one launch (start us, length us, event | category | flops | bytes accessed | tf_op | source)
XLA Modules:
  0.0 97.3 jit_solution(10993019039201614691)
XLA Ops:
  0.6 0.7 copy-done.4
  1.3 0.1 shard_map.68.pick_ref.pick
  1.4 0.0 copy-start.1
  1.4 0.2 shard_map.69
  1.6 2.6 %collective-permute-start = (f32[32,128]{1,0:T(8,128)S(1)}, f32[32,128]{1,0:T(8,128)S(1)}, u32[]{:S(2)}, u32[]{:S(2)}) collective-permute-start(f32[32,128]{1,0:T(8,128)S(1)} %get-tuple-element.33), channel_id=1, source_target_pairs={{0,128},{128,256},{256,384},{384,512},{512,640},{640,768},{768,896... | collective-permute-start | bytes 49160 | tf_op jit(solution)/shard_map/ppermute | solution.py:172
  4.2 0.8 collective-permute-start.1
  5.0 7.3 %collective-permute-start.2 = (f32[32,128]{1,0:T(8,128)S(1)}, f32[32,128]{1,0:T(8,128)S(1)}, u32[]{:S(2)}, u32[]{:S(2)}) collective-permute-start(f32[32,128]{1,0:T(8,128)S(1)} %get-tuple-element.35), channel_id=1, source_target_pairs={{0,1},{2,3},{4,5},{6,7},{8,9},{10,11},{12,13},{14,15},{16,17},{18,... | collective-permute-start | bytes 49160 | tf_op jit(solution)/shard_map/ppermute | solution.py:167
  12.3 6.0 %collective-permute-start.3 = (f32[32,128]{1,0:T(8,128)S(1)}, f32[32,128]{1,0:T(8,128)S(1)}, u32[]{:S(2)}, u32[]{:S(2)}) collective-permute-start(f32[32,128]{1,0:T(8,128)S(1)} %get-tuple-element.36), channel_id=1, source_target_pairs={{0,896},{128,0},{256,128},{384,256},{512,384},{640,512},{768,640},... | collective-permute-start | bytes 49160 | tf_op jit(solution)/shard_map/ppermute | solution.py:172
  18.4 0.0 copy-done.1
  18.4 0.9 copy-done
  19.3 0.1 shard_map.70
  19.4 0.0 collective-permute-done.g0
  19.5 0.0 collective-permute-done.1.g1
  19.5 0.0 collective-permute-done.2.g2
  19.5 0.0 collective-permute-done.3.g3
  19.5 0.5 shard_map.71
  20.0 0.0 collective-permute-start.4
  20.0 0.7 collective-permute-start.5
  20.7 4.9 %collective-permute-start.6 = (f32[32,128]{1,0:T(8,128)S(1)}, f32[32,128]{1,0:T(8,128)S(1)}, u32[]{:S(2)}, u32[]{:S(2)}) collective-permute-start(f32[32,128]{1,0:T(8,128)S(1)} %get-tuple-element.44), channel_id=1, source_target_pairs={{0,1},{2,3},{4,5},{6,7},{8,9},{10,11},{12,13},{14,15},{16,17},{18,... | collective-permute-start | bytes 49160 | tf_op jit(solution)/shard_map/ppermute | solution.py:167
  25.6 3.4 %collective-permute-start.7 = (f32[32,128]{1,0:T(8,128)S(1)}, f32[32,128]{1,0:T(8,128)S(1)}, u32[]{:S(2)}, u32[]{:S(2)}) collective-permute-start(f32[32,128]{1,0:T(8,128)S(1)} %get-tuple-element.45), channel_id=1, source_target_pairs={{0,896},{128,0},{256,128},{384,256},{512,384},{640,512},{768,640},... | collective-permute-start | bytes 49160 | tf_op jit(solution)/shard_map/ppermute | solution.py:172
  29.0 0.0 collective-permute-done.4.g0
  29.0 0.0 collective-permute-done.5.g1
  29.0 0.0 collective-permute-done.6.g2
  29.0 0.8 collective-permute-done.7.g3
  29.8 0.5 shard_map.72
  30.3 0.0 collective-permute-start.8
  30.3 0.7 collective-permute-start.9
  31.0 6.6 %collective-permute-start.10 = (f32[32,128]{1,0:T(8,128)S(1)}, f32[32,128]{1,0:T(8,128)S(1)}, u32[]{:S(2)}, u32[]{:S(2)}) collective-permute-start(f32[32,128]{1,0:T(8,128)S(1)} %get-tuple-element.50), channel_id=1, source_target_pairs={{0,1},{2,3},{4,5},{6,7},{8,9},{10,11},{12,13},{14,15},{16,17},{18,... | collective-permute-start | bytes 49160 | tf_op jit(solution)/shard_map/ppermute | solution.py:167
  37.6 1.8 %collective-permute-start.11 = (f32[32,128]{1,0:T(8,128)S(1)}, f32[32,128]{1,0:T(8,128)S(1)}, u32[]{:S(2)}, u32[]{:S(2)}) collective-permute-start(f32[32,128]{1,0:T(8,128)S(1)} %get-tuple-element.51), channel_id=1, source_target_pairs={{0,896},{128,0},{256,128},{384,256},{512,384},{640,512},{768,640},... | collective-permute-start | bytes 49160 | tf_op jit(solution)/shard_map/ppermute | solution.py:172
  39.4 0.0 collective-permute-done.8.g0
  39.4 0.0 collective-permute-done.9.g1
  39.4 0.0 collective-permute-done.10.g2
  39.4 1.3 %collective-permute-done.11.g3 = f32[32,128]{1,0:T(8,128)S(1)} collective-permute-done((f32[32,128]{1,0:T(8,128)S(1)}, f32[32,128]{1,0:T(8,128)S(1)}, u32[]{:S(2)}, u32[]{:S(2)}) %collective-permute-start.11) | collective-permute-done | bytes 16416 | tf_op jit(solution)/shard_map/ppermute | solution.py:172
  40.8 0.5 shard_map.73
  41.3 0.1 collective-permute-start.12
  41.4 0.7 collective-permute-start.13
  42.1 8.6 %collective-permute-start.14 = (f32[32,128]{1,0:T(8,128)S(1)}, f32[32,128]{1,0:T(8,128)S(1)}, u32[]{:S(2)}, u32[]{:S(2)}) collective-permute-start(f32[32,128]{1,0:T(8,128)S(1)} %get-tuple-element.54), channel_id=1, source_target_pairs={{0,1},{2,3},{4,5},{6,7},{8,9},{10,11},{12,13},{14,15},{16,17},{18,... | collective-permute-start | bytes 49160 | tf_op jit(solution)/shard_map/ppermute | solution.py:167
  50.6 2.4 %collective-permute-start.15 = (f32[32,128]{1,0:T(8,128)S(1)}, f32[32,128]{1,0:T(8,128)S(1)}, u32[]{:S(2)}, u32[]{:S(2)}) collective-permute-start(f32[32,128]{1,0:T(8,128)S(1)} %get-tuple-element.55), channel_id=1, source_target_pairs={{0,896},{128,0},{256,128},{384,256},{512,384},{640,512},{768,640},... | collective-permute-start | bytes 49160 | tf_op jit(solution)/shard_map/ppermute | solution.py:172
  53.0 0.6 shard_map.74
  53.6 0.0 collective-permute-done.12.g0
  53.6 0.0 collective-permute-done.13.g1
  53.6 0.0 collective-permute-done.14.g2
  53.6 0.7 collective-permute-done.15.g3
  54.3 0.3 shard_map.75
  54.6 23.5 %all_to_all.17 = f32[32,1,128]{2,1,0:T(1,128)S(1)} all-to-all(f32[32,1,128]{2,1,0:T(1,128)S(1)} %bitcast.8), channel_id=1, replica_groups=mesh['gx_0'=4,'gx_1'=2,'gy_0'=8,'gy_1'=16] {'gx_0','gy_0'}, dimensions={0} | all-to-all | bytes 32768 | tf_op jit(solution)/shard_map/all_to_all | solution.py:202
  78.1 0.1 reduce_sum.9
  78.2 18.4 %all_to_all.18 = f32[32,1,128]{2,1,0:T(1,128)S(1)} all-to-all(f32[32,1,128]{2,1,0:T(1,128)S(1)} %broadcast_in_dim.2), channel_id=1, replica_groups=mesh['gx_0'=4,'gx_1'=2,'gy_0'=8,'gy_1'=16] {'gx_1','gy_1'}, dimensions={0} | all-to-all | bytes 32768 | tf_op jit(solution)/shard_map/all_to_all | solution.py:204
  96.6 0.7 shard_map.76
  (7 shorter events, 0.0 us)
Async XLA Ops:
  0.6 0.8 copy-start.2
  0.6 0.7 copy-start.4
  1.4 16.9 %copy-start.1 = (f32[64,128]{1,0:T(8,128)S(1)}, f32[64,128]{1,0:T(8,128)}, u32[]{:S(2)}) copy-start(f32[64,128]{1,0:T(8,128)} %mass_ref.1) | copy-start | bytes 98308
  1.6 17.8 %collective-permute-start = (f32[32,128]{1,0:T(8,128)S(1)}, f32[32,128]{1,0:T(8,128)S(1)}, u32[]{:S(2)}, u32[]{:S(2)}) collective-permute-start(f32[32,128]{1,0:T(8,128)S(1)} %get-tuple-element.33), channel_id=1, source_target_pairs={{0,128},{128,256},{256,384},{384,512},{512,640},{640,768},{768,896... | collective-permute-start | bytes 49160 | tf_op jit(solution)/shard_map/ppermute | solution.py:172
  4.2 14.2 %copy-start.3 = (s32[64,6]{0,1:T(8,128)S(1)}, s32[64,6]{0,1:T(8,128)}, u32[]{:S(2)}) copy-start(s32[64,6]{0,1:T(8,128)} %param.8) | copy-start | bytes 4612
  4.2 15.3 %collective-permute-start.1 = (f32[32,128]{1,0:T(8,128)S(1)}, f32[32,128]{1,0:T(8,128)S(1)}, u32[]{:S(2)}, u32[]{:S(2)}) collective-permute-start(f32[32,128]{1,0:T(8,128)S(1)} %get-tuple-element.34), channel_id=1, source_target_pairs={{1,2},{3,4},{5,6},{7,8},{9,10},{11,12},{13,14},{15,16},{17,18},{19... | collective-permute-start | bytes 49160 | tf_op jit(solution)/shard_map/ppermute | solution.py:167
  5.0 14.5 %collective-permute-start.2 = (f32[32,128]{1,0:T(8,128)S(1)}, f32[32,128]{1,0:T(8,128)S(1)}, u32[]{:S(2)}, u32[]{:S(2)}) collective-permute-start(f32[32,128]{1,0:T(8,128)S(1)} %get-tuple-element.35), channel_id=1, source_target_pairs={{0,1},{2,3},{4,5},{6,7},{8,9},{10,11},{12,13},{14,15},{16,17},{18,... | collective-permute-start | bytes 49160 | tf_op jit(solution)/shard_map/ppermute | solution.py:167
  12.3 7.1 %collective-permute-start.3 = (f32[32,128]{1,0:T(8,128)S(1)}, f32[32,128]{1,0:T(8,128)S(1)}, u32[]{:S(2)}, u32[]{:S(2)}) collective-permute-start(f32[32,128]{1,0:T(8,128)S(1)} %get-tuple-element.36), channel_id=1, source_target_pairs={{0,896},{128,0},{256,128},{384,256},{512,384},{640,512},{768,640},... | collective-permute-start | bytes 49160 | tf_op jit(solution)/shard_map/ppermute | solution.py:172
  18.4 0.9 copy-start
  20.0 9.0 %collective-permute-start.4 = (f32[32,128]{1,0:T(8,128)S(1)}, f32[32,128]{1,0:T(8,128)S(1)}, u32[]{:S(2)}, u32[]{:S(2)}) collective-permute-start(f32[32,128]{1,0:T(8,128)S(1)} %get-tuple-element.42), channel_id=1, source_target_pairs={{0,128},{128,256},{256,384},{384,512},{512,640},{640,768},{768,896... | collective-permute-start | bytes 49160 | tf_op jit(solution)/shard_map/ppermute | solution.py:172
  20.0 9.0 %collective-permute-start.5 = (f32[32,128]{1,0:T(8,128)S(1)}, f32[32,128]{1,0:T(8,128)S(1)}, u32[]{:S(2)}, u32[]{:S(2)}) collective-permute-start(f32[32,128]{1,0:T(8,128)S(1)} %get-tuple-element.43), channel_id=1, source_target_pairs={{1,2},{3,4},{5,6},{7,8},{9,10},{11,12},{13,14},{15,16},{17,18},{19... | collective-permute-start | bytes 49160 | tf_op jit(solution)/shard_map/ppermute | solution.py:167
  20.7 8.3 %collective-permute-start.6 = (f32[32,128]{1,0:T(8,128)S(1)}, f32[32,128]{1,0:T(8,128)S(1)}, u32[]{:S(2)}, u32[]{:S(2)}) collective-permute-start(f32[32,128]{1,0:T(8,128)S(1)} %get-tuple-element.44), channel_id=1, source_target_pairs={{0,1},{2,3},{4,5},{6,7},{8,9},{10,11},{12,13},{14,15},{16,17},{18,... | collective-permute-start | bytes 49160 | tf_op jit(solution)/shard_map/ppermute | solution.py:167
  25.6 4.2 %collective-permute-start.7 = (f32[32,128]{1,0:T(8,128)S(1)}, f32[32,128]{1,0:T(8,128)S(1)}, u32[]{:S(2)}, u32[]{:S(2)}) collective-permute-start(f32[32,128]{1,0:T(8,128)S(1)} %get-tuple-element.45), channel_id=1, source_target_pairs={{0,896},{128,0},{256,128},{384,256},{512,384},{640,512},{768,640},... | collective-permute-start | bytes 49160 | tf_op jit(solution)/shard_map/ppermute | solution.py:172
  30.3 9.2 %collective-permute-start.8 = (f32[32,128]{1,0:T(8,128)S(1)}, f32[32,128]{1,0:T(8,128)S(1)}, u32[]{:S(2)}, u32[]{:S(2)}) collective-permute-start(f32[32,128]{1,0:T(8,128)S(1)} %get-tuple-element.48), channel_id=1, source_target_pairs={{0,128},{128,256},{256,384},{384,512},{512,640},{640,768},{768,896... | collective-permute-start | bytes 49160 | tf_op jit(solution)/shard_map/ppermute | solution.py:172
  30.3 9.1 %collective-permute-start.9 = (f32[32,128]{1,0:T(8,128)S(1)}, f32[32,128]{1,0:T(8,128)S(1)}, u32[]{:S(2)}, u32[]{:S(2)}) collective-permute-start(f32[32,128]{1,0:T(8,128)S(1)} %get-tuple-element.49), channel_id=1, source_target_pairs={{1,2},{3,4},{5,6},{7,8},{9,10},{11,12},{13,14},{15,16},{17,18},{19... | collective-permute-start | bytes 49160 | tf_op jit(solution)/shard_map/ppermute | solution.py:167
  31.0 8.5 %collective-permute-start.10 = (f32[32,128]{1,0:T(8,128)S(1)}, f32[32,128]{1,0:T(8,128)S(1)}, u32[]{:S(2)}, u32[]{:S(2)}) collective-permute-start(f32[32,128]{1,0:T(8,128)S(1)} %get-tuple-element.50), channel_id=1, source_target_pairs={{0,1},{2,3},{4,5},{6,7},{8,9},{10,11},{12,13},{14,15},{16,17},{18,... | collective-permute-start | bytes 49160 | tf_op jit(solution)/shard_map/ppermute | solution.py:167
  37.6 3.2 %collective-permute-start.11 = (f32[32,128]{1,0:T(8,128)S(1)}, f32[32,128]{1,0:T(8,128)S(1)}, u32[]{:S(2)}, u32[]{:S(2)}) collective-permute-start(f32[32,128]{1,0:T(8,128)S(1)} %get-tuple-element.51), channel_id=1, source_target_pairs={{0,896},{128,0},{256,128},{384,256},{512,384},{640,512},{768,640},... | collective-permute-start | bytes 49160 | tf_op jit(solution)/shard_map/ppermute | solution.py:172
  41.3 12.4 %collective-permute-start.12 = (f32[32,128]{1,0:T(8,128)S(1)}, f32[32,128]{1,0:T(8,128)S(1)}, u32[]{:S(2)}, u32[]{:S(2)}) collective-permute-start(f32[32,128]{1,0:T(8,128)S(1)} %get-tuple-element.52), channel_id=1, source_target_pairs={{0,128},{128,256},{256,384},{384,512},{512,640},{640,768},{768,896... | collective-permute-start | bytes 49160 | tf_op jit(solution)/shard_map/ppermute | solution.py:172
  41.4 12.2 %collective-permute-start.13 = (f32[32,128]{1,0:T(8,128)S(1)}, f32[32,128]{1,0:T(8,128)S(1)}, u32[]{:S(2)}, u32[]{:S(2)}) collective-permute-start(f32[32,128]{1,0:T(8,128)S(1)} %get-tuple-element.53), channel_id=1, source_target_pairs={{1,2},{3,4},{5,6},{7,8},{9,10},{11,12},{13,14},{15,16},{17,18},{19... | collective-permute-start | bytes 49160 | tf_op jit(solution)/shard_map/ppermute | solution.py:167
  42.1 11.6 %collective-permute-start.14 = (f32[32,128]{1,0:T(8,128)S(1)}, f32[32,128]{1,0:T(8,128)S(1)}, u32[]{:S(2)}, u32[]{:S(2)}) collective-permute-start(f32[32,128]{1,0:T(8,128)S(1)} %get-tuple-element.54), channel_id=1, source_target_pairs={{0,1},{2,3},{4,5},{6,7},{8,9},{10,11},{12,13},{14,15},{16,17},{18,... | collective-permute-start | bytes 49160 | tf_op jit(solution)/shard_map/ppermute | solution.py:167
  50.6 3.7 %collective-permute-start.15 = (f32[32,128]{1,0:T(8,128)S(1)}, f32[32,128]{1,0:T(8,128)S(1)}, u32[]{:S(2)}, u32[]{:S(2)}) collective-permute-start(f32[32,128]{1,0:T(8,128)S(1)} %get-tuple-element.55), channel_id=1, source_target_pairs={{0,896},{128,0},{256,128},{384,256},{512,384},{640,512},{768,640},... | collective-permute-start | bytes 49160 | tf_op jit(solution)/shard_map/ppermute | solution.py:172

commit v7 on v6

--- a/solution.py
+++ b/solution.py
@@ -48,13 +48,12 @@
     high = value.astype(jnp.bfloat16)
     rest = value - high.astype(jnp.float32)
     middle = rest.astype(jnp.bfloat16)
-    low = (rest - middle.astype(jnp.float32)).astype(jnp.bfloat16)
-    return jnp.concatenate([high, middle, low], axis=1)
+    return jnp.concatenate([high, middle], axis=1)
 
 
 def chosen(one_hot, parts):
     rows = jnp.dot(one_hot, parts, preferred_element_type=jnp.float32)
-    return rows[:, :128] + rows[:, 128:256] + rows[:, 256:]
+    return rows[:, :128] + rows[:, 128:]
 
 
 def one_hot_rows(numbers, depth):

time: 97.8 us -> 97.6 us (level)
  no operation moved by 1% of the time
where the time goes in v7:
time: 97.6 us; the launch traced here: 97.1 us
  starting transfers between devices  46.5 us (48%)
  blocking collectives  41.9 us (43%)
  Pallas kernels  3.29 us (3%)
  waiting for transfers between devices  2.86 us (3%)
  local copies, waits for them, and re-layouts  1.64 us (2%)
    ppermute x8, starting transfers between devices, swap(): return lax.ppermute(block, GY, pairs + [(j, i) for i, j in pairs])  30.2 us
    all_to_all x1, blocking collectives, shards(): part = lax.all_to_all(part, NEAR, 0, 0, tiled=True)  23.5 us
    all_to_all x1, blocking collectives, shards(): part = lax.all_to_all(part, FAR, 0, 0, tiled=True)  18.4 us
    ppermute x8, starting transfers between devices, cycle(): lax.ppermute(block, axis, [(i, (i + distance) % n) for i in range(n)])  16.4 us
    ppermute x8, waiting for transfers between devices, cycle(): lax.ppermute(block, axis, [(i, (i + distance) % n) for i in range(n)])  2.84 us
    pallas_call x8, Pallas kernels, call(): pl.pallas_call(kernel, out_shape=outs, in_specs=[spec] * len(args), out_s...  2.62 us
  transfers between devices with their start and end apart: 16, of which 3 were waited for; matrix products, arithmetic and copies ran while one was open for 0% of the time, Pallas kernels for 1%

profile of v7, /device:TPU:1, one launch (start us, length us, event | category | flops | bytes accessed | tf_op | source)
XLA Modules:
  0.0 97.1 jit_solution(10799457347893940138)
XLA Ops:
  0.6 0.0 copy-start.2
  0.6 0.7 copy-done.4
  1.3 0.1 shard_map.68.pick_ref.pick
  1.4 0.0 copy-start.1
  1.4 0.1 shard_map.69
  1.6 2.6 %collective-permute-start = (f32[32,128]{1,0:T(8,128)S(1)}, f32[32,128]{1,0:T(8,128)S(1)}, u32[]{:S(2)}, u32[]{:S(2)}) collective-permute-start(f32[32,128]{1,0:T(8,128)S(1)} %get-tuple-element.33), channel_id=1, source_target_pairs={{0,128},{128,256},{256,384},{384,512},{512,640},{640,768},{768,896... | collective-permute-start | bytes 49160 | tf_op jit(solution)/shard_map/ppermute | solution.py:171
  4.2 0.8 collective-permute-start.1
  5.0 7.3 %collective-permute-start.2 = (f32[32,128]{1,0:T(8,128)S(1)}, f32[32,128]{1,0:T(8,128)S(1)}, u32[]{:S(2)}, u32[]{:S(2)}) collective-permute-start(f32[32,128]{1,0:T(8,128)S(1)} %get-tuple-element.35), channel_id=1, source_target_pairs={{0,1},{2,3},{4,5},{6,7},{8,9},{10,11},{12,13},{14,15},{16,17},{18,... | collective-permute-start | bytes 49160 | tf_op jit(solution)/shard_map/ppermute | solution.py:166
  12.3 6.0 %collective-permute-start.3 = (f32[32,128]{1,0:T(8,128)S(1)}, f32[32,128]{1,0:T(8,128)S(1)}, u32[]{:S(2)}, u32[]{:S(2)}) collective-permute-start(f32[32,128]{1,0:T(8,128)S(1)} %get-tuple-element.36), channel_id=1, source_target_pairs={{0,896},{128,0},{256,128},{384,256},{512,384},{640,512},{768,640},... | collective-permute-start | bytes 49160 | tf_op jit(solution)/shard_map/ppermute | solution.py:171
  18.4 0.9 copy-done
  19.3 0.1 shard_map.70
  19.4 0.0 collective-permute-done.g0
  19.4 0.0 collective-permute-done.1.g1
  19.5 0.0 collective-permute-done.2.g2
  19.5 0.0 collective-permute-done.3.g3
  19.5 0.4 shard_map.71
  19.9 0.0 collective-permute-start.4
  20.0 0.7 collective-permute-start.5
  20.6 4.9 %collective-permute-start.6 = (f32[32,128]{1,0:T(8,128)S(1)}, f32[32,128]{1,0:T(8,128)S(1)}, u32[]{:S(2)}, u32[]{:S(2)}) collective-permute-start(f32[32,128]{1,0:T(8,128)S(1)} %get-tuple-element.44), channel_id=1, source_target_pairs={{0,1},{2,3},{4,5},{6,7},{8,9},{10,11},{12,13},{14,15},{16,17},{18,... | collective-permute-start | bytes 49160 | tf_op jit(solution)/shard_map/ppermute | solution.py:166
  25.5 3.4 %collective-permute-start.7 = (f32[32,128]{1,0:T(8,128)S(1)}, f32[32,128]{1,0:T(8,128)S(1)}, u32[]{:S(2)}, u32[]{:S(2)}) collective-permute-start(f32[32,128]{1,0:T(8,128)S(1)} %get-tuple-element.45), channel_id=1, source_target_pairs={{0,896},{128,0},{256,128},{384,256},{512,384},{640,512},{768,640},... | collective-permute-start | bytes 49160 | tf_op jit(solution)/shard_map/ppermute | solution.py:171
  28.9 0.0 collective-permute-done.4.g0
  28.9 0.0 collective-permute-done.5.g1
  28.9 0.0 collective-permute-done.6.g2
  28.9 0.8 collective-permute-done.7.g3
  29.7 0.4 shard_map.72
  30.2 0.0 collective-permute-start.8
  30.2 0.7 collective-permute-start.9
  30.9 6.6 %collective-permute-start.10 = (f32[32,128]{1,0:T(8,128)S(1)}, f32[32,128]{1,0:T(8,128)S(1)}, u32[]{:S(2)}, u32[]{:S(2)}) collective-permute-start(f32[32,128]{1,0:T(8,128)S(1)} %get-tuple-element.50), channel_id=1, source_target_pairs={{0,1},{2,3},{4,5},{6,7},{8,9},{10,11},{12,13},{14,15},{16,17},{18,... | collective-permute-start | bytes 49160 | tf_op jit(solution)/shard_map/ppermute | solution.py:166
  37.5 1.8 %collective-permute-start.11 = (f32[32,128]{1,0:T(8,128)S(1)}, f32[32,128]{1,0:T(8,128)S(1)}, u32[]{:S(2)}, u32[]{:S(2)}) collective-permute-start(f32[32,128]{1,0:T(8,128)S(1)} %get-tuple-element.51), channel_id=1, source_target_pairs={{0,896},{128,0},{256,128},{384,256},{512,384},{640,512},{768,640},... | collective-permute-start | bytes 49160 | tf_op jit(solution)/shard_map/ppermute | solution.py:171
  39.3 0.0 collective-permute-done.8.g0
  39.4 0.0 collective-permute-done.9.g1
  39.4 0.0 collective-permute-done.10.g2
  39.4 1.3 %collective-permute-done.11.g3 = f32[32,128]{1,0:T(8,128)S(1)} collective-permute-done((f32[32,128]{1,0:T(8,128)S(1)}, f32[32,128]{1,0:T(8,128)S(1)}, u32[]{:S(2)}, u32[]{:S(2)}) %collective-permute-start.11) | collective-permute-done | bytes 16416 | tf_op jit(solution)/shard_map/ppermute | solution.py:171
  40.7 0.4 shard_map.73
  41.2 0.1 collective-permute-start.12
  41.3 0.7 collective-permute-start.13
  42.0 8.5 %collective-permute-start.14 = (f32[32,128]{1,0:T(8,128)S(1)}, f32[32,128]{1,0:T(8,128)S(1)}, u32[]{:S(2)}, u32[]{:S(2)}) collective-permute-start(f32[32,128]{1,0:T(8,128)S(1)} %get-tuple-element.54), channel_id=1, source_target_pairs={{0,1},{2,3},{4,5},{6,7},{8,9},{10,11},{12,13},{14,15},{16,17},{18,... | collective-permute-start | bytes 49160 | tf_op jit(solution)/shard_map/ppermute | solution.py:166
  50.5 2.4 %collective-permute-start.15 = (f32[32,128]{1,0:T(8,128)S(1)}, f32[32,128]{1,0:T(8,128)S(1)}, u32[]{:S(2)}, u32[]{:S(2)}) collective-permute-start(f32[32,128]{1,0:T(8,128)S(1)} %get-tuple-element.55), channel_id=1, source_target_pairs={{0,896},{128,0},{256,128},{384,256},{512,384},{640,512},{768,640},... | collective-permute-start | bytes 49160 | tf_op jit(solution)/shard_map/ppermute | solution.py:171
  52.9 0.6 shard_map.74
  53.5 0.0 collective-permute-done.12.g0
  53.5 0.0 collective-permute-done.13.g1
  53.5 0.0 collective-permute-done.14.g2
  53.5 0.7 collective-permute-done.15.g3
  54.2 0.3 shard_map.75
  54.5 23.5 %all_to_all.17 = f32[32,1,128]{2,1,0:T(1,128)S(1)} all-to-all(f32[32,1,128]{2,1,0:T(1,128)S(1)} %bitcast.8), channel_id=1, replica_groups=mesh['gx_0'=4,'gx_1'=2,'gy_0'=8,'gy_1'=16] {'gx_0','gy_0'}, dimensions={0} | all-to-all | bytes 32768 | tf_op jit(solution)/shard_map/all_to_all | solution.py:201
  78.0 0.1 reduce_sum.9
  78.0 18.4 %all_to_all.18 = f32[32,1,128]{2,1,0:T(1,128)S(1)} all-to-all(f32[32,1,128]{2,1,0:T(1,128)S(1)} %broadcast_in_dim.2), channel_id=1, replica_groups=mesh['gx_0'=4,'gx_1'=2,'gy_0'=8,'gy_1'=16] {'gx_1','gy_1'}, dimensions={0} | all-to-all | bytes 32768 | tf_op jit(solution)/shard_map/all_to_all | solution.py:203
  96.4 0.7 shard_map.76
  (7 shorter events, 0.0 us)
Async XLA Ops:
  0.6 0.8 copy-start.2
  0.6 0.7 copy-start.4
  1.4 16.9 %copy-start.1 = (f32[64,128]{1,0:T(8,128)S(1)}, f32[64,128]{1,0:T(8,128)}, u32[]{:S(2)}) copy-start(f32[64,128]{1,0:T(8,128)} %mass_ref.1) | copy-start | bytes 98308
  1.6 17.8 %collective-permute-start = (f32[32,128]{1,0:T(8,128)S(1)}, f32[32,128]{1,0:T(8,128)S(1)}, u32[]{:S(2)}, u32[]{:S(2)}) collective-permute-start(f32[32,128]{1,0:T(8,128)S(1)} %get-tuple-element.33), channel_id=1, source_target_pairs={{0,128},{128,256},{256,384},{384,512},{512,640},{640,768},{768,896... | collective-permute-start | bytes 49160 | tf_op jit(solution)/shard_map/ppermute | solution.py:171
  4.2 14.2 %copy-start.3 = (s32[64,6]{0,1:T(8,128)S(1)}, s32[64,6]{0,1:T(8,128)}, u32[]{:S(2)}) copy-start(s32[64,6]{0,1:T(8,128)} %param.8) | copy-start | bytes 4612
  4.2 15.3 %collective-permute-start.1 = (f32[32,128]{1,0:T(8,128)S(1)}, f32[32,128]{1,0:T(8,128)S(1)}, u32[]{:S(2)}, u32[]{:S(2)}) collective-permute-start(f32[32,128]{1,0:T(8,128)S(1)} %get-tuple-element.34), channel_id=1, source_target_pairs={{1,2},{3,4},{5,6},{7,8},{9,10},{11,12},{13,14},{15,16},{17,18},{19... | collective-permute-start | bytes 49160 | tf_op jit(solution)/shard_map/ppermute | solution.py:166
  5.0 14.5 %collective-permute-start.2 = (f32[32,128]{1,0:T(8,128)S(1)}, f32[32,128]{1,0:T(8,128)S(1)}, u32[]{:S(2)}, u32[]{:S(2)}) collective-permute-start(f32[32,128]{1,0:T(8,128)S(1)} %get-tuple-element.35), channel_id=1, source_target_pairs={{0,1},{2,3},{4,5},{6,7},{8,9},{10,11},{12,13},{14,15},{16,17},{18,... | collective-permute-start | bytes 49160 | tf_op jit(solution)/shard_map/ppermute | solution.py:166
  12.3 7.1 %collective-permute-start.3 = (f32[32,128]{1,0:T(8,128)S(1)}, f32[32,128]{1,0:T(8,128)S(1)}, u32[]{:S(2)}, u32[]{:S(2)}) collective-permute-start(f32[32,128]{1,0:T(8,128)S(1)} %get-tuple-element.36), channel_id=1, source_target_pairs={{0,896},{128,0},{256,128},{384,256},{512,384},{640,512},{768,640},... | collective-permute-start | bytes 49160 | tf_op jit(solution)/shard_map/ppermute | solution.py:171
  18.4 0.9 copy-start
  19.9 9.0 %collective-permute-start.4 = (f32[32,128]{1,0:T(8,128)S(1)}, f32[32,128]{1,0:T(8,128)S(1)}, u32[]{:S(2)}, u32[]{:S(2)}) collective-permute-start(f32[32,128]{1,0:T(8,128)S(1)} %get-tuple-element.42), channel_id=1, source_target_pairs={{0,128},{128,256},{256,384},{384,512},{512,640},{640,768},{768,896... | collective-permute-start | bytes 49160 | tf_op jit(solution)/shard_map/ppermute | solution.py:171
  20.0 9.0 %collective-permute-start.5 = (f32[32,128]{1,0:T(8,128)S(1)}, f32[32,128]{1,0:T(8,128)S(1)}, u32[]{:S(2)}, u32[]{:S(2)}) collective-permute-start(f32[32,128]{1,0:T(8,128)S(1)} %get-tuple-element.43), channel_id=1, source_target_pairs={{1,2},{3,4},{5,6},{7,8},{9,10},{11,12},{13,14},{15,16},{17,18},{19... | collective-permute-start | bytes 49160 | tf_op jit(solution)/shard_map/ppermute | solution.py:166
  20.6 8.3 %collective-permute-start.6 = (f32[32,128]{1,0:T(8,128)S(1)}, f32[32,128]{1,0:T(8,128)S(1)}, u32[]{:S(2)}, u32[]{:S(2)}) collective-permute-start(f32[32,128]{1,0:T(8,128)S(1)} %get-tuple-element.44), channel_id=1, source_target_pairs={{0,1},{2,3},{4,5},{6,7},{8,9},{10,11},{12,13},{14,15},{16,17},{18,... | collective-permute-start | bytes 49160 | tf_op jit(solution)/shard_map/ppermute | solution.py:166
  25.5 4.2 %collective-permute-start.7 = (f32[32,128]{1,0:T(8,128)S(1)}, f32[32,128]{1,0:T(8,128)S(1)}, u32[]{:S(2)}, u32[]{:S(2)}) collective-permute-start(f32[32,128]{1,0:T(8,128)S(1)} %get-tuple-element.45), channel_id=1, source_target_pairs={{0,896},{128,0},{256,128},{384,256},{512,384},{640,512},{768,640},... | collective-permute-start | bytes 49160 | tf_op jit(solution)/shard_map/ppermute | solution.py:171
  30.2 9.2 %collective-permute-start.8 = (f32[32,128]{1,0:T(8,128)S(1)}, f32[32,128]{1,0:T(8,128)S(1)}, u32[]{:S(2)}, u32[]{:S(2)}) collective-permute-start(f32[32,128]{1,0:T(8,128)S(1)} %get-tuple-element.48), channel_id=1, source_target_pairs={{0,128},{128,256},{256,384},{384,512},{512,640},{640,768},{768,896... | collective-permute-start | bytes 49160 | tf_op jit(solution)/shard_map/ppermute | solution.py:171
  30.2 9.1 %collective-permute-start.9 = (f32[32,128]{1,0:T(8,128)S(1)}, f32[32,128]{1,0:T(8,128)S(1)}, u32[]{:S(2)}, u32[]{:S(2)}) collective-permute-start(f32[32,128]{1,0:T(8,128)S(1)} %get-tuple-element.49), channel_id=1, source_target_pairs={{1,2},{3,4},{5,6},{7,8},{9,10},{11,12},{13,14},{15,16},{17,18},{19... | collective-permute-start | bytes 49160 | tf_op jit(solution)/shard_map/ppermute | solution.py:166
  30.9 8.5 %collective-permute-start.10 = (f32[32,128]{1,0:T(8,128)S(1)}, f32[32,128]{1,0:T(8,128)S(1)}, u32[]{:S(2)}, u32[]{:S(2)}) collective-permute-start(f32[32,128]{1,0:T(8,128)S(1)} %get-tuple-element.50), channel_id=1, source_target_pairs={{0,1},{2,3},{4,5},{6,7},{8,9},{10,11},{12,13},{14,15},{16,17},{18,... | collective-permute-start | bytes 49160 | tf_op jit(solution)/shard_map/ppermute | solution.py:166
  37.5 3.2 %collective-permute-start.11 = (f32[32,128]{1,0:T(8,128)S(1)}, f32[32,128]{1,0:T(8,128)S(1)}, u32[]{:S(2)}, u32[]{:S(2)}) collective-permute-start(f32[32,128]{1,0:T(8,128)S(1)} %get-tuple-element.51), channel_id=1, source_target_pairs={{0,896},{128,0},{256,128},{384,256},{512,384},{640,512},{768,640},... | collective-permute-start | bytes 49160 | tf_op jit(solution)/shard_map/ppermute | solution.py:171
  41.2 12.4 %collective-permute-start.12 = (f32[32,128]{1,0:T(8,128)S(1)}, f32[32,128]{1,0:T(8,128)S(1)}, u32[]{:S(2)}, u32[]{:S(2)}) collective-permute-start(f32[32,128]{1,0:T(8,128)S(1)} %get-tuple-element.52), channel_id=1, source_target_pairs={{0,128},{128,256},{256,384},{384,512},{512,640},{640,768},{768,896... | collective-permute-start | bytes 49160 | tf_op jit(solution)/shard_map/ppermute | solution.py:171
  41.3 12.2 %collective-permute-start.13 = (f32[32,128]{1,0:T(8,128)S(1)}, f32[32,128]{1,0:T(8,128)S(1)}, u32[]{:S(2)}, u32[]{:S(2)}) collective-permute-start(f32[32,128]{1,0:T(8,128)S(1)} %get-tuple-element.53), channel_id=1, source_target_pairs={{1,2},{3,4},{5,6},{7,8},{9,10},{11,12},{13,14},{15,16},{17,18},{19... | collective-permute-start | bytes 49160 | tf_op jit(solution)/shard_map/ppermute | solution.py:166
  42.0 11.6 %collective-permute-start.14 = (f32[32,128]{1,0:T(8,128)S(1)}, f32[32,128]{1,0:T(8,128)S(1)}, u32[]{:S(2)}, u32[]{:S(2)}) collective-permute-start(f32[32,128]{1,0:T(8,128)S(1)} %get-tuple-element.54), channel_id=1, source_target_pairs={{0,1},{2,3},{4,5},{6,7},{8,9},{10,11},{12,13},{14,15},{16,17},{18,... | collective-permute-start | bytes 49160 | tf_op jit(solution)/shard_map/ppermute | solution.py:166
  50.5 3.7 %collective-permute-start.15 = (f32[32,128]{1,0:T(8,128)S(1)}, f32[32,128]{1,0:T(8,128)S(1)}, u32[]{:S(2)}, u32[]{:S(2)}) collective-permute-start(f32[32,128]{1,0:T(8,128)S(1)} %get-tuple-element.55), channel_id=1, source_target_pairs={{0,896},{128,0},{256,128},{384,256},{512,384},{640,512},{768,640},... | collective-permute-start | bytes 49160 | tf_op jit(solution)/shard_map/ppermute | solution.py:171

commit v8 on v5

--- a/solution.py
+++ b/solution.py
@@ -70,7 +70,7 @@
 
 
 def pick_kernel(list_ref, pick_ref):
-    odd = lax.axis_index("gy_1") % 2 == 1
+    odd = (lax.axis_index("gy_1") + lax.axis_index("gx_1")) % 2 == 1
     up, down = list_ref[0, 0:1, :], list_ref[0, 1:2, :]
     rows = (jnp.where(odd, up, down), jnp.where(odd, down, up), list_ref[0, 2:3, :], list_ref[0, 3:4, :])
     for g in range(4):
@@ -88,7 +88,7 @@
         diag = diag + coeff_ref[e]
         held_ref[e] = coeff_ref[e]
     diag_ref[...] = diag
-    odd = lax.axis_index("gy_1") % 2 == 1
+    odd = (lax.axis_index("gy_1") + lax.axis_index("gx_1")) % 2 == 1
     edges = edges_ref[...]
     edges = jnp.where(odd & (edges >= BLK) & (edges < BLK + 2 * HB), edges ^ HB, edges)
     for e in range(EDG):
@@ -163,8 +163,8 @@
 
 def swap(block, first):
     n = lax.axis_size(GY)
-    pairs = [(i, i + 1) for i in range(first, n - 1, 2)]
-    return lax.ppermute(block, GY, pairs + [(j, i) for i, j in pairs])
+    pairs = [(c * n + i, c * n + i + 1) for c in range(2) for i in range((first + c) % 2, n - 1, 2)]
+    return lax.ppermute(block, ("gx_1",) + GY, pairs + [(j, i) for i, j in pairs])
 
 
 def cycle(block, axis, distance):

time: 97.6 us -> 96.7 us (level)
  blocking collectives: 41.7 us -> 42.8 us
  starting transfers between devices: 46.5 us -> 45.5 us
    ppermute x8, starting transfers between devices: 30.2 us -> 14.9 us  [swap(): lax.ppermute(block, ('gx_1',) + GY, pairs + [(j, i) for i, j in pairs])]
    ppermute x8, starting transfers between devices: 16.4 us -> 30.5 us  [cycle(): lax.ppermute(block, axis, [(i, (i + distance) % n) for i in range(n)])]
    all_to_all x1, blocking collectives: 24.6 us -> 28.1 us  [shards(): part = lax.all_to_all(part, NEAR, 0, 0, tiled=True)]
    all_to_all x1, blocking collectives: 17 us -> 14.7 us  [shards(): part = lax.all_to_all(part, FAR, 0, 0, tiled=True)]
where the time goes in v8:
time: 96.7 us; the launch traced here: 96.2 us
  starting transfers between devices  45.5 us (47%)
  blocking collectives  42.8 us (44%)
  Pallas kernels  3.46 us (4%)
  waiting for transfers between devices  1.9 us (2%)
  local copies, waits for them, and re-layouts  1.63 us (2%)
    ppermute x8, starting transfers between devices, cycle(): lax.ppermute(block, axis, [(i, (i + distance) % n) for i in range(n)])  30.5 us
    all_to_all x1, blocking collectives, shards(): part = lax.all_to_all(part, NEAR, 0, 0, tiled=True)  28.1 us
    ppermute x8, starting transfers between devices, swap(): lax.ppermute(block, ('gx_1',) + GY, pairs + [(j, i) for i, j in pairs])  14.9 us
    all_to_all x1, blocking collectives, shards(): part = lax.all_to_all(part, FAR, 0, 0, tiled=True)  14.7 us
    pallas_call x8, Pallas kernels, call(): pl.pallas_call(kernel, out_shape=outs, in_specs=[spec] * len(args), out_s...  2.79 us
  transfers between devices with their start and end apart: 16, of which 3 were waited for; matrix products, arithmetic and copies ran while one was open for 0% of the time, Pallas kernels for 1%

profile of v8, /device:TPU:1, one launch (start us, length us, event | category | flops | bytes accessed | tf_op | source)
XLA Modules:
  0.0 96.2 jit_solution(8318381474732553916)
XLA Ops:
  0.6 0.7 copy-done.4
  1.3 0.1 shard_map.68.pick_ref.pick
  1.4 0.0 copy-start.1
  1.4 0.2 shard_map.69
  1.6 2.6 %collective-permute-start = (f32[32,128]{1,0:T(8,128)S(1)}, f32[32,128]{1,0:T(8,128)S(1)}, u32[]{:S(2)}, u32[]{:S(2)}) collective-permute-start(f32[32,128]{1,0:T(8,128)S(1)} %get-tuple-element.33), channel_id=1, source_target_pairs={{0,128},{128,256},{256,384},{384,512},{512,640},{640,768},{768,896... | collective-permute-start | bytes 49160 | tf_op jit(solution)/shard_map/ppermute | solution.py:172
  4.2 4.1 %collective-permute-start.1 = (f32[32,128]{1,0:T(8,128)S(1)}, f32[32,128]{1,0:T(8,128)S(1)}, u32[]{:S(2)}, u32[]{:S(2)}) collective-permute-start(f32[32,128]{1,0:T(8,128)S(1)} %get-tuple-element.34), channel_id=1, source_target_pairs={{1,2},{3,4},{5,6},{7,8},{9,10},{11,12},{13,14},{15,16},{17,18},{19... | collective-permute-start | bytes 49160 | tf_op jit(solution)/shard_map/ppermute | solution.py:167
  8.3 0.7 collective-permute-start.2
  9.0 9.4 %collective-permute-start.3 = (f32[32,128]{1,0:T(8,128)S(1)}, f32[32,128]{1,0:T(8,128)S(1)}, u32[]{:S(2)}, u32[]{:S(2)}) collective-permute-start(f32[32,128]{1,0:T(8,128)S(1)} %get-tuple-element.36), channel_id=1, source_target_pairs={{0,896},{128,0},{256,128},{384,256},{512,384},{640,512},{768,640},... | collective-permute-start | bytes 49160 | tf_op jit(solution)/shard_map/ppermute | solution.py:172
  18.4 0.0 copy-done.1
  18.4 0.9 copy-done
  19.3 0.1 shard_map.70
  19.4 0.0 collective-permute-done.g0
  19.5 0.0 collective-permute-done.1.g1
  19.5 0.0 collective-permute-done.2.g2
  19.5 0.0 collective-permute-done.3.g3
  19.5 0.5 shard_map.71
  20.0 0.0 collective-permute-start.4
  20.0 3.6 %collective-permute-start.5 = (f32[32,128]{1,0:T(8,128)S(1)}, f32[32,128]{1,0:T(8,128)S(1)}, u32[]{:S(2)}, u32[]{:S(2)}) collective-permute-start(f32[32,128]{1,0:T(8,128)S(1)} %get-tuple-element.43), channel_id=1, source_target_pairs={{1,2},{3,4},{5,6},{7,8},{9,10},{11,12},{13,14},{15,16},{17,18},{19... | collective-permute-start | bytes 49160 | tf_op jit(solution)/shard_map/ppermute | solution.py:167
  23.7 0.7 collective-permute-start.6
  24.3 7.6 %collective-permute-start.7 = (f32[32,128]{1,0:T(8,128)S(1)}, f32[32,128]{1,0:T(8,128)S(1)}, u32[]{:S(2)}, u32[]{:S(2)}) collective-permute-start(f32[32,128]{1,0:T(8,128)S(1)} %get-tuple-element.45), channel_id=1, source_target_pairs={{0,896},{128,0},{256,128},{384,256},{512,384},{640,512},{768,640},... | collective-permute-start | bytes 49160 | tf_op jit(solution)/shard_map/ppermute | solution.py:172
  31.9 0.0 collective-permute-done.4.g0
  31.9 0.0 collective-permute-done.5.g1
  31.9 0.0 collective-permute-done.6.g2
  31.9 0.8 collective-permute-done.7.g3
  32.8 0.5 shard_map.72
  33.3 0.0 collective-permute-start.8
  33.3 1.9 %collective-permute-start.9 = (f32[32,128]{1,0:T(8,128)S(1)}, f32[32,128]{1,0:T(8,128)S(1)}, u32[]{:S(2)}, u32[]{:S(2)}) collective-permute-start(f32[32,128]{1,0:T(8,128)S(1)} %get-tuple-element.49), channel_id=1, source_target_pairs={{1,2},{3,4},{5,6},{7,8},{9,10},{11,12},{13,14},{15,16},{17,18},{19... | collective-permute-start | bytes 49160 | tf_op jit(solution)/shard_map/ppermute | solution.py:167
  35.2 0.7 collective-permute-start.10
  35.9 4.8 %collective-permute-start.11 = (f32[32,128]{1,0:T(8,128)S(1)}, f32[32,128]{1,0:T(8,128)S(1)}, u32[]{:S(2)}, u32[]{:S(2)}) collective-permute-start(f32[32,128]{1,0:T(8,128)S(1)} %get-tuple-element.51), channel_id=1, source_target_pairs={{0,896},{128,0},{256,128},{384,256},{512,384},{640,512},{768,640},... | collective-permute-start | bytes 49160 | tf_op jit(solution)/shard_map/ppermute | solution.py:172
  40.7 0.0 collective-permute-done.8.g0
  40.7 0.0 collective-permute-done.9.g1
  40.7 0.0 collective-permute-done.10.g2
  40.7 0.8 collective-permute-done.11.g3
  41.5 0.5 shard_map.73
  42.0 0.0 collective-permute-start.12
  42.0 2.6 %collective-permute-start.13 = (f32[32,128]{1,0:T(8,128)S(1)}, f32[32,128]{1,0:T(8,128)S(1)}, u32[]{:S(2)}, u32[]{:S(2)}) collective-permute-start(f32[32,128]{1,0:T(8,128)S(1)} %get-tuple-element.53), channel_id=1, source_target_pairs={{1,2},{3,4},{5,6},{7,8},{9,10},{11,12},{13,14},{15,16},{17,18},{19... | collective-permute-start | bytes 49160 | tf_op jit(solution)/shard_map/ppermute | solution.py:167
  44.7 0.7 collective-permute-start.14
  45.3 6.1 %collective-permute-start.15 = (f32[32,128]{1,0:T(8,128)S(1)}, f32[32,128]{1,0:T(8,128)S(1)}, u32[]{:S(2)}, u32[]{:S(2)}) collective-permute-start(f32[32,128]{1,0:T(8,128)S(1)} %get-tuple-element.55), channel_id=1, source_target_pairs={{0,896},{128,0},{256,128},{384,256},{512,384},{640,512},{768,640},... | collective-permute-start | bytes 49160 | tf_op jit(solution)/shard_map/ppermute | solution.py:172
  51.4 0.6 shard_map.74
  52.0 0.0 collective-permute-done.12.g0
  52.0 0.0 collective-permute-done.13.g1
  52.0 0.0 collective-permute-done.14.g2
  52.0 0.2 collective-permute-done.15.g3
  52.3 0.3 shard_map.75
  52.6 28.1 %all_to_all.17 = f32[64,1,128]{2,1,0:T(1,128)S(1)} all-to-all(f32[64,1,128]{2,1,0:T(1,128)S(1)} %bitcast.8), channel_id=1, replica_groups=mesh['gx_0'=4,'gx_1'=2,'gy_0'=8,'gy_1'=16] {'gx_0','gx_1','gy_0'}, dimensions={0} | all-to-all | bytes 65536 | tf_op jit(solution)/shard_map/all_to_all | solution.py:202
  80.7 0.1 reduce_sum.9
  80.8 14.7 %all_to_all.18 = f32[16,1,128]{2,1,0:T(1,128)S(1)} all-to-all(f32[16,1,128]{2,1,0:T(1,128)S(1)} %broadcast_in_dim.2), channel_id=1, replica_groups=mesh['gx_0'=4,'gx_1'=2,'gy_0'=8,'gy_1'=16] {'gy_1'}, dimensions={0} | all-to-all | bytes 16384 | tf_op jit(solution)/shard_map/all_to_all | solution.py:204
  95.5 0.7 shard_map.76
  (7 shorter events, 0.0 us)
Async XLA Ops:
  0.6 0.8 copy-start.2
  0.6 0.7 copy-start.4
  1.4 16.9 %copy-start.1 = (f32[64,128]{1,0:T(8,128)S(1)}, f32[64,128]{1,0:T(8,128)}, u32[]{:S(2)}) copy-start(f32[64,128]{1,0:T(8,128)} %mass_ref.1) | copy-start | bytes 98308
  1.6 17.8 %collective-permute-start = (f32[32,128]{1,0:T(8,128)S(1)}, f32[32,128]{1,0:T(8,128)S(1)}, u32[]{:S(2)}, u32[]{:S(2)}) collective-permute-start(f32[32,128]{1,0:T(8,128)S(1)} %get-tuple-element.33), channel_id=1, source_target_pairs={{0,128},{128,256},{256,384},{384,512},{512,640},{640,768},{768,896... | collective-permute-start | bytes 49160 | tf_op jit(solution)/shard_map/ppermute | solution.py:172
  4.2 14.2 %copy-start.3 = (s32[64,6]{0,1:T(8,128)S(1)}, s32[64,6]{0,1:T(8,128)}, u32[]{:S(2)}) copy-start(s32[64,6]{0,1:T(8,128)} %param.8) | copy-start | bytes 4612
  4.2 15.3 %collective-permute-start.1 = (f32[32,128]{1,0:T(8,128)S(1)}, f32[32,128]{1,0:T(8,128)S(1)}, u32[]{:S(2)}, u32[]{:S(2)}) collective-permute-start(f32[32,128]{1,0:T(8,128)S(1)} %get-tuple-element.34), channel_id=1, source_target_pairs={{1,2},{3,4},{5,6},{7,8},{9,10},{11,12},{13,14},{15,16},{17,18},{19... | collective-permute-start | bytes 49160 | tf_op jit(solution)/shard_map/ppermute | solution.py:167
  8.3 11.1 %collective-permute-start.2 = (f32[32,128]{1,0:T(8,128)S(1)}, f32[32,128]{1,0:T(8,128)S(1)}, u32[]{:S(2)}, u32[]{:S(2)}) collective-permute-start(f32[32,128]{1,0:T(8,128)S(1)} %get-tuple-element.35), channel_id=1, source_target_pairs={{0,1},{2,3},{4,5},{6,7},{8,9},{10,11},{12,13},{14,15},{16,17},{18,... | collective-permute-start | bytes 49160 | tf_op jit(solution)/shard_map/ppermute | solution.py:167
  9.0 10.5 %collective-permute-start.3 = (f32[32,128]{1,0:T(8,128)S(1)}, f32[32,128]{1,0:T(8,128)S(1)}, u32[]{:S(2)}, u32[]{:S(2)}) collective-permute-start(f32[32,128]{1,0:T(8,128)S(1)} %get-tuple-element.36), channel_id=1, source_target_pairs={{0,896},{128,0},{256,128},{384,256},{512,384},{640,512},{768,640},... | collective-permute-start | bytes 49160 | tf_op jit(solution)/shard_map/ppermute | solution.py:172
  18.4 0.9 copy-start
  20.0 12.0 %collective-permute-start.4 = (f32[32,128]{1,0:T(8,128)S(1)}, f32[32,128]{1,0:T(8,128)S(1)}, u32[]{:S(2)}, u32[]{:S(2)}) collective-permute-start(f32[32,128]{1,0:T(8,128)S(1)} %get-tuple-element.42), channel_id=1, source_target_pairs={{0,128},{128,256},{256,384},{384,512},{512,640},{640,768},{768,896... | collective-permute-start | bytes 49160 | tf_op jit(solution)/shard_map/ppermute | solution.py:172
  20.0 11.9 %collective-permute-start.5 = (f32[32,128]{1,0:T(8,128)S(1)}, f32[32,128]{1,0:T(8,128)S(1)}, u32[]{:S(2)}, u32[]{:S(2)}) collective-permute-start(f32[32,128]{1,0:T(8,128)S(1)} %get-tuple-element.43), channel_id=1, source_target_pairs={{1,2},{3,4},{5,6},{7,8},{9,10},{11,12},{13,14},{15,16},{17,18},{19... | collective-permute-start | bytes 49160 | tf_op jit(solution)/shard_map/ppermute | solution.py:167
  23.7 8.3 %collective-permute-start.6 = (f32[32,128]{1,0:T(8,128)S(1)}, f32[32,128]{1,0:T(8,128)S(1)}, u32[]{:S(2)}, u32[]{:S(2)}) collective-permute-start(f32[32,128]{1,0:T(8,128)S(1)} %get-tuple-element.44), channel_id=1, source_target_pairs={{0,1},{2,3},{4,5},{6,7},{8,9},{10,11},{12,13},{14,15},{16,17},{18,... | collective-permute-start | bytes 49160 | tf_op jit(solution)/shard_map/ppermute | solution.py:167
  24.3 8.5 %collective-permute-start.7 = (f32[32,128]{1,0:T(8,128)S(1)}, f32[32,128]{1,0:T(8,128)S(1)}, u32[]{:S(2)}, u32[]{:S(2)}) collective-permute-start(f32[32,128]{1,0:T(8,128)S(1)} %get-tuple-element.45), channel_id=1, source_target_pairs={{0,896},{128,0},{256,128},{384,256},{512,384},{640,512},{768,640},... | collective-permute-start | bytes 49160 | tf_op jit(solution)/shard_map/ppermute | solution.py:172
  33.3 7.4 %collective-permute-start.8 = (f32[32,128]{1,0:T(8,128)S(1)}, f32[32,128]{1,0:T(8,128)S(1)}, u32[]{:S(2)}, u32[]{:S(2)}) collective-permute-start(f32[32,128]{1,0:T(8,128)S(1)} %get-tuple-element.48), channel_id=1, source_target_pairs={{0,128},{128,256},{256,384},{384,512},{512,640},{640,768},{768,896... | collective-permute-start | bytes 49160 | tf_op jit(solution)/shard_map/ppermute | solution.py:172
  33.3 7.4 %collective-permute-start.9 = (f32[32,128]{1,0:T(8,128)S(1)}, f32[32,128]{1,0:T(8,128)S(1)}, u32[]{:S(2)}, u32[]{:S(2)}) collective-permute-start(f32[32,128]{1,0:T(8,128)S(1)} %get-tuple-element.49), channel_id=1, source_target_pairs={{1,2},{3,4},{5,6},{7,8},{9,10},{11,12},{13,14},{15,16},{17,18},{19... | collective-permute-start | bytes 49160 | tf_op jit(solution)/shard_map/ppermute | solution.py:167
  35.2 5.5 %collective-permute-start.10 = (f32[32,128]{1,0:T(8,128)S(1)}, f32[32,128]{1,0:T(8,128)S(1)}, u32[]{:S(2)}, u32[]{:S(2)}) collective-permute-start(f32[32,128]{1,0:T(8,128)S(1)} %get-tuple-element.50), channel_id=1, source_target_pairs={{0,1},{2,3},{4,5},{6,7},{8,9},{10,11},{12,13},{14,15},{16,17},{18,... | collective-permute-start | bytes 49160 | tf_op jit(solution)/shard_map/ppermute | solution.py:167
  35.9 5.7 %collective-permute-start.11 = (f32[32,128]{1,0:T(8,128)S(1)}, f32[32,128]{1,0:T(8,128)S(1)}, u32[]{:S(2)}, u32[]{:S(2)}) collective-permute-start(f32[32,128]{1,0:T(8,128)S(1)} %get-tuple-element.51), channel_id=1, source_target_pairs={{0,896},{128,0},{256,128},{384,256},{512,384},{640,512},{768,640},... | collective-permute-start | bytes 49160 | tf_op jit(solution)/shard_map/ppermute | solution.py:172
  42.0 10.0 %collective-permute-start.12 = (f32[32,128]{1,0:T(8,128)S(1)}, f32[32,128]{1,0:T(8,128)S(1)}, u32[]{:S(2)}, u32[]{:S(2)}) collective-permute-start(f32[32,128]{1,0:T(8,128)S(1)} %get-tuple-element.52), channel_id=1, source_target_pairs={{0,128},{128,256},{256,384},{384,512},{512,640},{640,768},{768,896... | collective-permute-start | bytes 49160 | tf_op jit(solution)/shard_map/ppermute | solution.py:172
  42.0 10.0 %collective-permute-start.13 = (f32[32,128]{1,0:T(8,128)S(1)}, f32[32,128]{1,0:T(8,128)S(1)}, u32[]{:S(2)}, u32[]{:S(2)}) collective-permute-start(f32[32,128]{1,0:T(8,128)S(1)} %get-tuple-element.53), channel_id=1, source_target_pairs={{1,2},{3,4},{5,6},{7,8},{9,10},{11,12},{13,14},{15,16},{17,18},{19... | collective-permute-start | bytes 49160 | tf_op jit(solution)/shard_map/ppermute | solution.py:167
  44.7 7.4 %collective-permute-start.14 = (f32[32,128]{1,0:T(8,128)S(1)}, f32[32,128]{1,0:T(8,128)S(1)}, u32[]{:S(2)}, u32[]{:S(2)}) collective-permute-start(f32[32,128]{1,0:T(8,128)S(1)} %get-tuple-element.54), channel_id=1, source_target_pairs={{0,1},{2,3},{4,5},{6,7},{8,9},{10,11},{12,13},{14,15},{16,17},{18,... | collective-permute-start | bytes 49160 | tf_op jit(solution)/shard_map/ppermute | solution.py:167
  45.3 6.9 %collective-permute-start.15 = (f32[32,128]{1,0:T(8,128)S(1)}, f32[32,128]{1,0:T(8,128)S(1)}, u32[]{:S(2)}, u32[]{:S(2)}) collective-permute-start(f32[32,128]{1,0:T(8,128)S(1)} %get-tuple-element.55), channel_id=1, source_target_pairs={{0,896},{128,0},{256,128},{384,256},{512,384},{640,512},{768,640},... | collective-permute-start | bytes 49160 | tf_op jit(solution)/shard_map/ppermute | solution.py:172
